TPU v7x, 32 devices: a whole 2x2x4 slice. The times are simulated.
32 devices in a mesh: row: 8 (over z, core), col: 4 (over y, x).
Axes of the slice: x: 2, y: 2, z: 4, core: 2. Of those that a mesh axis runs over, the one named last changes fastest.
Arguments:
- waves_row: bfloat16 [8, 64, 2048], P('row', None, 'col'), may hold values from -6 to 6
- waves_col: bfloat16 [4, 64, 2048], P('col', None, 'row'), may hold values from -6 to 6
- window_row: int32 [8], P('row'), may hold values from 0 to 32
- window_col: int32 [4], P('col'), may hold values from 0 to 32
- plane_wave: bfloat16 [2048, 1024], replicated, may hold values from -0.125 to 0.125
- screened: bfloat16 [8, 1024, 1024], P(None, 'row'), may hold values from -0.1875 to 0.1875
- owner_slot: int32 [8], replicated, may hold values from 0 to 7, each once
- transfer_table: int32 [8, 4], P(None, 'col'), may hold values from 0 to 7, as said below
- trial: bfloat16 [1024, 512], P('col'), may hold values from -6 to 6
Outputs:
- applied: float32 [2048, 512], P(('row', 'col'))
Inputs may be any that keep to these rules, and one draw needn't show every extreme that they name: `transfer_table`: for every column k-point, the row k-points name each of the 8 momentum transfers exactly once.
All inputs are finite; a program needn't handle non-finite values.
Results may differ from a plain program's by a relative error of at most 0.014.
Values may be sent and summed in bfloat16 or wider, within the bound.
No kernel may reach another device: no remote copies, remote signals or barrier semaphores. Data moves between devices by JAX's collectives and lax.ppermute only.
A program may use at most 64 MiB of HBM per device.

v0:
```python
import jax
import jax.numpy as jnp
from jax import lax
from jax.sharding import PartitionSpec as P

NG = 1024
NVW = 16
NCW = 16
NP = 256


def pair_products(waves, start):
    valence = lax.dynamic_slice_in_dim(waves, start, NVW, 0).astype(jnp.float32)
    conduction = lax.dynamic_slice_in_dim(waves, start + NVW, NCW, 0).astype(jnp.float32)
    return (
        (valence[:, None, :] * conduction[None, :, :]).reshape(NVW * NCW, -1).astype(jnp.bfloat16)
    )


def table_rows(plane_wave, position, points):
    return lax.dynamic_slice_in_dim(plane_wave, position * points, points, 0)


def shards(
    waves_row,
    waves_col,
    window_row,
    window_col,
    plane_wave,
    screened,
    owner_slot,
    transfer_table,
    trial,
):
    window_bands = lax.dynamic_slice_in_dim(waves_row, window_row[0], NVW + NCW, 1)
    row_all = lax.all_gather(window_bands, "col", axis=2, tiled=True)
    dens_row = jnp.dot(
        pair_products(row_all[0], 0), plane_wave, preferred_element_type=jnp.float32
    ).astype(jnp.bfloat16)
    col_points = waves_col.shape[2]
    col_table = table_rows(plane_wave, lax.axis_index("row"), col_points)
    col_partial = jnp.dot(
        pair_products(waves_col[0], window_col[0]), col_table, preferred_element_type=jnp.float32
    )
    dens_col = lax.psum(col_partial, "row").astype(jnp.bfloat16)
    slots = owner_slot[transfer_table[:, 0]]
    chosen = screened[slots]
    whole = lax.all_to_all(chosen, "row", split_axis=0, concat_axis=1, tiled=True)
    weighted = lax.dot_general(
        whole[0], dens_col, (((1,), (1,)), ((), ())), preferred_element_type=jnp.float32
    ).astype(jnp.bfloat16)
    scale = (lax.axis_size("col") * NP) ** (-0.5)
    block_scale = NG ** (-0.5)
    block = (jnp.dot(dens_row, weighted, preferred_element_type=jnp.float32) * block_scale).astype(
        jnp.bfloat16
    )
    return lax.psum_scatter(
        (jnp.dot(block, trial, preferred_element_type=jnp.float32) * scale).astype(jnp.bfloat16),
        "col",
        scatter_dimension=0,
        tiled=True,
    ).astype(jnp.float32)


def solution(mesh):
    return jax.shard_map(
        shards,
        mesh=mesh,
        in_specs=(
            P("row", None, "col"),
            P("col", None, "row"),
            P("row"),
            P("col"),
            P(),
            P(None, "row", None),
            P(),
            P(None, "col"),
            P("col", None),
        ),
        out_specs=P(("row", "col"), None),
        check_vma=False,
    )
```

profile of v0, /device:TPU:0, one launch (start us, length us, event | category | flops | bytes accessed | tf_op | source)
XLA Modules:
  0.0 148.1 jit_solution(18441581295906073506)
XLA Ops:
  6.5 0.0 copy-start
  6.5 0.8 fusion.11
  7.4 1.3 gather_fusion
  8.7 0.0 copy-done
  8.7 2.0 %gather_fusion.1 = bf16[8,128,1024]{2,1,0:T(8,128)(2,1)} fusion(bf16[8,128,1024]{2,1,0:T(8,128)(2,1)S(1)} %copy-done, s32[1024]{0:T(1024)S(1)} %pad_clamp_fusion), kind=kCustom, calls=%fused_computation.1 | custom fusion | bytes 4194336 | tf_op jit(solution)/shard_map/gather | solution.py:47
  10.7 0.0 copy-start.3
  10.7 0.0 copy-start.2
  10.7 6.5 %all-to-all-start = ((bf16[8,128,1024]{2,1,0:T(8,128)(2,1)}), bf16[8,128,1024]{2,1,0:T(8,128)(2,1)}, u32[]{:S(2)}, u32[]{:S(2)}) async-start(bf16[8,128,1024]{2,1,0:T(8,128)(2,1)} %gather_fusion.1), calls=%async_computation | async-start | bytes 4194304 | tf_op jit(solution)/shard_map/all_to_all | solution.py:48
  17.2 0.0 reduce-scatter.2.cloned.1.call-start
  18.5 0.0 copy-done.3
  18.6 1.4 fusion.6
  19.9 0.0 copy-done.2
  20.0 8.5 %all_gather.3 = bf16[1,32,2048]{2,1,0:T(8,128)(2,1)S(1)} all-gather(bf16[1,32,512]{2,1,0:T(8,128)(2,1)S(1)} %constant_dynamic-slice_fusion), channel_id=1, replica_groups=mesh['row'=8,'col'=4] {'col'}, dimensions={2}, use_global_device_ids=true | all-gather | bytes 163840 | tf_op jit(solution)/shard_map/all_gather | solution.py:36
  28.5 0.2 multiply_convert_fusion
  28.6 4.3 %convolution_convert_fusion.1 = bf16[256,1024]{1,0:T(8,128)(2,1)} fusion(bf16[256,2048]{1,0:T(8,128)(2,1)S(1)} %bitcast.43, bf16[2048,1024]{1,0:T(8,128)(2,1)} %param.13), kind=kOutput, calls=%fused_computation.4 | convolution fusion | flops 1074003968 | bytes 5767168 | tf_op jit(solution)/shard_map/dot_general | solution.py:37
  32.9 79.8 %all-reduce.1 = bf16[256,1024]{1,0:T(8,128)(2,1)} all-reduce(f32[256,1024]{1,0:T(8,128)S(1)} %fusion.6), channel_id=1, replica_groups=mesh['row'=8,'col'=4] {'row'}, use_global_device_ids=true, to_apply=%region_0.0 | all-reduce | flops 262144 | bytes 1572864 | tf_op jit(solution)/shard_map/psum | solution.py:45
  112.7 0.0 all-to-all-done
  112.7 0.0 copy-start.1
  112.7 2.9 %fusion.3 = bf16[256,256]{1,0:T(8,128)(2,1)S(1)} fusion(bf16[256,1024]{1,0:T(8,128)(2,1)} %convolution_convert_fusion.1, bf16[1024,1024]{1,0:T(8,128)(2,1)} %bitcast.7, bf16[256,1024]{1,0:T(8,128)(2,1)} %all-reduce.1), kind=kOutput, calls=%fused_computation.9 | convolution fusion | flops 671481856 | bytes 3276800 | tf_op jit(solution)/shard_map/dot_general | solution.py:54
  115.6 0.0 copy-done.1
  115.7 0.9 fusion.1
  116.6 0.0 reduce-scatter.2.cloned.1.call-update
  116.6 23.1 %reduce-scatter.2.cloned.1.call-done = bf16[64,512]{1,0:T(8,128)(2,1)} async-done(((bf16[256,512]{1,0:T(8,128)(2,1)}), bf16[64,512]{1,0:T(8,128)(2,1)}) %reduce-scatter.2.cloned.1.call-update) | async-done | bytes 65552 | tf_op jit(solution)/shard_map/reduce_scatter | solution.py:57
  139.7 1.5 %convert_element_type.67 = f32[64,512]{1,0:T(8,128)} convert(bf16[64,512]{1,0:T(8,128)(2,1)} %reduce-scatter.2.cloned.1.call-done) | non-fusion elementwise | flops 32768 | bytes 196608 | tf_op jit(solution)/shard_map/convert_element_type | solution.py:62
  (7 shorter events, 0.1 us)
Async XLA Ops:
  6.5 2.1 %copy-start = (bf16[8,128,1024]{2,1,0:T(8,128)(2,1)S(1)}, bf16[8,128,1024]{2,1,0:T(8,128)(2,1)}, u32[]{:S(2)}) copy-start(bf16[8,128,1024]{2,1,0:T(8,128)(2,1)} %param.14) | copy-start | bytes 6291460
  10.7 7.8 %copy-start.3 = (bf16[1,64,256]{2,1,0:T(8,128)(2,1)S(1)}, bf16[1,64,256]{2,1,0:T(8,128)(2,1)}, u32[]{:S(2)}) copy-start(bf16[1,64,256]{2,1,0:T(8,128)(2,1)} %param.10) | copy-start | bytes 98308
  10.7 9.3 %copy-start.2 = (bf16[1,64,512]{2,1,0:T(8,128)(2,1)S(1)}, bf16[1,64,512]{2,1,0:T(8,128)(2,1)}, u32[]{:S(2)}) copy-start(bf16[1,64,512]{2,1,0:T(8,128)(2,1)} %param.9) | copy-start | bytes 196612
  10.7 102.0 %all-to-all-start = ((bf16[8,128,1024]{2,1,0:T(8,128)(2,1)}), bf16[8,128,1024]{2,1,0:T(8,128)(2,1)}, u32[]{:S(2)}, u32[]{:S(2)}) async-start(bf16[8,128,1024]{2,1,0:T(8,128)(2,1)} %gather_fusion.1), calls=%async_computation | async-start | bytes 4194304 | tf_op jit(solution)/shard_map/all_to_all | solution.py:48
  17.2 122.6 %reduce-scatter.2.cloned.1.call-start = ((), (), s32[]{:S(2)}) async-start(), calls=%async_computation.2 | async-start | bytes 327680 | tf_op jit(solution)/shard_map/reduce_scatter | solution.py:57
  112.7 2.9 %copy-start.1 = (bf16[256,512]{1,0:T(8,128)(2,1)S(1)}, bf16[256,512]{1,0:T(8,128)(2,1)}, u32[]{:S(2)}) copy-start(bf16[256,512]{1,0:T(8,128)(2,1)} %param.17) | copy-start | bytes 786436
Sparse Core Ops, SparseCore 0:
  116.7 22.9 reduce-scatter.1
where the time goes:
time: 148 us
  blocking collectives  88.3 us (60%)
  waiting for transfers between devices  23.1 us (16%)
  between operations  14.8 us (10%)
  matrix products  9.5 us (6%)
  starting transfers between devices  6.52 us (4%)
  local copies, waits for them, and re-layouts  3.31 us (2%)
  other arithmetic  2.56 us (2%)
    psum x1, blocking collectives, shards(): dens_col = lax.psum(col_partial, 'row').astype(jnp.bfloat16)  79.8 us
    reduce_scatter x1, waiting for transfers between devices, shards(): lax.psum_scatter((jnp.dot(block, trial, preferred_element_type=jnp.float3...  23.1 us
    all_gather x1, blocking collectives, shards(): row_all = lax.all_gather(window_bands, 'col', axis=2, tiled=True)  8.46 us
    all_to_all x1, starting transfers between devices, shards(): lax.all_to_all(chosen, 'row', split_axis=0, concat_axis=1, tiled=True)  6.49 us
    dot_general x1, matrix products, shards(): jnp.dot(pair_products(row_all[0], 0), plane_wave, preferred_element_type=...  4.29 us
  transfers between devices with their start and end apart: 2, of which 1 were waited for; matrix products, arithmetic and copies ran while one was open for 4% of the time, Pallas kernels for 0%

commit v1 on v0

v1 whole, which is shorter than its diff:
```python
import functools

import jax
import jax.numpy as jnp
from jax import lax
from jax.experimental import pallas as pl
from jax.experimental.pallas import tpu as pltpu
from jax.sharding import PartitionSpec as P

NVW = 16
NCW = 16
NP = NVW * NCW
GRANT = 16 << 20
VMEM = pl.BlockSpec(memory_space=pltpu.VMEM)
SMEM = pl.BlockSpec(memory_space=pltpu.SMEM)


def call(kernel, outs, *args, scratch=(), flops=0, moved=0, scalars=0):
    return pl.pallas_call(
        kernel,
        out_shape=outs,
        in_specs=[SMEM] * scalars + [VMEM] * (len(args) - scalars),
        out_specs=jax.tree.map(lambda _: VMEM, outs),
        scratch_shapes=list(scratch),
        cost_estimate=pl.CostEstimate(flops=flops, bytes_accessed=moved, transcendentals=0),
        compiler_params=pltpu.CompilerParams(vmem_limit_bytes=GRANT),
    )(*args)


def density_kernel(count, place_ref, *refs):
    pieces, (table_ref, out_ref, prod_ref) = refs[:count], refs[count:]
    for step, piece in enumerate(pieces):
        points = piece.shape[1]
        bands = piece[...].astype(jnp.float32)
        valence, conduction = bands[:NVW], bands[NVW:]
        products = (valence[:, None, :] * conduction[None, :, :]).reshape(NP, points)
        at = pl.multiple_of(place_ref[step] * points, 128)
        prod_ref[:, pl.ds(at, points)] = products.astype(jnp.bfloat16)
    out_ref[...] = jnp.dot(
        prod_ref[...], table_ref[...], preferred_element_type=jnp.float32
    ).astype(jnp.bfloat16)


def density(places, pieces, table):
    points, waves = table.shape
    return call(
        functools.partial(density_kernel, len(pieces)),
        jax.ShapeDtypeStruct((NP, waves), jnp.bfloat16),
        places,
        *pieces,
        table,
        scratch=[pltpu.VMEM((NP, points), jnp.bfloat16)],
        flops=2 * NP * points * waves,
        moved=2 * points * waves,
        scalars=1,
    )


def weighted_kernel(slots_ref, screened_ref, dens_ref, out_ref):
    def body(k, carry):
        out_ref[k] = lax.dot_general(
            screened_ref[slots_ref[k]],
            dens_ref[...],
            (((1,), (1,)), ((), ())),
            preferred_element_type=jnp.float32,
        ).astype(jnp.bfloat16)
        return carry

    lax.fori_loop(0, out_ref.shape[0], body, 0)


def gather_cols(x, axis):
    n = lax.axis_size(axis)
    return [x] + [lax.ppermute(x, axis, [(i, i ^ s) for i in range(n)]) for s in range(1, n)]


def partial_kernel(count, place_ref, scale_block, scale, *refs):
    dens_ref, pieces, (trial_ref, out_ref) = refs[0], refs[1 : 1 + count], refs[1 + count :]
    total = None
    for step, piece in enumerate(pieces):
        rows = piece.shape[0]
        at = pl.multiple_of(place_ref[step] * rows, 128)
        term = jnp.dot(dens_ref[:, pl.ds(at, rows)], piece[...], preferred_element_type=jnp.float32)
        total = term if total is None else total + term
    block = (total * scale_block).astype(jnp.bfloat16)
    applied = jnp.dot(block, trial_ref[...], preferred_element_type=jnp.float32) * scale
    out_ref[...] = applied.astype(jnp.bfloat16)


def shards(
    waves_row,
    waves_col,
    window_row,
    window_col,
    plane_wave,
    screened,
    owner_slot,
    transfer_table,
    trial,
):
    rows, cols = lax.axis_size("row"), lax.axis_size("col")
    chips = rows // 2
    me_row, me_col = lax.axis_index("row"), lax.axis_index("col")
    waves = plane_wave.shape[1]
    share = screened.shape[1]

    bands_col = lax.dynamic_slice_in_dim(waves_col[0], window_col[0], NVW + NCW, 0)
    bands_row = lax.dynamic_slice_in_dim(waves_row[0], window_row[0], NVW + NCW, 0)
    other = lax.ppermute(bands_col, "row", [(i, i ^ 1) for i in range(rows)])
    even = me_row % 2 == 0
    pair = jnp.concatenate(
        [jnp.where(even, bands_col, other), jnp.where(even, other, bands_col)], axis=1
    )
    chip_pieces = [pair] + [
        lax.ppermute(pair, "row", [(i, i ^ (2 * s)) for i in range(rows)]) for s in range(1, chips)
    ]
    row_pieces = gather_cols(bands_row, "col")

    dens_col = density((me_row // 2) ^ jnp.arange(chips), chip_pieces, plane_wave)
    slots = owner_slot[transfer_table[:, 0]]
    weighted = call(
        weighted_kernel,
        jax.ShapeDtypeStruct((rows, share, NP), jnp.bfloat16),
        slots,
        screened,
        dens_col,
        flops=2 * rows * share * waves * NP,
        moved=2 * rows * share * waves,
        scalars=1,
    ).reshape(chips, 2 * share, NP)

    def message(s):
        return lax.dynamic_index_in_dim(weighted, (me_row // 2) ^ s, 0, keepdims=False)

    arrived = [message(0)] + [
        lax.ppermute(message(s), "row", [(i, i ^ (2 * s)) for i in range(rows)])
        for s in range(1, chips)
    ]
    stack = jnp.stack(arrived).reshape(chips, 2, share, NP)
    mine = lax.dynamic_index_in_dim(stack, me_row % 2, 1, keepdims=False)
    theirs = lax.dynamic_index_in_dim(stack, 1 - me_row % 2, 1, keepdims=False)
    theirs = lax.ppermute(theirs, "row", [(i, i ^ 1) for i in range(rows)])
    pieces = [mine[s] for s in range(chips)] + [theirs[s] for s in range(chips)]
    order = (me_row // 2) ^ jnp.arange(chips)
    places = jnp.concatenate([2 * order + me_row % 2, 2 * order + 1 - me_row % 2])

    dens_row = density(me_col ^ jnp.arange(cols), row_pieces, plane_wave)
    scale = (cols * NP) ** (-0.5)

    def kernel(place_ref, *refs):
        partial_kernel(len(pieces), place_ref, waves ** (-0.5), scale, *refs)

    partial = call(
        kernel,
        jax.ShapeDtypeStruct((NP, trial.shape[1]), jnp.bfloat16),
        places,
        dens_row,
        *pieces,
        trial,
        flops=2 * NP * waves * NP + 2 * NP * NP * trial.shape[1],
        moved=2 * NP * waves,
        scalars=1,
    ).reshape(cols, NP // cols, trial.shape[1])

    def part(s):
        return lax.dynamic_index_in_dim(partial, me_col ^ s, 0, keepdims=False)

    total = part(0).astype(jnp.float32)
    for s in range(1, cols):
        total += lax.ppermute(part(s), "col", [(i, i ^ s) for i in range(cols)]).astype(jnp.float32)
    return total


def solution(mesh):
    return jax.shard_map(
        shards,
        mesh=mesh,
        in_specs=(
            P("row", None, "col"),
            P("col", None, "row"),
            P("row"),
            P("col"),
            P(),
            P(None, "row", None),
            P(),
            P(None, "col"),
            P("col", None),
        ),
        out_specs=P(("row", "col"), None),
        check_vma=False,
    )
```

time: 148 us -> 53.5 us (0.36)
  blocking collectives: 88.3 us -> 0 us
  between operations: 14.8 us -> 1.53 us
  starting transfers between devices: 6.52 us -> 16.7 us
  matrix products: 9.5 us -> 0 us
  Pallas kernels: 0 us -> 8.3 us
  waiting for transfers between devices: 23.1 us -> 17.6 us
  local copies, waits for them, and re-layouts: 3.31 us -> 6.74 us
    psum x1 -> x0, blocking collectives: 79.8 us -> none  [shards(): dens_col = lax.psum(col_partial, 'row').astype(jnp.bfloat16)]
    reduce_scatter x1 -> x0, waiting for transfers between devices: 23.1 us -> none  [shards(): lax.psum_scatter((jnp.dot(block, trial, preferred_element_type=jnp.float3...]
    ppermute x0 -> x14, waiting for transfers between devices: none -> 17.6 us  [the longest x3 6.39 us: shards(): lax.ppermute(message(s), 'row', [(i, i ^ 2 * s) for i in range(rows)])]
    ppermute x0 -> x14, starting transfers between devices: none -> 16.7 us  [the longest x3 5.03 us: gather_cols(): lax.ppermute(x, axis, [(i, i ^ s) for i in range(n)])]
    dot_general x4 -> x0, matrix products: 9.5 us -> none  [the longest x1 4.29 us: shards(): jnp.dot(pair_products(row_all[0], 0), plane_wave, preferred_element_type=...]
    all_gather x1 -> x0, blocking collectives: 8.46 us -> none  [shards(): row_all = lax.all_gather(window_bands, 'col', axis=2, tiled=True)]
    pallas_call x0 -> x4, Pallas kernels: none -> 8.3 us  [call(): pl.pallas_call(kernel, out_shape=outs, in_specs=[SMEM] * scalars + [VMEM]...]
    all_to_all x1 -> x0, starting transfers between devices: 6.49 us -> none  [shards(): lax.all_to_all(chosen, 'row', split_axis=0, concat_axis=1, tiled=True)]
  transfers between devices with their start and end apart: 2 -> 14, of which waited for: 1 -> 9; matrix products, arithmetic and copies ran while one was open for 4% -> 7% of each run, Pallas kernels for 0% -> 13%
where the time goes in v1:
time: 53.5 us; the launch traced here: 53.1 us
  waiting for transfers between devices  17.6 us (33%)
  starting transfers between devices  16.7 us (31%)
  Pallas kernels  8.3 us (16%)
  local copies, waits for them, and re-layouts  6.74 us (13%)
  other arithmetic  2.26 us (4%)
  between operations  1.53 us (3%)
    pallas_call x4, Pallas kernels, call(): pl.pallas_call(kernel, out_shape=outs, in_specs=[SMEM] * scalars + [VMEM]...  8.3 us
    ppermute x3, waiting for transfers between devices, shards(): lax.ppermute(message(s), 'row', [(i, i ^ 2 * s) for i in range(rows)])  6.39 us
    ppermute x3, starting transfers between devices, gather_cols(): lax.ppermute(x, axis, [(i, i ^ s) for i in range(n)])  5.03 us
    unnamed x10, local copies, waits for them, and re-layouts  4.54 us
    ppermute x3, starting transfers between devices, shards(): lax.ppermute(pair, 'row', [(i, i ^ 2 * s) for i in range(rows)])  4.45 us
    ppermute x3, waiting for transfers between devices, shards(): lax.ppermute(pair, 'row', [(i, i ^ 2 * s) for i in range(rows)])  4.16 us
    ppermute x3, waiting for transfers between devices, gather_cols(): lax.ppermute(x, axis, [(i, i ^ s) for i in range(n)])  3.84 us
    ppermute x3, starting transfers between devices, shards(): lax.ppermute(part(s), 'col', [(i, i ^ s) for i in range(cols)])  3.55 us
  transfers between devices with their start and end apart: 14, of which 9 were waited for; matrix products, arithmetic and copies ran while one was open for 7% of the time, Pallas kernels for 13%

profile of v1, /device:TPU:0, one launch (start us, length us, event | category | flops | bytes accessed | tf_op | source)
XLA Modules:
  0.0 53.1 jit_solution(14133021361309803421)
XLA Ops:
  0.0 0.0 copy-start
  0.7 0.1 copy-done
  0.9 3.0 %collective-permute-start = (bf16[32,512]{1,0:T(8,128)(2,1)S(1)}, bf16[32,512]{1,0:T(8,128)(2,1)S(1)}, u32[]{:S(2)}, u32[]{:S(2)}) collective-permute-start(bf16[32,512]{1,0:T(8,128)(2,1)S(1)} %dynamic-slice_bitcast_fusion.11.refs_0_), channel_id=1, source_target_pairs={{0,1},{1,0},{2,3},{3,2},{4,5},{5,4},{6,7},{7,6},{8,9},{9,8},{10,11... | collective-permute-start | bytes 98312 | tf_op jit(solution)/shard_map/ppermute | solution.py:74
  3.9 1.5 %collective-permute-start.1 = (bf16[32,512]{1,0:T(8,128)(2,1)S(1)}, bf16[32,512]{1,0:T(8,128)(2,1)S(1)}, u32[]{:S(2)}, u32[]{:S(2)}) collective-permute-start(bf16[32,512]{1,0:T(8,128)(2,1)S(1)} %dynamic-slice_bitcast_fusion.11.refs_0_), channel_id=1, source_target_pairs={{0,2},{1,3},{2,0},{3,1},{4,6},{5,7},{6,4},{7,5},{8,10},{9,11},{10,... | collective-permute-start | bytes 98312 | tf_op jit(solution)/shard_map/ppermute | solution.py:74
  6.1 0.7 %dynamic-slice_bitcast_fusion.12 = bf16[32,256]{1,0:T(8,128)(2,1)S(1)} fusion(bf16[1,64,256]{2,1,0:T(8,128)(2,1)} %param.10, s32[]{:T(128)S(6)} %select_n.84), kind=kLoop, calls=%fused_computation.22 | loop fusion | bytes 32772 | tf_op jit(solution)/shard_map/dynamic_slice | solution.py:107
  6.8 0.0 collective-permute-start.3
  6.8 0.7 %fusion.2 = s32[8]{0:T(128)S(1)} fusion(s32[8,1]{0,1:T(1,128)} %param.16), kind=kLoop, calls=%fused_computation.28 | loop fusion | flops 24 | bytes 64 | tf_op jit(solution)/shard_map/select_n | solution.py:120
  7.5 0.5 collective-permute-done.3
  8.0 0.7 %broadcast_select_fusion.1 = (bf16[32,256]{1,0:T(8,128)(2,1)S(1)}, bf16[32,256]{1,0:T(8,128)(2,1)S(1)}) fusion(bf16[32,256]{1,0:T(8,128)(2,1)S(1)} %collective-permute-done.3, pred[]{:T(512)S(6)} %eq.9, bf16[1,64,256]{2,1,0:T(8,128)(2,1)} %param.10, s32[]{:T(128)S(6)} %select_n.84), kind=kLoop, calls=%fused_computation.24 | loop fusion | flops 16384 | bytes 65541 | tf_op jit(solution)/shard_map/jit(_where)/select_n | solution.py:112
  8.7 1.6 %collective-permute-start.4 = (bf16[32,512]{1,0:T(8,128)(2,1)S(1)}, bf16[32,512]{1,0:T(8,128)(2,1)S(1)}, u32[]{:S(2)}, u32[]{:S(2)}) collective-permute-start(bf16[32,512]{1,0:T(8,128)(2,1)S(1)} %pad_maximum_fusion.1.refs_0_), channel_id=1, source_target_pairs={{0,8},{4,12},{8,0},{12,4},{16,24},{20,28},{24,16},{28,20},{1,9},{5... | collective-permute-start | bytes 98312 | tf_op jit(solution)/shard_map/ppermute | solution.py:115
  10.4 2.6 %collective-permute-start.5 = (bf16[32,512]{1,0:T(8,128)(2,1)S(1)}, bf16[32,512]{1,0:T(8,128)(2,1)S(1)}, u32[]{:S(2)}, u32[]{:S(2)}) collective-permute-start(bf16[32,512]{1,0:T(8,128)(2,1)S(1)} %pad_maximum_fusion.1.refs_0_), channel_id=1, source_target_pairs={{0,16},{4,20},{8,24},{12,28},{16,0},{20,4},{24,8},{28,12},{1,17},{... | collective-permute-start | bytes 98312 | tf_op jit(solution)/shard_map/ppermute | solution.py:115
  13.0 0.2 collective-permute-start.6
  13.2 1.3 %gather_fusion = s32[8]{0:T(128)S(1)} fusion(s32[8]{0:T(128)} %param.15, s32[1024]{0:T(1024)S(1)} %pad_clamp_fusion), kind=kCustom, calls=%fused_computation | custom fusion | bytes 96 | tf_op jit(solution)/shard_map/gather | solution.py:120
  14.5 0.0 collective-permute-done.4.refs_1_
  14.5 1.3 %collective-permute-done.5.refs_2_ = bf16[32,512]{1,0:T(8,128)(2,1)S(1)} collective-permute-done((bf16[32,512]{1,0:T(8,128)(2,1)S(1)}, bf16[32,512]{1,0:T(8,128)(2,1)S(1)}, u32[]{:S(2)}, u32[]{:S(2)}) %collective-permute-start.5) | collective-permute-done | bytes 32800 | tf_op jit(solution)/shard_map/ppermute | solution.py:115
  15.8 2.9 %collective-permute-done.6.refs_3_ = bf16[32,512]{1,0:T(8,128)(2,1)S(1)} collective-permute-done((bf16[32,512]{1,0:T(8,128)(2,1)S(1)}, bf16[32,512]{1,0:T(8,128)(2,1)S(1)}, u32[]{:S(2)}, u32[]{:S(2)}) %collective-permute-start.6) | collective-permute-done | bytes 32800 | tf_op jit(solution)/shard_map/ppermute | solution.py:115
  18.7 0.0 copy-start.1
  18.7 2.2 %copy-done.1 = bf16[2048,1024]{1,0:T(8,128)(2,1)S(1)} copy-done((bf16[2048,1024]{1,0:T(8,128)(2,1)S(1)}, bf16[2048,1024]{1,0:T(8,128)(2,1)}, u32[]{:S(2)}) %copy-start.1) | copy-done | bytes 4194328
  20.9 0.0 copy-start.3
  20.9 2.0 %shard_map.92.dens_ref = bf16[256,1024]{1,0:T(8,128)(2,1)S(1)} custom-call(s32[4]{0:T(128)S(1)} %iota_xor_fusion.1.place_ref, bf16[32,512]{1,0:T(8,128)(2,1)S(1)} %pad_maximum_fusion.1.refs_0_, bf16[32,512]{1,0:T(8,128)(2,1)S(1)} %collective-permute-done.4.refs_1_, bf16[32,512]{1,0:T(8,128)(2,1)S(1)} %collective-permute-done.5.refs_2_, ...), custom_call_target="tpu_custom_call" | custom-call | flops 1073741824 | bytes 4194304 | tf_op jit(solution)/shard_map/pallas_call | solution.py:19
  22.9 0.0 copy-done.3
  22.9 3.0 %shard_map.93 = bf16[8,128,256]{2,1,0:T(8,128)(2,1)S(1)} custom-call(s32[8]{0:T(128)S(1)} %gather_fusion, bf16[8,128,1024]{2,1,0:T(8,128)(2,1)S(1)} %copy-done.3, bf16[256,1024]{1,0:T(8,128)(2,1)S(1)} %shard_map.92.dens_ref), custom_call_target="tpu_custom_call" | custom-call | flops 536870912 | bytes 2097152 | tf_op jit(solution)/shard_map/pallas_call | solution.py:19
  25.9 0.0 copy-start.4
  26.0 0.1 collective-permute-start.8
  26.1 1.0 %collective-permute-start.9 = (bf16[256,256]{1,0:T(8,128)(2,1)S(1)}, bf16[256,256]{1,0:T(8,128)(2,1)S(1)}, u32[]{:S(2)}, u32[]{:S(2)}) collective-permute-start(bf16[256,256]{1,0:T(8,128)(2,1)S(1)} %get-tuple-element.10), channel_id=1, source_target_pairs={{0,24},{4,28},{8,16},{12,20},{16,8},{20,12},{24,0},{28,4},{1,25},{... | collective-permute-start | bytes 393224 | tf_op jit(solution)/shard_map/ppermute | solution.py:136
  27.1 2.5 %collective-permute-start.7 = (bf16[256,256]{1,0:T(8,128)(2,1)S(1)}, bf16[256,256]{1,0:T(8,128)(2,1)S(1)}, u32[]{:S(2)}, u32[]{:S(2)}) collective-permute-start(bf16[256,256]{1,0:T(8,128)(2,1)S(1)} %get-tuple-element.12), channel_id=1, source_target_pairs={{0,8},{4,12},{8,0},{12,4},{16,24},{20,28},{24,16},{28,20},{1,9},{5... | collective-permute-start | bytes 393224 | tf_op jit(solution)/shard_map/ppermute | solution.py:136
  29.6 6.2 %collective-permute-done.8 = bf16[256,256]{1,0:T(8,128)(2,1)S(1)} collective-permute-done((bf16[256,256]{1,0:T(8,128)(2,1)S(1)}, bf16[256,256]{1,0:T(8,128)(2,1)S(1)}, u32[]{:S(2)}, u32[]{:S(2)}) %collective-permute-start.8) | collective-permute-done | bytes 131104 | tf_op jit(solution)/shard_map/ppermute | solution.py:136
  35.7 0.5 collective-permute-start.2
  36.2 0.0 collective-permute-done.9
  36.2 0.2 collective-permute-done.7
  36.4 0.1 pad_maximum_fusion
  36.5 0.1 collective-permute-start.10
  36.6 0.1 pad_add_fusion.place_ref
  36.7 0.0 collective-permute-done.refs_1_
  36.7 0.0 collective-permute-done.1.refs_2_
  36.7 3.8 %collective-permute-done.2.refs_3_ = bf16[32,512]{1,0:T(8,128)(2,1)S(1)} collective-permute-done((bf16[32,512]{1,0:T(8,128)(2,1)S(1)}, bf16[32,512]{1,0:T(8,128)(2,1)S(1)}, u32[]{:S(2)}, u32[]{:S(2)}) %collective-permute-start.2) | collective-permute-done | bytes 32800 | tf_op jit(solution)/shard_map/ppermute | solution.py:74
  40.5 0.0 copy-start.2
  40.6 2.2 %copy-done.2 = bf16[2048,1024]{1,0:T(8,128)(2,1)S(1)} copy-done((bf16[2048,1024]{1,0:T(8,128)(2,1)S(1)}, bf16[2048,1024]{1,0:T(8,128)(2,1)}, u32[]{:S(2)}) %copy-start.2) | copy-done | bytes 4194328
  42.7 2.1 %shard_map.91.refs_0_ = bf16[256,1024]{1,0:T(8,128)(2,1)S(1)} custom-call(s32[4]{0:T(128)S(1)} %iota_xor_fusion.place_ref, bf16[32,512]{1,0:T(8,128)(2,1)S(1)} %dynamic-slice_bitcast_fusion.11.refs_0_, bf16[32,512]{1,0:T(8,128)(2,1)S(1)} %collective-permute-done.refs_1_, bf16[32,512]{1,0:T(8,128)(2,1)S(1)} %collective-permute-done.1.refs_2_, ...), custom_call_target="tpu_custom_call" | custom-call | flops 1073741824 | bytes 4194304 | tf_op jit(solution)/shard_map/pallas_call | solution.py:19
  44.8 0.0 collective-permute-done.10
  44.9 0.0 copy-done.4
  44.9 1.2 %shard_map.94 = bf16[256,512]{1,0:T(8,128)(2,1)S(1)} custom-call(s32[8]{0:T(128)S(1)} %pad_add_fusion.place_ref, bf16[256,1024]{1,0:T(8,128)(2,1)S(1)} %shard_map.91.refs_0_, bf16[128,256]{1,0:T(8,128)(2,1)S(1)} %get-tuple-element.8.refs_1_, bf16[128,256]{1,0:T(8,128)(2,1)S(1)} %get-tuple-element.7.refs_2_, bf16[128,256]{1,0:T(8,128)(2,1)S(1)} %get-tuple-element.6.refs_3_, ...), custom_call_target="tpu_custom_call" | custom-call | flops 201326592 | bytes 524288 | tf_op jit(solution)/shard_map/pallas_call | solution.py:19
  46.1 0.6 %collective-permute-start.11 = (bf16[64,512]{1,0:T(8,128)(2,1)S(1)}, bf16[64,512]{1,0:T(8,128)(2,1)S(1)}, u32[]{:S(2)}, u32[]{:S(2)}) collective-permute-start(bf16[64,512]{1,0:T(8,128)(2,1)S(1)} %get-tuple-element.13), channel_id=1, source_target_pairs={{0,1},{1,0},{2,3},{3,2},{4,5},{5,4},{6,7},{7,6},{8,9},{9,8},{10,11... | collective-permute-start | bytes 196616 | tf_op jit(solution)/shard_map/ppermute | solution.py:170
  46.7 0.5 collective-permute-start.12
  47.3 2.4 %collective-permute-start.13 = (bf16[64,512]{1,0:T(8,128)(2,1)S(1)}, bf16[64,512]{1,0:T(8,128)(2,1)S(1)}, u32[]{:S(2)}, u32[]{:S(2)}) collective-permute-start(bf16[64,512]{1,0:T(8,128)(2,1)S(1)} %get-tuple-element.14), channel_id=1, source_target_pairs={{0,3},{1,2},{2,1},{3,0},{4,7},{5,6},{6,5},{7,4},{8,11},{9,10},{10,... | collective-permute-start | bytes 196616 | tf_op jit(solution)/shard_map/ppermute | solution.py:170
  49.7 0.8 %collective-permute-done.11 = bf16[64,512]{1,0:T(8,128)(2,1)S(1)} collective-permute-done((bf16[64,512]{1,0:T(8,128)(2,1)S(1)}, bf16[64,512]{1,0:T(8,128)(2,1)S(1)}, u32[]{:S(2)}, u32[]{:S(2)}) %collective-permute-start.11) | collective-permute-done | bytes 65568 | tf_op jit(solution)/shard_map/ppermute | solution.py:170
  50.5 0.5 %collective-permute-done.12 = bf16[64,512]{1,0:T(8,128)(2,1)S(1)} collective-permute-done((bf16[64,512]{1,0:T(8,128)(2,1)S(1)}, bf16[64,512]{1,0:T(8,128)(2,1)S(1)}, u32[]{:S(2)}, u32[]{:S(2)}) %collective-permute-start.12) | collective-permute-done | bytes 65568 | tf_op jit(solution)/shard_map/ppermute | solution.py:170
  51.0 1.4 %collective-permute-done.13 = bf16[64,512]{1,0:T(8,128)(2,1)S(1)} collective-permute-done((bf16[64,512]{1,0:T(8,128)(2,1)S(1)}, bf16[64,512]{1,0:T(8,128)(2,1)S(1)}, u32[]{:S(2)}, u32[]{:S(2)}) %collective-permute-start.13) | collective-permute-done | bytes 65568 | tf_op jit(solution)/shard_map/ppermute | solution.py:170
  52.4 0.7 %fusion.1 = f32[64,512]{1,0:T(8,128)} fusion(bf16[64,512]{1,0:T(8,128)(2,1)S(1)} %collective-permute-done.13, bf16[64,512]{1,0:T(8,128)(2,1)S(1)} %collective-permute-done.12, bf16[64,512]{1,0:T(8,128)(2,1)S(1)} %collective-permute-done.11, bf16[4,64,512]{2,1,0:T(8,128)(2,1)S(1)} %bitcast.57, s32[]{:T(128)S(6)} %select_n.93), kind=kLoop, calls=%fused_computation.5 | loop fusion | flops 229376 | bytes 393220 | tf_op jit(solution)/shard_map/add | solution.py:170
  (11 shorter events, 0.2 us)
Async XLA Ops:
  0.0 0.8 %copy-start = (bf16[1,64,512]{2,1,0:T(8,128)(2,1)S(1)}, bf16[1,64,512]{2,1,0:T(8,128)(2,1)}, u32[]{:S(2)}) copy-start(bf16[1,64,512]{2,1,0:T(8,128)(2,1)} %param.9) | copy-start | bytes 196612
  0.9 35.8 %collective-permute-start = (bf16[32,512]{1,0:T(8,128)(2,1)S(1)}, bf16[32,512]{1,0:T(8,128)(2,1)S(1)}, u32[]{:S(2)}, u32[]{:S(2)}) collective-permute-start(bf16[32,512]{1,0:T(8,128)(2,1)S(1)} %dynamic-slice_bitcast_fusion.11.refs_0_), channel_id=1, source_target_pairs={{0,1},{1,0},{2,3},{3,2},{4,5},{5,4},{6,7},{7,6},{8,9},{9,8},{10,11... | collective-permute-start | bytes 98312 | tf_op jit(solution)/shard_map/ppermute | solution.py:74
  3.9 32.8 %collective-permute-start.1 = (bf16[32,512]{1,0:T(8,128)(2,1)S(1)}, bf16[32,512]{1,0:T(8,128)(2,1)S(1)}, u32[]{:S(2)}, u32[]{:S(2)}) collective-permute-start(bf16[32,512]{1,0:T(8,128)(2,1)S(1)} %dynamic-slice_bitcast_fusion.11.refs_0_), channel_id=1, source_target_pairs={{0,2},{1,3},{2,0},{3,1},{4,6},{5,7},{6,4},{7,5},{8,10},{9,11},{10,... | collective-permute-start | bytes 98312 | tf_op jit(solution)/shard_map/ppermute | solution.py:74
  6.8 1.2 %collective-permute-start.3 = (bf16[32,256]{1,0:T(8,128)(2,1)S(1)}, bf16[32,256]{1,0:T(8,128)(2,1)S(1)}, u32[]{:S(2)}, u32[]{:S(2)}) collective-permute-start(bf16[32,256]{1,0:T(8,128)(2,1)S(1)} %dynamic-slice_bitcast_fusion.12), channel_id=1, source_target_pairs={{0,4},{4,0},{8,12},{12,8},{16,20},{20,16},{24,28},{28,24},{1,5},{5... | collective-permute-start | bytes 49160 | tf_op jit(solution)/shard_map/ppermute | solution.py:109
  8.7 5.8 %collective-permute-start.4 = (bf16[32,512]{1,0:T(8,128)(2,1)S(1)}, bf16[32,512]{1,0:T(8,128)(2,1)S(1)}, u32[]{:S(2)}, u32[]{:S(2)}) collective-permute-start(bf16[32,512]{1,0:T(8,128)(2,1)S(1)} %pad_maximum_fusion.1.refs_0_), channel_id=1, source_target_pairs={{0,8},{4,12},{8,0},{12,4},{16,24},{20,28},{24,16},{28,20},{1,9},{5... | collective-permute-start | bytes 98312 | tf_op jit(solution)/shard_map/ppermute | solution.py:115
  10.4 5.4 %collective-permute-start.5 = (bf16[32,512]{1,0:T(8,128)(2,1)S(1)}, bf16[32,512]{1,0:T(8,128)(2,1)S(1)}, u32[]{:S(2)}, u32[]{:S(2)}) collective-permute-start(bf16[32,512]{1,0:T(8,128)(2,1)S(1)} %pad_maximum_fusion.1.refs_0_), channel_id=1, source_target_pairs={{0,16},{4,20},{8,24},{12,28},{16,0},{20,4},{24,8},{28,12},{1,17},{... | collective-permute-start | bytes 98312 | tf_op jit(solution)/shard_map/ppermute | solution.py:115
  13.0 5.7 %collective-permute-start.6 = (bf16[32,512]{1,0:T(8,128)(2,1)S(1)}, bf16[32,512]{1,0:T(8,128)(2,1)S(1)}, u32[]{:S(2)}, u32[]{:S(2)}) collective-permute-start(bf16[32,512]{1,0:T(8,128)(2,1)S(1)} %pad_maximum_fusion.1.refs_0_), channel_id=1, source_target_pairs={{0,24},{4,28},{8,16},{12,20},{16,8},{20,12},{24,0},{28,4},{1,25},{... | collective-permute-start | bytes 98312 | tf_op jit(solution)/shard_map/ppermute | solution.py:115
  18.7 2.2 %copy-start.1 = (bf16[2048,1024]{1,0:T(8,128)(2,1)S(1)}, bf16[2048,1024]{1,0:T(8,128)(2,1)}, u32[]{:S(2)}) copy-start(bf16[2048,1024]{1,0:T(8,128)(2,1)} %refs_4_.3) | copy-start | bytes 12582916
  20.9 2.0 %copy-start.3 = (bf16[8,128,1024]{2,1,0:T(8,128)(2,1)S(1)}, bf16[8,128,1024]{2,1,0:T(8,128)(2,1)}, u32[]{:S(2)}) copy-start(bf16[8,128,1024]{2,1,0:T(8,128)(2,1)} %screened_ref.1) | copy-start | bytes 6291460
  25.9 18.9 %copy-start.4 = (bf16[256,512]{1,0:T(8,128)(2,1)S(1)}, bf16[256,512]{1,0:T(8,128)(2,1)}, u32[]{:S(2)}) copy-start(bf16[256,512]{1,0:T(8,128)(2,1)} %refs_9_.1) | copy-start | bytes 786436
  26.0 9.7 %collective-permute-start.8 = (bf16[256,256]{1,0:T(8,128)(2,1)S(1)}, bf16[256,256]{1,0:T(8,128)(2,1)S(1)}, u32[]{:S(2)}, u32[]{:S(2)}) collective-permute-start(bf16[256,256]{1,0:T(8,128)(2,1)S(1)} %get-tuple-element.11), channel_id=1, source_target_pairs={{0,16},{4,20},{8,24},{12,28},{16,0},{20,4},{24,8},{28,12},{1,17},{... | collective-permute-start | bytes 393224 | tf_op jit(solution)/shard_map/ppermute | solution.py:136
  26.1 10.1 %collective-permute-start.9 = (bf16[256,256]{1,0:T(8,128)(2,1)S(1)}, bf16[256,256]{1,0:T(8,128)(2,1)S(1)}, u32[]{:S(2)}, u32[]{:S(2)}) collective-permute-start(bf16[256,256]{1,0:T(8,128)(2,1)S(1)} %get-tuple-element.10), channel_id=1, source_target_pairs={{0,24},{4,28},{8,16},{12,20},{16,8},{20,12},{24,0},{28,4},{1,25},{... | collective-permute-start | bytes 393224 | tf_op jit(solution)/shard_map/ppermute | solution.py:136
  27.1 9.4 %collective-permute-start.7 = (bf16[256,256]{1,0:T(8,128)(2,1)S(1)}, bf16[256,256]{1,0:T(8,128)(2,1)S(1)}, u32[]{:S(2)}, u32[]{:S(2)}) collective-permute-start(bf16[256,256]{1,0:T(8,128)(2,1)S(1)} %get-tuple-element.12), channel_id=1, source_target_pairs={{0,8},{4,12},{8,0},{12,4},{16,24},{20,28},{24,16},{28,20},{1,9},{5... | collective-permute-start | bytes 393224 | tf_op jit(solution)/shard_map/ppermute | solution.py:136
  35.7 4.8 %collective-permute-start.2 = (bf16[32,512]{1,0:T(8,128)(2,1)S(1)}, bf16[32,512]{1,0:T(8,128)(2,1)S(1)}, u32[]{:S(2)}, u32[]{:S(2)}) collective-permute-start(bf16[32,512]{1,0:T(8,128)(2,1)S(1)} %dynamic-slice_bitcast_fusion.11.refs_0_), channel_id=1, source_target_pairs={{0,3},{1,2},{2,1},{3,0},{4,7},{5,6},{6,5},{7,4},{8,11},{9,10},{10,... | collective-permute-start | bytes 98312 | tf_op jit(solution)/shard_map/ppermute | solution.py:74
  36.5 8.3 %collective-permute-start.10 = (bf16[4,128,256]{2,1,0:T(8,128)(2,1)S(1)}, bf16[4,128,256]{2,1,0:T(8,128)(2,1)S(1)}, u32[]{:S(2)}, u32[]{:S(2)}) collective-permute-start(bf16[4,128,256]{2,1,0:T(8,128)(2,1)S(1)} %dynamic-slice_bitcast_fusion), channel_id=1, source_target_pairs={{0,4},{4,0},{8,12},{12,8},{16,20},{20,16},{24,28},{28,24},{1,5},{5... | collective-permute-start | bytes 786440 | tf_op jit(solution)/shard_map/ppermute | solution.py:142
  40.5 2.2 %copy-start.2 = (bf16[2048,1024]{1,0:T(8,128)(2,1)S(1)}, bf16[2048,1024]{1,0:T(8,128)(2,1)}, u32[]{:S(2)}) copy-start(bf16[2048,1024]{1,0:T(8,128)(2,1)} %refs_4_.3) | copy-start | bytes 12582916
  46.1 4.3 %collective-permute-start.11 = (bf16[64,512]{1,0:T(8,128)(2,1)S(1)}, bf16[64,512]{1,0:T(8,128)(2,1)S(1)}, u32[]{:S(2)}, u32[]{:S(2)}) collective-permute-start(bf16[64,512]{1,0:T(8,128)(2,1)S(1)} %get-tuple-element.13), channel_id=1, source_target_pairs={{0,1},{1,0},{2,3},{3,2},{4,5},{5,4},{6,7},{7,6},{8,9},{9,8},{10,11... | collective-permute-start | bytes 196616 | tf_op jit(solution)/shard_map/ppermute | solution.py:170
  46.7 4.3 %collective-permute-start.12 = (bf16[64,512]{1,0:T(8,128)(2,1)S(1)}, bf16[64,512]{1,0:T(8,128)(2,1)S(1)}, u32[]{:S(2)}, u32[]{:S(2)}) collective-permute-start(bf16[64,512]{1,0:T(8,128)(2,1)S(1)} %get-tuple-element.15), channel_id=1, source_target_pairs={{0,2},{1,3},{2,0},{3,1},{4,6},{5,7},{6,4},{7,5},{8,10},{9,11},{10,... | collective-permute-start | bytes 196616 | tf_op jit(solution)/shard_map/ppermute | solution.py:170
  47.3 5.2 %collective-permute-start.13 = (bf16[64,512]{1,0:T(8,128)(2,1)S(1)}, bf16[64,512]{1,0:T(8,128)(2,1)S(1)}, u32[]{:S(2)}, u32[]{:S(2)}) collective-permute-start(bf16[64,512]{1,0:T(8,128)(2,1)S(1)} %get-tuple-element.14), channel_id=1, source_target_pairs={{0,3},{1,2},{2,1},{3,0},{4,7},{5,6},{6,5},{7,4},{8,11},{9,10},{10,... | collective-permute-start | bytes 196616 | tf_op jit(solution)/shard_map/ppermute | solution.py:170

commit v2 on v0

v2 whole, which is shorter than its diff:
```python
import functools

import jax
import jax.numpy as jnp
from jax import lax
from jax.experimental import pallas as pl
from jax.experimental.pallas import tpu as pltpu
from jax.sharding import PartitionSpec as P


NVW = 16
NCW = 16
NP = NVW * NCW
GRANT = 16 << 20
VMEM = pl.BlockSpec(memory_space=pltpu.VMEM)
SMEM = pl.BlockSpec(memory_space=pltpu.SMEM)


def call(kernel, outs, *args, spaces, scratch=(), flops=0, moved=0):
    return pl.pallas_call(
        kernel,
        out_shape=outs,
        in_specs=spaces,
        out_specs=jax.tree.map(lambda _: VMEM, outs),
        scratch_shapes=list(scratch),
        cost_estimate=pl.CostEstimate(flops=flops, bytes_accessed=moved, transcendentals=0),
        compiler_params=pltpu.CompilerParams(vmem_limit_bytes=GRANT),
    )(*args)


def swap(x, axis, step):
    return lax.ppermute(x, axis, [(i, i ^ step) for i in range(lax.axis_size(axis))])


def density_kernel(todo, place_ref, bands_ref, table_ref, *refs):
    addend_ref, out_ref, prod_ref = refs if len(refs) == 3 else (None, *refs)
    _, _, points = bands_ref.shape
    for s in todo:
        bands = bands_ref[s].astype(jnp.float32)
        products = bands[:NVW][:, None, :] * bands[NVW:][None, :, :]
        prod_ref[s] = products.reshape(NP, points).astype(jnp.bfloat16)
    waves = table_ref.shape[1]
    tile = min(256, waves)
    for n in range(0, waves, tile):
        total = None if addend_ref is None else addend_ref[:, n : n + tile]
        for s in todo:
            at = pl.multiple_of(place_ref[s] * points, points)
            term = jnp.dot(
                prod_ref[s],
                table_ref[pl.ds(at, points), n : n + tile],
                preferred_element_type=jnp.float32,
            )
            total = term if total is None else total + term
        out_ref[:, n : n + tile] = total.astype(out_ref.dtype)


def density(places, bands, table, addend=None, final=True, todo=None):
    waves = table.shape[1]
    count, _, points = bands.shape
    todo = range(count) if todo is None else todo
    more = [] if addend is None else [addend]
    return call(
        functools.partial(density_kernel, todo),
        jax.ShapeDtypeStruct((NP, waves), jnp.bfloat16 if final else jnp.float32),
        places,
        bands,
        table,
        *more,
        spaces=[SMEM, VMEM, VMEM] + [VMEM] * len(more),
        scratch=[pltpu.VMEM((count, NP, points), jnp.bfloat16)],
        flops=2 * NP * len(todo) * points * waves,
        moved=2 * len(todo) * points * waves,
    )


def weighted_kernel(me_ref, owner_ref, transfer_ref, screened_ref, dens_ref, keep_ref, give_ref, all_ref):
    slots, share, waves = screened_ref.shape
    whole = lax.dot_general(
        screened_ref[...].reshape(slots * share, waves),
        dens_ref[...],
        (((1,), (1,)), ((), ())),
        preferred_element_type=jnp.float32,
    )
    all_ref[...] = whole.astype(jnp.bfloat16).reshape(slots, share, NP)
    me = me_ref[0]
    for s in range(slots // 2):
        to = me ^ (2 * s)
        keep_ref[s] = all_ref[owner_ref[transfer_ref[to]]]
        give_ref[s] = all_ref[owner_ref[transfer_ref[to ^ 1]]]


def block_kernel(me_row_ref, me_col_ref, dens_ref, *refs):
    count = dens_ref.shape[1] // refs[0].shape[0]
    pieces, outs, (weighted_ref, block_ref) = refs[:count], refs[count:-2], refs[-2:]
    me = me_row_ref[0]
    for s, piece in enumerate(pieces):
        share = piece.shape[0] // 2
        first = me ^ (2 * s)
        weighted_ref[pl.ds(pl.multiple_of(first * share, share), share), :] = piece[:share]
        second = first ^ 1
        weighted_ref[pl.ds(pl.multiple_of(second * share, share), share), :] = piece[share:]
    block = jnp.dot(dens_ref[...], weighted_ref[...], preferred_element_type=jnp.float32)
    block_ref[...] = (block * dens_ref.shape[1] ** (-0.5)).astype(jnp.bfloat16)
    rows = outs[0].shape[0]
    for s, out in enumerate(outs):
        at = pl.multiple_of((me_col_ref[0] ^ s) * rows, rows)
        out[...] = block_ref[pl.ds(at, rows), :]


def apply_kernel(scale, *refs):
    count = len(refs) // 2
    total = None
    for block, trial in zip(refs[:count], refs[count:-1]):
        term = jnp.dot(block[...], trial[...], preferred_element_type=jnp.float32)
        total = term if total is None else total + term
    refs[-1][...] = total * scale


def shards(
    waves_row,
    waves_col,
    window_row,
    window_col,
    plane_wave,
    screened,
    owner_slot,
    transfer_table,
    trial,
):
    rows, cols = lax.axis_size("row"), lax.axis_size("col")
    chips = rows // 2
    me_row, me_col = lax.axis_index("row"), lax.axis_index("col")
    waves, share = plane_wave.shape[1], screened.shape[1]
    steps = jnp.arange(chips, dtype=jnp.int32)

    bands = lax.dynamic_slice_in_dim(waves_col[0], window_col[0], NVW + NCW, 0)[None]
    near = me_row ^ (2 * steps)
    own = density(near, bands, plane_wave, final=False)
    step = 2
    while step < rows:
        bands = jnp.concatenate([bands, swap(bands, "row", step)])
        step *= 2
    other = swap(bands, "row", 1)
    half = density(near, bands, plane_wave, own, final=False, todo=range(1, chips))
    dens_col = density(near ^ 1, other, plane_wave, half)

    piece = jax.ShapeDtypeStruct((chips, share, NP), jnp.bfloat16)
    keep, give = call(
        weighted_kernel,
        (piece, piece),
        me_row[None],
        owner_slot,
        transfer_table[:, 0],
        screened,
        dens_col,
        spaces=[SMEM, SMEM, SMEM, VMEM, VMEM],
        scratch=[pltpu.VMEM((rows, share, NP), jnp.bfloat16)],
        flops=2 * rows * share * waves * NP,
        moved=2 * rows * share * waves,
    )
    both = jnp.concatenate([keep, swap(give, "row", 1)], axis=1)
    pieces = [both[0]] + [None] * (chips - 1)
    for s in [*range(2, chips), 1]:
        pieces[s] = swap(both[s], "row", 2 * s)

    late_waves, late_trial, _ = lax.optimization_barrier((waves_row, trial, both))
    bands_row = lax.dynamic_slice_in_dim(late_waves[0], window_row[0], NVW + NCW, 0)
    row_bands = jnp.stack([bands_row] + [swap(bands_row, "col", s) for s in range(1, cols)])
    dens_row = density(me_col ^ jnp.arange(cols, dtype=jnp.int32), row_bands, plane_wave)
    trials = [late_trial] + [swap(late_trial, "col", s) for s in range(1, cols)]

    lines = call(
        block_kernel,
        [jax.ShapeDtypeStruct((NP // cols, NP), jnp.bfloat16)] * cols,
        me_row[None],
        me_col[None],
        dens_row,
        *pieces,
        spaces=[SMEM, SMEM] + [VMEM] * (1 + chips),
        scratch=[pltpu.VMEM((waves, NP), jnp.bfloat16), pltpu.VMEM((NP, NP), jnp.bfloat16)],
        flops=2 * NP * waves * NP,
        moved=2 * waves * NP,
    )
    lines = [lines[0]] + [swap(lines[s], "col", s) for s in range(1, cols)]
    return call(
        functools.partial(apply_kernel, (cols * NP) ** (-0.5)),
        jax.ShapeDtypeStruct((NP // cols, trial.shape[1]), jnp.float32),
        *lines,
        *trials,
        spaces=[VMEM] * (2 * cols),
        flops=2 * NP * NP * trial.shape[1],
        moved=2 * cols * NP * trial.shape[1],
    )


def solution(mesh):
    return jax.shard_map(
        shards,
        mesh=mesh,
        in_specs=(
            P("row", None, "col"),
            P("col", None, "row"),
            P("row"),
            P("col"),
            P(),
            P(None, "row", None),
            P(),
            P(None, "col"),
            P("col", None),
        ),
        out_specs=P(("row", "col"), None),
        check_vma=False,
    )
```

time: 148 us -> 52.1 us (0.35)
  blocking collectives: 88.3 us -> 0 us
  starting transfers between devices: 6.52 us -> 22.5 us
  between operations: 14.8 us -> 1.53 us
  matrix products: 9.5 us -> 0 us
  waiting for transfers between devices: 23.1 us -> 14.6 us
  Pallas kernels: 0 us -> 7.65 us
  other arithmetic: 2.56 us -> 0.04 us
  local copies, waits for them, and re-layouts: 3.31 us -> 5.5 us
    psum x1 -> x0, blocking collectives: 79.8 us -> none  [shards(): dens_col = lax.psum(col_partial, 'row').astype(jnp.bfloat16)]
    reduce_scatter x1 -> x0, waiting for transfers between devices: 23.1 us -> none  [shards(): lax.psum_scatter((jnp.dot(block, trial, preferred_element_type=jnp.float3...]
    ppermute x0 -> x16, starting transfers between devices: none -> 22.5 us  [swap(): lax.ppermute(x, axis, [(i, i ^ step) for i in range(lax.axis_size(axis))])]
    ppermute x0 -> x16, waiting for transfers between devices: none -> 14.6 us  [swap(): lax.ppermute(x, axis, [(i, i ^ step) for i in range(lax.axis_size(axis))])]
    dot_general x4 -> x0, matrix products: 9.5 us -> none  [the longest x1 4.29 us: shards(): jnp.dot(pair_products(row_all[0], 0), plane_wave, preferred_element_type=...]
    all_gather x1 -> x0, blocking collectives: 8.46 us -> none  [shards(): row_all = lax.all_gather(window_bands, 'col', axis=2, tiled=True)]
    pallas_call x0 -> x7, Pallas kernels: none -> 7.65 us  [call(): pl.pallas_call(kernel, out_shape=outs, in_specs=spaces, out_specs=jax.tre...]
    all_to_all x1 -> x0, starting transfers between devices: 6.49 us -> none  [shards(): lax.all_to_all(chosen, 'row', split_axis=0, concat_axis=1, tiled=True)]
  transfers between devices with their start and end apart: 2 -> 16, of which waited for: 1 -> 7; matrix products, arithmetic and copies ran while one was open for 4% -> 0% of each run, Pallas kernels for 0% -> 8%
where the time goes in v2:
time: 52.1 us; the launch traced here: 51.8 us
  starting transfers between devices  22.5 us (43%)
  waiting for transfers between devices  14.6 us (28%)
  Pallas kernels  7.65 us (15%)
  local copies, waits for them, and re-layouts  5.5 us (11%)
  between operations  1.53 us (3%)
    ppermute x16, starting transfers between devices, swap(): lax.ppermute(x, axis, [(i, i ^ step) for i in range(lax.axis_size(axis))])  22.5 us
    ppermute x16, waiting for transfers between devices, swap(): lax.ppermute(x, axis, [(i, i ^ step) for i in range(lax.axis_size(axis))])  14.6 us
    pallas_call x7, Pallas kernels, call(): pl.pallas_call(kernel, out_shape=outs, in_specs=spaces, out_specs=jax.tre...  7.65 us
    unnamed x15, local copies, waits for them, and re-layouts  4.67 us
  transfers between devices with their start and end apart: 16, of which 7 were waited for; matrix products, arithmetic and copies ran while one was open for 0% of the time, Pallas kernels for 8%

profile of v2, /device:TPU:0, one launch (start us, length us, event | category | flops | bytes accessed | tf_op | source)
XLA Modules:
  0.0 51.8 jit_solution(4835633014007797663)
XLA Ops:
  0.0 0.0 copy-start
  0.7 0.7 %constant_dynamic-slice_fusion.1.bands_ref = bf16[1,32,256]{2,1,0:T(8,128)(2,1)S(1)} fusion(bf16[1,64,256]{2,1,0:T(8,128)(2,1)} %param.10, s32[]{:T(128)S(6)} %select_n.6), kind=kLoop, calls=%fused_computation.10 | loop fusion | bytes 32772 | tf_op jit(solution)/shard_map/dynamic_slice | solution.py:136
  1.4 3.1 %collective-permute-start = (bf16[1,32,256]{2,1,0:T(8,128)(2,1)S(1)}, bf16[1,32,256]{2,1,0:T(8,128)(2,1)S(1)}, u32[]{:S(2)}, u32[]{:S(2)}) collective-permute-start(bf16[1,32,256]{2,1,0:T(8,128)(2,1)S(1)} %constant_dynamic-slice_fusion.1.bands_ref), channel_id=1, source_target_pairs={{0,8},{4,12},{8,0},{12,4},{16,24},{20,28},{24,16},{28,20},{1,9},{5... | collective-permute-start | bytes 49160 | tf_op jit(solution)/shard_map/ppermute | solution.py:32
  4.5 1.7 %collective-permute-done = bf16[1,32,256]{2,1,0:T(8,128)(2,1)S(1)} collective-permute-done((bf16[1,32,256]{2,1,0:T(8,128)(2,1)S(1)}, bf16[1,32,256]{2,1,0:T(8,128)(2,1)S(1)}, u32[]{:S(2)}, u32[]{:S(2)}) %collective-permute-start) | collective-permute-done | bytes 16416 | tf_op jit(solution)/shard_map/ppermute | solution.py:32
  6.2 3.0 %collective-permute-start.1 = (bf16[2,32,256]{2,1,0:T(8,128)(2,1)S(1)}, bf16[2,32,256]{2,1,0:T(8,128)(2,1)S(1)}, u32[]{:S(2)}, u32[]{:S(2)}) collective-permute-start(bf16[2,32,256]{2,1,0:T(8,128)(2,1)S(1)} %pad_maximum_fusion.2), channel_id=1, source_target_pairs={{0,16},{4,20},{8,24},{12,28},{16,0},{20,4},{24,8},{28,12},{1,17},{... | collective-permute-start | bytes 98312 | tf_op jit(solution)/shard_map/ppermute | solution.py:32
  9.2 1.9 %collective-permute-done.1 = bf16[2,32,256]{2,1,0:T(8,128)(2,1)S(1)} collective-permute-done((bf16[2,32,256]{2,1,0:T(8,128)(2,1)S(1)}, bf16[2,32,256]{2,1,0:T(8,128)(2,1)S(1)}, u32[]{:S(2)}, u32[]{:S(2)}) %collective-permute-start.1) | collective-permute-done | bytes 32800 | tf_op jit(solution)/shard_map/ppermute | solution.py:32
  11.1 0.1 collective-permute-start.2
  11.2 0.0 copy-start.1
  11.3 2.2 %copy-done.1 = bf16[2048,1024]{1,0:T(8,128)(2,1)S(1)} copy-done((bf16[2048,1024]{1,0:T(8,128)(2,1)S(1)}, bf16[2048,1024]{1,0:T(8,128)(2,1)}, u32[]{:S(2)}) %copy-start.1) | copy-done | bytes 4194328
  13.4 0.8 %shard_map.91.refs_0_ = f32[256,1024]{1,0:T(8,128)S(1)} custom-call(s32[4]{0:T(128)S(1)} %get-tuple-element.25.place_ref, bf16[1,32,256]{2,1,0:T(8,128)(2,1)S(1)} %constant_dynamic-slice_fusion.1.bands_ref, bf16[2048,1024]{1,0:T(8,128)(2,1)S(1)} %copy-done.1), custom_call_target="tpu_custom_call" | custom-call | flops 134217728 | bytes 524288 | tf_op jit(solution)/shard_map/pallas_call | solution.py:20
  14.3 1.1 %shard_map.92.refs_0_ = f32[256,1024]{1,0:T(8,128)S(1)} custom-call(s32[4]{0:T(128)S(1)} %get-tuple-element.25.place_ref, bf16[4,32,256]{2,1,0:T(8,128)(2,1)S(1)} %pad_maximum_fusion.1.bands_ref, bf16[2048,1024]{1,0:T(8,128)(2,1)S(1)} %copy-done.1, f32[256,1024]{1,0:T(8,128)S(1)} %shard_map.91.refs_0_), custom_call_target="tpu_custom_call" | custom-call | flops 402653184 | bytes 1572864 | tf_op jit(solution)/shard_map/pallas_call | solution.py:20
  15.4 0.0 copy-start.3
  15.4 0.0 copy-start.5
  15.4 0.0 copy-start.6
  15.5 0.0 collective-permute-done.2.bands_ref
  15.5 0.0 copy-start.4
  15.5 1.3 %shard_map.93.dens_ref = bf16[256,1024]{1,0:T(8,128)(2,1)S(1)} custom-call(s32[4]{0:T(128)S(1)} %get-tuple-element.26.place_ref, bf16[4,32,256]{2,1,0:T(8,128)(2,1)S(1)} %collective-permute-done.2.bands_ref, bf16[2048,1024]{1,0:T(8,128)(2,1)S(1)} %copy-done.1, f32[256,1024]{1,0:T(8,128)S(1)} %shard_map.92.refs_0_), custom_call_target="tpu_custom_call" | custom-call | flops 536870912 | bytes 2097152 | tf_op jit(solution)/shard_map/pallas_call | solution.py:20
  16.7 0.3 copy-done.3
  17.0 0.0 copy-done.5
  17.0 0.0 copy-done.6
  17.0 1.3 %shard_map.94 = (bf16[4,128,256]{2,1,0:T(8,128)(2,1)S(1)}, bf16[4,128,256]{2,1,0:T(8,128)(2,1)S(1)}) custom-call(s32[1]{0:T(128)} %bitcast.me_ref.me_row_ref, s32[8]{0:T(128)S(1)} %copy-done.5, s32[8]{0:T(128)S(1)} %bitcast.24, bf16[8,128,1024]{2,1,0:T(8,128)(2,1)S(1)} %copy-done.3, bf16[256,1024]{1,0:T(8,128)(2,1)S(1)} %shard_map.93.dens_ref), custom_call_target="tpu_custom_call" | custom-call | flops 536870912 | bytes 2097152 | tf_op jit(solution)/shard_map/pallas_call | solution.py:20
  18.3 0.6 %collective-permute-start.3 = (bf16[4,128,256]{2,1,0:T(8,128)(2,1)S(1)}, bf16[4,128,256]{2,1,0:T(8,128)(2,1)S(1)}, u32[]{:S(2)}, u32[]{:S(2)}) collective-permute-start(bf16[4,128,256]{2,1,0:T(8,128)(2,1)S(1)} %get-tuple-element.14), channel_id=1, source_target_pairs={{0,4},{4,0},{8,12},{12,8},{16,20},{20,16},{24,28},{28,24},{1,5},{5... | collective-permute-start | bytes 786440 | tf_op jit(solution)/shard_map/ppermute | solution.py:32
  19.6 0.5 collective-permute-done.3
  20.1 2.0 %collective-permute-start.7 = (bf16[256,256]{1,0:T(8,128)(2,1)S(1)}, bf16[256,256]{1,0:T(8,128)(2,1)S(1)}, u32[]{:S(2)}, u32[]{:S(2)}) collective-permute-start(bf16[256,256]{1,0:T(8,128)(2,1)S(1)} %get-tuple-element.23), channel_id=1, source_target_pairs={{0,8},{4,12},{8,0},{12,4},{16,24},{20,28},{24,16},{28,20},{1,9},{5... | collective-permute-start | bytes 393224 | tf_op jit(solution)/shard_map/ppermute | solution.py:32
  22.1 0.0 copy-done
  22.1 1.5 %collective-permute-start.4 = (bf16[32,512]{1,0:T(8,128)(2,1)S(1)}, bf16[32,512]{1,0:T(8,128)(2,1)S(1)}, u32[]{:S(2)}, u32[]{:S(2)}) collective-permute-start(bf16[32,512]{1,0:T(8,128)(2,1)S(1)} %fusion), channel_id=1, source_target_pairs={{0,1},{1,0},{2,3},{3,2},{4,5},{5,4},{6,7},{7,6},{8,9},{9,8},{10,11... | collective-permute-start | bytes 98312 | tf_op jit(solution)/shard_map/ppermute | solution.py:32
  23.7 1.5 %collective-permute-start.5 = (bf16[32,512]{1,0:T(8,128)(2,1)S(1)}, bf16[32,512]{1,0:T(8,128)(2,1)S(1)}, u32[]{:S(2)}, u32[]{:S(2)}) collective-permute-start(bf16[32,512]{1,0:T(8,128)(2,1)S(1)} %fusion), channel_id=1, source_target_pairs={{0,2},{1,3},{2,0},{3,1},{4,6},{5,7},{6,4},{7,5},{8,10},{9,11},{10,... | collective-permute-start | bytes 98312 | tf_op jit(solution)/shard_map/ppermute | solution.py:32
  25.2 0.5 collective-permute-start.6
  25.7 0.0 copy-done.4
  25.7 1.5 %collective-permute-start.13 = (bf16[256,512]{1,0:T(8,128)(2,1)S(1)}, bf16[256,512]{1,0:T(8,128)(2,1)S(1)}, u32[]{:S(2)}, u32[]{:S(2)}) collective-permute-start(bf16[256,512]{1,0:T(8,128)(2,1)S(1)} %copy-done.4), channel_id=1, source_target_pairs={{0,1},{1,0},{2,3},{3,2},{4,5},{5,4},{6,7},{7,6},{8,9},{9,8},{10,11... | collective-permute-start | bytes 786440 | tf_op jit(solution)/shard_map/ppermute | solution.py:32
  27.2 0.0 collective-permute-done.4
  27.2 1.5 %collective-permute-start.14 = (bf16[256,512]{1,0:T(8,128)(2,1)S(1)}, bf16[256,512]{1,0:T(8,128)(2,1)S(1)}, u32[]{:S(2)}, u32[]{:S(2)}) collective-permute-start(bf16[256,512]{1,0:T(8,128)(2,1)S(1)} %copy-done.4), channel_id=1, source_target_pairs={{0,2},{1,3},{2,0},{3,1},{4,6},{5,7},{6,4},{7,5},{8,10},{9,11},{10,... | collective-permute-start | bytes 786440 | tf_op jit(solution)/shard_map/ppermute | solution.py:32
  28.8 0.0 collective-permute-done.5
  28.8 0.6 %collective-permute-start.15 = (bf16[256,512]{1,0:T(8,128)(2,1)S(1)}, bf16[256,512]{1,0:T(8,128)(2,1)S(1)}, u32[]{:S(2)}, u32[]{:S(2)}) collective-permute-start(bf16[256,512]{1,0:T(8,128)(2,1)S(1)} %copy-done.4), channel_id=1, source_target_pairs={{0,3},{1,2},{2,1},{3,0},{4,7},{5,6},{6,5},{7,4},{8,11},{9,10},{10,... | collective-permute-start | bytes 786440 | tf_op jit(solution)/shard_map/ppermute | solution.py:32
  29.4 0.9 %collective-permute-done.6 = bf16[32,512]{1,0:T(8,128)(2,1)S(1)} collective-permute-done((bf16[32,512]{1,0:T(8,128)(2,1)S(1)}, bf16[32,512]{1,0:T(8,128)(2,1)S(1)}, u32[]{:S(2)}, u32[]{:S(2)}) %collective-permute-start.6) | collective-permute-done | bytes 32800 | tf_op jit(solution)/shard_map/ppermute | solution.py:32
  30.4 2.8 %collective-permute-start.8 = (bf16[256,256]{1,0:T(8,128)(2,1)S(1)}, bf16[256,256]{1,0:T(8,128)(2,1)S(1)}, u32[]{:S(2)}, u32[]{:S(2)}) collective-permute-start(bf16[256,256]{1,0:T(8,128)(2,1)S(1)} %get-tuple-element.22), channel_id=1, source_target_pairs={{0,16},{4,20},{8,24},{12,28},{16,0},{20,4},{24,8},{28,12},{1,17},{... | collective-permute-start | bytes 393224 | tf_op jit(solution)/shard_map/ppermute | solution.py:32
  33.2 0.0 collective-permute-done.7.refs_1_
  33.2 0.0 collective-permute-start.9
  33.2 0.0 copy-start.2
  33.2 2.2 %copy-done.2 = bf16[2048,1024]{1,0:T(8,128)(2,1)S(1)} copy-done((bf16[2048,1024]{1,0:T(8,128)(2,1)S(1)}, bf16[2048,1024]{1,0:T(8,128)(2,1)}, u32[]{:S(2)}) %copy-start.2) | copy-done | bytes 4194328
  35.4 1.8 %shard_map.95.dens_ref = bf16[256,1024]{1,0:T(8,128)(2,1)S(1)} custom-call(s32[4]{0:T(128)S(1)} %iota_xor_fusion.place_ref, bf16[4,32,512]{2,1,0:T(8,128)(2,1)S(1)} %pad_maximum_fusion.bands_ref, bf16[2048,1024]{1,0:T(8,128)(2,1)S(1)} %copy-done.2), custom_call_target="tpu_custom_call" | custom-call | flops 1073741824 | bytes 4194304 | tf_op jit(solution)/shard_map/pallas_call | solution.py:20
  37.2 4.4 %collective-permute-done.8.refs_2_ = bf16[256,256]{1,0:T(8,128)(2,1)S(1)} collective-permute-done((bf16[256,256]{1,0:T(8,128)(2,1)S(1)}, bf16[256,256]{1,0:T(8,128)(2,1)S(1)}, u32[]{:S(2)}, u32[]{:S(2)}) %collective-permute-start.8) | collective-permute-done | bytes 131104 | tf_op jit(solution)/shard_map/ppermute | solution.py:32
  41.6 0.0 collective-permute-done.9.refs_3_
  41.6 0.3 shard_map.96
  42.0 0.8 %collective-permute-start.10 = (bf16[64,256]{1,0:T(8,128)(2,1)S(1)}, bf16[64,256]{1,0:T(8,128)(2,1)S(1)}, u32[]{:S(2)}, u32[]{:S(2)}) collective-permute-start(bf16[64,256]{1,0:T(8,128)(2,1)S(1)} %get-tuple-element.17), channel_id=1, source_target_pairs={{0,1},{1,0},{2,3},{3,2},{4,5},{5,4},{6,7},{7,6},{8,9},{9,8},{10,11... | collective-permute-start | bytes 98312 | tf_op jit(solution)/shard_map/ppermute | solution.py:32
  42.8 1.4 %collective-permute-start.11 = (bf16[64,256]{1,0:T(8,128)(2,1)S(1)}, bf16[64,256]{1,0:T(8,128)(2,1)S(1)}, u32[]{:S(2)}, u32[]{:S(2)}) collective-permute-start(bf16[64,256]{1,0:T(8,128)(2,1)S(1)} %get-tuple-element.18), channel_id=1, source_target_pairs={{0,2},{1,3},{2,0},{3,1},{4,6},{5,7},{6,4},{7,5},{8,10},{9,11},{10,... | collective-permute-start | bytes 98312 | tf_op jit(solution)/shard_map/ppermute | solution.py:32
  44.2 1.8 %collective-permute-done.10.refs_1_ = bf16[64,256]{1,0:T(8,128)(2,1)S(1)} collective-permute-done((bf16[64,256]{1,0:T(8,128)(2,1)S(1)}, bf16[64,256]{1,0:T(8,128)(2,1)S(1)}, u32[]{:S(2)}, u32[]{:S(2)}) %collective-permute-start.10) | collective-permute-done | bytes 32800 | tf_op jit(solution)/shard_map/ppermute | solution.py:32
  46.0 1.5 %collective-permute-start.12 = (bf16[64,256]{1,0:T(8,128)(2,1)S(1)}, bf16[64,256]{1,0:T(8,128)(2,1)S(1)}, u32[]{:S(2)}, u32[]{:S(2)}) collective-permute-start(bf16[64,256]{1,0:T(8,128)(2,1)S(1)} %get-tuple-element.19), channel_id=1, source_target_pairs={{0,3},{1,2},{2,1},{3,0},{4,7},{5,6},{6,5},{7,4},{8,11},{9,10},{10,... | collective-permute-start | bytes 98312 | tf_op jit(solution)/shard_map/ppermute | solution.py:32
  47.5 0.0 collective-permute-done.11.refs_2_
  47.5 3.3 %collective-permute-done.12.refs_3_ = bf16[64,256]{1,0:T(8,128)(2,1)S(1)} collective-permute-done((bf16[64,256]{1,0:T(8,128)(2,1)S(1)}, bf16[64,256]{1,0:T(8,128)(2,1)S(1)}, u32[]{:S(2)}, u32[]{:S(2)}) %collective-permute-start.12) | collective-permute-done | bytes 32800 | tf_op jit(solution)/shard_map/ppermute | solution.py:32
  50.8 0.0 collective-permute-done.13.refs_5_
  50.8 0.0 collective-permute-done.14.refs_6_
  50.8 0.0 collective-permute-done.15.refs_7_
  50.8 1.0 %shard_map.97 = f32[64,512]{1,0:T(8,128)} custom-call(bf16[64,256]{1,0:T(8,128)(2,1)S(1)} %get-tuple-element.16.refs_0_, bf16[64,256]{1,0:T(8,128)(2,1)S(1)} %collective-permute-done.10.refs_1_, bf16[64,256]{1,0:T(8,128)(2,1)S(1)} %collective-permute-done.11.refs_2_, bf16[64,256]{1,0:T(8,128)(2,1)S(1)} %collective-permute-done.12.refs_3_, ...), custom_call_target="tpu_custom_call" | custom-call | flops 67108864 | bytes 1048576 | tf_op jit(solution)/shard_map/pallas_call | solution.py:20
  (10 shorter events, 0.1 us)
Async XLA Ops:
  0.0 22.1 %copy-start = (bf16[1,64,512]{2,1,0:T(8,128)(2,1)S(1)}, bf16[1,64,512]{2,1,0:T(8,128)(2,1)}, u32[]{:S(2)}) copy-start(bf16[1,64,512]{2,1,0:T(8,128)(2,1)} %param.9) | copy-start | bytes 196612
  1.4 4.8 %collective-permute-start = (bf16[1,32,256]{2,1,0:T(8,128)(2,1)S(1)}, bf16[1,32,256]{2,1,0:T(8,128)(2,1)S(1)}, u32[]{:S(2)}, u32[]{:S(2)}) collective-permute-start(bf16[1,32,256]{2,1,0:T(8,128)(2,1)S(1)} %constant_dynamic-slice_fusion.1.bands_ref), channel_id=1, source_target_pairs={{0,8},{4,12},{8,0},{12,4},{16,24},{20,28},{24,16},{28,20},{1,9},{5... | collective-permute-start | bytes 49160 | tf_op jit(solution)/shard_map/ppermute | solution.py:32
  6.2 4.9 %collective-permute-start.1 = (bf16[2,32,256]{2,1,0:T(8,128)(2,1)S(1)}, bf16[2,32,256]{2,1,0:T(8,128)(2,1)S(1)}, u32[]{:S(2)}, u32[]{:S(2)}) collective-permute-start(bf16[2,32,256]{2,1,0:T(8,128)(2,1)S(1)} %pad_maximum_fusion.2), channel_id=1, source_target_pairs={{0,16},{4,20},{8,24},{12,28},{16,0},{20,4},{24,8},{28,12},{1,17},{... | collective-permute-start | bytes 98312 | tf_op jit(solution)/shard_map/ppermute | solution.py:32
  11.1 4.3 %collective-permute-start.2 = (bf16[4,32,256]{2,1,0:T(8,128)(2,1)S(1)}, bf16[4,32,256]{2,1,0:T(8,128)(2,1)S(1)}, u32[]{:S(2)}, u32[]{:S(2)}) collective-permute-start(bf16[4,32,256]{2,1,0:T(8,128)(2,1)S(1)} %pad_maximum_fusion.1.bands_ref), channel_id=1, source_target_pairs={{0,4},{4,0},{8,12},{12,8},{16,20},{20,16},{24,28},{28,24},{1,5},{5... | collective-permute-start | bytes 196616 | tf_op jit(solution)/shard_map/ppermute | solution.py:32
  11.2 2.2 %copy-start.1 = (bf16[2048,1024]{1,0:T(8,128)(2,1)S(1)}, bf16[2048,1024]{1,0:T(8,128)(2,1)}, u32[]{:S(2)}) copy-start(bf16[2048,1024]{1,0:T(8,128)(2,1)} %table_ref.7) | copy-start | bytes 12582916
  15.4 1.6 %copy-start.3 = (bf16[8,128,1024]{2,1,0:T(8,128)(2,1)S(1)}, bf16[8,128,1024]{2,1,0:T(8,128)(2,1)}, u32[]{:S(2)}) copy-start(bf16[8,128,1024]{2,1,0:T(8,128)(2,1)} %screened_ref.1) | copy-start | bytes 6291460
  15.4 1.6 %copy-start.5 = (s32[8]{0:T(128)S(1)}, s32[8]{0:T(128)}, u32[]{:S(2)}) copy-start(s32[8]{0:T(128)} %owner_ref.1) | copy-start | bytes 100
  15.4 1.6 %copy-start.6 = (s32[8,1]{0,1:T(1,128)S(1)}, s32[8,1]{0,1:T(1,128)}, u32[]{:S(2)}) copy-start(s32[8,1]{0,1:T(1,128)} %param.16) | copy-start | bytes 100
  15.5 10.2 %copy-start.4 = (bf16[256,512]{1,0:T(8,128)(2,1)S(1)}, bf16[256,512]{1,0:T(8,128)(2,1)}, u32[]{:S(2)}) copy-start(bf16[256,512]{1,0:T(8,128)(2,1)} %refs_4_) | copy-start | bytes 786436
  18.3 1.7 %collective-permute-start.3 = (bf16[4,128,256]{2,1,0:T(8,128)(2,1)S(1)}, bf16[4,128,256]{2,1,0:T(8,128)(2,1)S(1)}, u32[]{:S(2)}, u32[]{:S(2)}) collective-permute-start(bf16[4,128,256]{2,1,0:T(8,128)(2,1)S(1)} %get-tuple-element.14), channel_id=1, source_target_pairs={{0,4},{4,0},{8,12},{12,8},{16,20},{20,16},{24,28},{28,24},{1,5},{5... | collective-permute-start | bytes 786440 | tf_op jit(solution)/shard_map/ppermute | solution.py:32
  20.1 13.1 %collective-permute-start.7 = (bf16[256,256]{1,0:T(8,128)(2,1)S(1)}, bf16[256,256]{1,0:T(8,128)(2,1)S(1)}, u32[]{:S(2)}, u32[]{:S(2)}) collective-permute-start(bf16[256,256]{1,0:T(8,128)(2,1)S(1)} %get-tuple-element.23), channel_id=1, source_target_pairs={{0,8},{4,12},{8,0},{12,4},{16,24},{20,28},{24,16},{28,20},{1,9},{5... | collective-permute-start | bytes 393224 | tf_op jit(solution)/shard_map/ppermute | solution.py:32
  22.1 5.1 %collective-permute-start.4 = (bf16[32,512]{1,0:T(8,128)(2,1)S(1)}, bf16[32,512]{1,0:T(8,128)(2,1)S(1)}, u32[]{:S(2)}, u32[]{:S(2)}) collective-permute-start(bf16[32,512]{1,0:T(8,128)(2,1)S(1)} %fusion), channel_id=1, source_target_pairs={{0,1},{1,0},{2,3},{3,2},{4,5},{5,4},{6,7},{7,6},{8,9},{9,8},{10,11... | collective-permute-start | bytes 98312 | tf_op jit(solution)/shard_map/ppermute | solution.py:32
  23.7 5.1 %collective-permute-start.5 = (bf16[32,512]{1,0:T(8,128)(2,1)S(1)}, bf16[32,512]{1,0:T(8,128)(2,1)S(1)}, u32[]{:S(2)}, u32[]{:S(2)}) collective-permute-start(bf16[32,512]{1,0:T(8,128)(2,1)S(1)} %fusion), channel_id=1, source_target_pairs={{0,2},{1,3},{2,0},{3,1},{4,6},{5,7},{6,4},{7,5},{8,10},{9,11},{10,... | collective-permute-start | bytes 98312 | tf_op jit(solution)/shard_map/ppermute | solution.py:32
  25.2 5.2 %collective-permute-start.6 = (bf16[32,512]{1,0:T(8,128)(2,1)S(1)}, bf16[32,512]{1,0:T(8,128)(2,1)S(1)}, u32[]{:S(2)}, u32[]{:S(2)}) collective-permute-start(bf16[32,512]{1,0:T(8,128)(2,1)S(1)} %fusion), channel_id=1, source_target_pairs={{0,3},{1,2},{2,1},{3,0},{4,7},{5,6},{6,5},{7,4},{8,11},{9,10},{10,... | collective-permute-start | bytes 98312 | tf_op jit(solution)/shard_map/ppermute | solution.py:32
  25.7 25.1 %collective-permute-start.13 = (bf16[256,512]{1,0:T(8,128)(2,1)S(1)}, bf16[256,512]{1,0:T(8,128)(2,1)S(1)}, u32[]{:S(2)}, u32[]{:S(2)}) collective-permute-start(bf16[256,512]{1,0:T(8,128)(2,1)S(1)} %copy-done.4), channel_id=1, source_target_pairs={{0,1},{1,0},{2,3},{3,2},{4,5},{5,4},{6,7},{7,6},{8,9},{9,8},{10,11... | collective-permute-start | bytes 786440 | tf_op jit(solution)/shard_map/ppermute | solution.py:32
  27.2 23.6 %collective-permute-start.14 = (bf16[256,512]{1,0:T(8,128)(2,1)S(1)}, bf16[256,512]{1,0:T(8,128)(2,1)S(1)}, u32[]{:S(2)}, u32[]{:S(2)}) collective-permute-start(bf16[256,512]{1,0:T(8,128)(2,1)S(1)} %copy-done.4), channel_id=1, source_target_pairs={{0,2},{1,3},{2,0},{3,1},{4,6},{5,7},{6,4},{7,5},{8,10},{9,11},{10,... | collective-permute-start | bytes 786440 | tf_op jit(solution)/shard_map/ppermute | solution.py:32
  28.8 22.0 %collective-permute-start.15 = (bf16[256,512]{1,0:T(8,128)(2,1)S(1)}, bf16[256,512]{1,0:T(8,128)(2,1)S(1)}, u32[]{:S(2)}, u32[]{:S(2)}) collective-permute-start(bf16[256,512]{1,0:T(8,128)(2,1)S(1)} %copy-done.4), channel_id=1, source_target_pairs={{0,3},{1,2},{2,1},{3,0},{4,7},{5,6},{6,5},{7,4},{8,11},{9,10},{10,... | collective-permute-start | bytes 786440 | tf_op jit(solution)/shard_map/ppermute | solution.py:32
  30.4 11.3 %collective-permute-start.8 = (bf16[256,256]{1,0:T(8,128)(2,1)S(1)}, bf16[256,256]{1,0:T(8,128)(2,1)S(1)}, u32[]{:S(2)}, u32[]{:S(2)}) collective-permute-start(bf16[256,256]{1,0:T(8,128)(2,1)S(1)} %get-tuple-element.22), channel_id=1, source_target_pairs={{0,16},{4,20},{8,24},{12,28},{16,0},{20,4},{24,8},{28,12},{1,17},{... | collective-permute-start | bytes 393224 | tf_op jit(solution)/shard_map/ppermute | solution.py:32
  33.2 8.5 %collective-permute-start.9 = (bf16[256,256]{1,0:T(8,128)(2,1)S(1)}, bf16[256,256]{1,0:T(8,128)(2,1)S(1)}, u32[]{:S(2)}, u32[]{:S(2)}) collective-permute-start(bf16[256,256]{1,0:T(8,128)(2,1)S(1)} %get-tuple-element.21), channel_id=1, source_target_pairs={{0,24},{4,28},{8,16},{12,20},{16,8},{20,12},{24,0},{28,4},{1,25},{... | collective-permute-start | bytes 393224 | tf_op jit(solution)/shard_map/ppermute | solution.py:32
  33.2 2.2 %copy-start.2 = (bf16[2048,1024]{1,0:T(8,128)(2,1)S(1)}, bf16[2048,1024]{1,0:T(8,128)(2,1)}, u32[]{:S(2)}) copy-start(bf16[2048,1024]{1,0:T(8,128)(2,1)} %table_ref.7) | copy-start | bytes 12582916
  42.0 4.0 %collective-permute-start.10 = (bf16[64,256]{1,0:T(8,128)(2,1)S(1)}, bf16[64,256]{1,0:T(8,128)(2,1)S(1)}, u32[]{:S(2)}, u32[]{:S(2)}) collective-permute-start(bf16[64,256]{1,0:T(8,128)(2,1)S(1)} %get-tuple-element.17), channel_id=1, source_target_pairs={{0,1},{1,0},{2,3},{3,2},{4,5},{5,4},{6,7},{7,6},{8,9},{9,8},{10,11... | collective-permute-start | bytes 98312 | tf_op jit(solution)/shard_map/ppermute | solution.py:32
  42.8 4.7 %collective-permute-start.11 = (bf16[64,256]{1,0:T(8,128)(2,1)S(1)}, bf16[64,256]{1,0:T(8,128)(2,1)S(1)}, u32[]{:S(2)}, u32[]{:S(2)}) collective-permute-start(bf16[64,256]{1,0:T(8,128)(2,1)S(1)} %get-tuple-element.18), channel_id=1, source_target_pairs={{0,2},{1,3},{2,0},{3,1},{4,6},{5,7},{6,4},{7,5},{8,10},{9,11},{10,... | collective-permute-start | bytes 98312 | tf_op jit(solution)/shard_map/ppermute | solution.py:32
  46.0 4.8 %collective-permute-start.12 = (bf16[64,256]{1,0:T(8,128)(2,1)S(1)}, bf16[64,256]{1,0:T(8,128)(2,1)S(1)}, u32[]{:S(2)}, u32[]{:S(2)}) collective-permute-start(bf16[64,256]{1,0:T(8,128)(2,1)S(1)} %get-tuple-element.19), channel_id=1, source_target_pairs={{0,3},{1,2},{2,1},{3,0},{4,7},{5,6},{6,5},{7,4},{8,11},{9,10},{10,... | collective-permute-start | bytes 98312 | tf_op jit(solution)/shard_map/ppermute | solution.py:32

commit v3 on v2

v3 whole, which is shorter than its diff:
```python
import functools

import jax
import jax.numpy as jnp
from jax import lax
from jax.experimental import pallas as pl
from jax.experimental.pallas import tpu as pltpu
from jax.sharding import PartitionSpec as P


NVW = 16
NCW = 16
NP = NVW * NCW
GRANT = 16 << 20
VMEM = pl.BlockSpec(memory_space=pltpu.VMEM)
SMEM = pl.BlockSpec(memory_space=pltpu.SMEM)


def call(kernel, outs, *args, spaces, scratch=(), flops=0, moved=0):
    return pl.pallas_call(
        kernel,
        out_shape=outs,
        in_specs=spaces,
        out_specs=jax.tree.map(lambda _: VMEM, outs),
        scratch_shapes=list(scratch),
        cost_estimate=pl.CostEstimate(flops=flops, bytes_accessed=moved, transcendentals=0),
        compiler_params=pltpu.CompilerParams(vmem_limit_bytes=GRANT),
    )(*args)


def swap(x, axis, step):
    return lax.ppermute(x, axis, [(i, i ^ step) for i in range(lax.axis_size(axis))])


def products_of(bands):
    bands = bands.astype(jnp.float32)
    products = bands[:NVW][:, None, :] * bands[NVW:][None, :, :]
    return products.reshape(NP, bands.shape[1]).astype(jnp.bfloat16)


def products_kernel(bands_ref, out_ref):
    out_ref[...] = products_of(bands_ref[0])


def products(bands):
    return call(
        products_kernel,
        jax.ShapeDtypeStruct((NP, bands.shape[2]), jnp.bfloat16),
        bands,
        spaces=[VMEM],
        flops=1 << 32,
        moved=NP * bands.shape[2],
    )


def density_kernel(todo, given, place_ref, bands_ref, table_ref, *refs):
    refs, out_ref, prod_ref = list(refs[:-2]), refs[-2], refs[-1]
    ready_ref = refs.pop(0) if given else None
    addend_ref = refs.pop(0) if refs else None
    _, _, points = bands_ref.shape
    for s in todo:
        if s or not given:
            prod_ref[s] = products_of(bands_ref[s])
    waves = table_ref.shape[1]
    tile = min(256, waves)
    for n in range(0, waves, tile):
        total = None if addend_ref is None else addend_ref[:, n : n + tile]
        for s in todo:
            at = pl.multiple_of(place_ref[s] * points, points)
            term = jnp.dot(
                prod_ref[s] if s or not given else ready_ref[...],
                table_ref[pl.ds(at, points), n : n + tile],
                preferred_element_type=jnp.float32,
            )
            total = term if total is None else total + term
        out_ref[:, n : n + tile] = total.astype(out_ref.dtype)


def density(places, bands, table, ready=None, addend=None, final=True, todo=None):
    waves = table.shape[1]
    count, _, points = bands.shape
    todo = range(count) if todo is None else todo
    more = [x for x in (ready, addend) if x is not None]
    return call(
        functools.partial(density_kernel, todo, ready is not None),
        jax.ShapeDtypeStruct((NP, waves), jnp.bfloat16 if final else jnp.float32),
        places,
        bands,
        table,
        *more,
        spaces=[SMEM, VMEM, VMEM] + [VMEM] * len(more),
        scratch=[pltpu.VMEM((count, NP, points), jnp.bfloat16)],
        flops=2 * NP * len(todo) * points * waves,
        moved=2 * len(todo) * points * waves,
    )


def weighted_kernel(flip, me_ref, owner_ref, transfer_ref, screened_ref, dens_ref, out_ref, rows_ref):
    chips, share, waves = rows_ref.shape
    me = me_ref[0] ^ flip
    for s in range(chips):
        rows_ref[s] = screened_ref[owner_ref[transfer_ref[me ^ (2 * s)]]]
    out_ref[...] = (
        lax.dot_general(
            rows_ref[...].reshape(chips * share, waves),
            dens_ref[...],
            (((1,), (1,)), ((), ())),
            preferred_element_type=jnp.float32,
        )
        .astype(jnp.bfloat16)
        .reshape(chips, share, NP)
    )


def partial_kernel(scale, me_row_ref, me_col_ref, dens_ref, trial_ref, *refs):
    count = dens_ref.shape[1] // refs[0].shape[0]
    pieces, outs, (weighted_ref, part_ref) = refs[:count], refs[count:-2], refs[-2:]
    me = me_row_ref[0]
    for s, piece in enumerate(pieces):
        share = piece.shape[0] // 2
        first = me ^ (2 * s)
        weighted_ref[pl.ds(pl.multiple_of(first * share, share), share), :] = piece[:share]
        second = first ^ 1
        weighted_ref[pl.ds(pl.multiple_of(second * share, share), share), :] = piece[share:]
    block = jnp.dot(dens_ref[...], weighted_ref[...], preferred_element_type=jnp.float32)
    block = (block * dens_ref.shape[1] ** (-0.5)).astype(jnp.bfloat16)
    part_ref[...] = jnp.dot(block, trial_ref[...], preferred_element_type=jnp.float32) * scale
    rows = outs[0].shape[0]
    for s, out in enumerate(outs):
        at = pl.multiple_of((me_col_ref[0] ^ s) * rows, rows)
        out[...] = part_ref[pl.ds(at, rows), :].astype(out.dtype)


def shards(
    waves_row,
    waves_col,
    window_row,
    window_col,
    plane_wave,
    screened,
    owner_slot,
    transfer_table,
    trial,
):
    rows, cols = lax.axis_size("row"), lax.axis_size("col")
    chips = rows // 2
    me_row, me_col = lax.axis_index("row"), lax.axis_index("col")
    waves, share = plane_wave.shape[1], screened.shape[1]
    steps = jnp.arange(chips, dtype=jnp.int32)

    def window(array, start):
        return lax.dynamic_slice_in_dim(array, start[0], NVW + NCW, 1)

    near = me_row ^ (2 * steps)
    bands = window(waves_col, window_col)
    own = products(bands)
    if rows > 2:
        bands = jnp.concatenate([bands, window(swap(waves_col, "row", 2), window_col)])
    half, step = None, 4
    while step < rows:
        done = step // 4 if step > 4 else 0
        more = {} if half is None else {"addend": half}
        half = density(
            near,
            bands,
            plane_wave,
            final=False,
            todo=range(done, step // 2),
            ready=own if half is None else None,
            **more,
        )
        bands = jnp.concatenate([bands, swap(bands, "row", step)])
        step *= 2
    other = swap(bands, "row", 1)
    half = density(
        near,
        bands,
        plane_wave,
        final=False,
        todo=range(chips // 2 if half is not None else 0, chips),
        addend=half,
        ready=own if half is None else None,
    )
    dens_col = density(near ^ 1, other, plane_wave, addend=half)

    def weighted(flip):
        return call(
            functools.partial(weighted_kernel, flip),
            jax.ShapeDtypeStruct((chips, share, NP), jnp.bfloat16),
            me_row[None],
            owner_slot,
            transfer_table[:, 0],
            screened,
            dens_col,
            spaces=[SMEM, SMEM, SMEM, VMEM, VMEM],
            scratch=[pltpu.VMEM((chips, share, waves), jnp.bfloat16)],
            flops=2 * chips * share * waves * NP,
            moved=2 * chips * share * waves,
        )

    give, keep = weighted(1), weighted(0)
    both = jnp.concatenate([keep, swap(give, "row", 1)], axis=1)
    pieces = [both[0]] + [None] * (chips - 1)
    for s in [*range(2, chips), 1]:
        pieces[s] = swap(both[s], "row", 2 * s)

    late_waves, _ = lax.optimization_barrier((waves_row, both))
    bands_row = window(late_waves, window_row)
    own_row = products(bands_row)
    row_bands = jnp.concatenate([bands_row] + [swap(bands_row, "col", s) for s in range(1, cols)])
    places = me_col ^ jnp.arange(cols, dtype=jnp.int32)
    dens_row = density(places, row_bands, plane_wave, own_row)

    vectors = trial.shape[1]
    kinds = [jnp.float32] + [jnp.bfloat16] * (cols - 1)
    parts = call(
        functools.partial(partial_kernel, (cols * NP) ** (-0.5)),
        [jax.ShapeDtypeStruct((NP // cols, vectors), kind) for kind in kinds],
        me_row[None],
        me_col[None],
        dens_row,
        trial,
        *pieces,
        spaces=[SMEM, SMEM] + [VMEM] * (2 + chips),
        scratch=[pltpu.VMEM((waves, NP), jnp.bfloat16), pltpu.VMEM((NP, vectors), jnp.float32)],
        flops=2 * NP * NP * (waves + vectors),
        moved=2 * waves * NP,
    )
    total = parts[0]
    for s in range(1, cols):
        total += swap(parts[s], "col", s).astype(jnp.float32)
    return total


def solution(mesh):
    return jax.shard_map(
        shards,
        mesh=mesh,
        in_specs=(
            P("row", None, "col"),
            P("col", None, "row"),
            P("row"),
            P("col"),
            P(),
            P(None, "row", None),
            P(),
            P(None, "col"),
            P("col", None),
        ),
        out_specs=P(("row", "col"), None),
        check_vma=False,
    )
```

time: 52.1 us -> 48.1 us (0.923)
  starting transfers between devices: 22.5 us -> 18.7 us
  local copies, waits for them, and re-layouts: 5.5 us -> 3.4 us
  other arithmetic: 0.04 us -> 1.55 us
    ppermute x16 -> x13, starting transfers between devices: 22.5 us -> 18.7 us  [swap(): lax.ppermute(x, axis, [(i, i ^ step) for i in range(lax.axis_size(axis))])]
    unnamed x15 -> x14, local copies, waits for them, and re-layouts: 4.67 us -> 2.63 us
    concatenate x0 -> x2, other arithmetic: none -> 0.8 us  [the longest x1 0.79 us: shards(): jnp.concatenate([bands_row] + [swap(bands_row, 'col', s) for s in range(1...]
    add x0 -> x1, other arithmetic: none -> 0.69 us  [shards(): total += swap(parts[s], 'col', s).astype(jnp.float32)]
    ppermute x16 -> x13, waiting for transfers between devices: 14.6 us -> 14.8 us  [swap(): lax.ppermute(x, axis, [(i, i ^ step) for i in range(lax.axis_size(axis))])]
    pallas_call x7 -> x9, Pallas kernels: 7.65 us -> 7.77 us  [call(): pl.pallas_call(kernel, out_shape=outs, in_specs=spaces, out_specs=jax.tre...]
  transfers between devices with their start and end apart: 16 -> 13, of which waited for: 7 -> 8; matrix products, arithmetic and copies ran while one was open for 0% -> 3% of each run, Pallas kernels for 8% -> 15%
where the time goes in v3:
time: 48.1 us; the launch traced here: 47.7 us
  starting transfers between devices  18.7 us (39%)
  waiting for transfers between devices  14.8 us (31%)
  Pallas kernels  7.77 us (16%)
  local copies, waits for them, and re-layouts  3.4 us (7%)
  other arithmetic  1.55 us (3%)
  between operations  1.54 us (3%)
    ppermute x13, starting transfers between devices, swap(): lax.ppermute(x, axis, [(i, i ^ step) for i in range(lax.axis_size(axis))])  18.7 us
    ppermute x13, waiting for transfers between devices, swap(): lax.ppermute(x, axis, [(i, i ^ step) for i in range(lax.axis_size(axis))])  14.8 us
    pallas_call x9, Pallas kernels, call(): pl.pallas_call(kernel, out_shape=outs, in_specs=spaces, out_specs=jax.tre...  7.77 us
    unnamed x14, local copies, waits for them, and re-layouts  2.63 us
  transfers between devices with their start and end apart: 13, of which 8 were waited for; matrix products, arithmetic and copies ran while one was open for 3% of the time, Pallas kernels for 15%

profile of v3, /device:TPU:0, one launch (start us, length us, event | category | flops | bytes accessed | tf_op | source)
XLA Modules:
  0.0 47.7 jit_solution(5309454238643248895)
XLA Ops:
  0.0 0.0 copy-start
  0.7 0.1 copy-done
  0.9 3.0 %collective-permute-start.4 = (bf16[1,32,512]{2,1,0:T(8,128)(2,1)S(1)}, bf16[1,32,512]{2,1,0:T(8,128)(2,1)S(1)}, u32[]{:S(2)}, u32[]{:S(2)}) collective-permute-start(bf16[1,32,512]{2,1,0:T(8,128)(2,1)S(1)} %constant_dynamic-slice_fusion.bands_ref), channel_id=1, source_target_pairs={{0,1},{1,0},{2,3},{3,2},{4,5},{5,4},{6,7},{7,6},{8,9},{9,8},{10,11... | collective-permute-start | bytes 98312 | tf_op jit(solution)/shard_map/ppermute | solution.py:32
  3.9 1.5 %collective-permute-start.5 = (bf16[1,32,512]{2,1,0:T(8,128)(2,1)S(1)}, bf16[1,32,512]{2,1,0:T(8,128)(2,1)}, u32[]{:S(2)}, u32[]{:S(2)}) collective-permute-start(bf16[1,32,512]{2,1,0:T(8,128)(2,1)S(1)} %constant_dynamic-slice_fusion.bands_ref), channel_id=1, source_target_pairs={{0,2},{1,3},{2,0},{3,1},{4,6},{5,7},{6,4},{7,5},{8,10},{9,11},{10,... | collective-permute-start | bytes 98312 | tf_op jit(solution)/shard_map/ppermute | solution.py:32
  5.4 0.0 collective-permute-start.6
  5.4 2.0 %collective-permute-start = (bf16[1,64,256]{2,1,0:T(8,128)(2,1)}, bf16[1,64,256]{2,1,0:T(8,128)(2,1)S(1)}, u32[]{:S(2)}, u32[]{:S(2)}) collective-permute-start(bf16[1,64,256]{2,1,0:T(8,128)(2,1)} %param.10), channel_id=1, source_target_pairs={{0,8},{4,12},{8,0},{12,4},{16,24},{20,28},{24,16},{28,20},{1,9},{5... | collective-permute-start | bytes 98312 | tf_op jit(solution)/shard_map/ppermute | solution.py:32
  8.1 0.7 %constant_dynamic-slice_fusion.2.bands_ref = bf16[1,32,256]{2,1,0:T(8,128)(2,1)S(1)} fusion(bf16[1,64,256]{2,1,0:T(8,128)(2,1)} %param.10, s32[]{:T(128)S(6)} %select_n.7), kind=kLoop, calls=%fused_computation.23 | loop fusion | bytes 32772 | tf_op jit(solution)/shard_map/dynamic_slice | solution.py:152
  8.9 0.7 %collective-permute-done = bf16[1,64,256]{2,1,0:T(8,128)(2,1)S(1)} collective-permute-done((bf16[1,64,256]{2,1,0:T(8,128)(2,1)}, bf16[1,64,256]{2,1,0:T(8,128)(2,1)S(1)}, u32[]{:S(2)}, u32[]{:S(2)}) %collective-permute-start) | collective-permute-done | bytes 32800 | tf_op jit(solution)/shard_map/ppermute | solution.py:32
  9.6 3.1 %collective-permute-start.1 = (bf16[2,32,256]{2,1,0:T(8,128)(2,1)S(1)}, bf16[2,32,256]{2,1,0:T(8,128)(2,1)S(1)}, u32[]{:S(2)}, u32[]{:S(2)}) collective-permute-start(bf16[2,32,256]{2,1,0:T(8,128)(2,1)S(1)} %pad_maximum_fusion.3.bands_ref), channel_id=1, source_target_pairs={{0,16},{4,20},{8,24},{12,28},{16,0},{20,4},{24,8},{28,12},{1,17},{... | collective-permute-start | bytes 98312 | tf_op jit(solution)/shard_map/ppermute | solution.py:32
  12.7 1.9 %collective-permute-done.1 = bf16[2,32,256]{2,1,0:T(8,128)(2,1)S(1)} collective-permute-done((bf16[2,32,256]{2,1,0:T(8,128)(2,1)S(1)}, bf16[2,32,256]{2,1,0:T(8,128)(2,1)S(1)}, u32[]{:S(2)}, u32[]{:S(2)}) %collective-permute-start.1) | collective-permute-done | bytes 32800 | tf_op jit(solution)/shard_map/ppermute | solution.py:32
  14.6 0.1 collective-permute-start.2
  14.7 0.0 copy-start.1
  14.7 2.2 %copy-done.1 = bf16[2048,1024]{1,0:T(8,128)(2,1)S(1)} copy-done((bf16[2048,1024]{1,0:T(8,128)(2,1)S(1)}, bf16[2048,1024]{1,0:T(8,128)(2,1)}, u32[]{:S(2)}) %copy-start.1) | copy-done | bytes 4194328
  16.9 1.0 %shard_map.92.refs_0_ = f32[256,1024]{1,0:T(8,128)S(1)} custom-call(s32[4]{0:T(128)S(1)} %multiply_xor_fusion.place_ref, bf16[2,32,256]{2,1,0:T(8,128)(2,1)S(1)} %pad_maximum_fusion.3.bands_ref, bf16[2048,1024]{1,0:T(8,128)(2,1)S(1)} %copy-done.1, bf16[256,256]{1,0:T(8,128)(2,1)S(1)} %shard_map.91.refs_0_), custom_call_target="tpu_custom_call" | custom-call | flops 268435456 | bytes 1048576 | tf_op jit(solution)/shard_map/pallas_call | solution.py:20
  17.9 1.0 %shard_map.93.refs_0_ = f32[256,1024]{1,0:T(8,128)S(1)} custom-call(s32[4]{0:T(128)S(1)} %multiply_xor_fusion.place_ref, bf16[4,32,256]{2,1,0:T(8,128)(2,1)S(1)} %pad_maximum_fusion.2.bands_ref, bf16[2048,1024]{1,0:T(8,128)(2,1)S(1)} %copy-done.1, f32[256,1024]{1,0:T(8,128)S(1)} %shard_map.92.refs_0_), custom_call_target="tpu_custom_call" | custom-call | flops 268435456 | bytes 1048576 | tf_op jit(solution)/shard_map/pallas_call | solution.py:20
  18.9 0.0 copy-start.3
  18.9 0.0 copy-start.5
  18.9 0.0 copy-start.6
  18.9 0.0 collective-permute-done.2.bands_ref
  18.9 1.3 %shard_map.94.dens_ref = bf16[256,1024]{1,0:T(8,128)(2,1)S(1)} custom-call(s32[4]{0:T(128)S(1)} %broadcast_xor_fusion.place_ref, bf16[4,32,256]{2,1,0:T(8,128)(2,1)S(1)} %collective-permute-done.2.bands_ref, bf16[2048,1024]{1,0:T(8,128)(2,1)S(1)} %copy-done.1, f32[256,1024]{1,0:T(8,128)S(1)} %shard_map.93.refs_0_), custom_call_target="tpu_custom_call" | custom-call | flops 536870912 | bytes 2097152 | tf_op jit(solution)/shard_map/pallas_call | solution.py:20
  20.2 0.3 copy-done.3
  20.5 0.0 copy-done.5
  20.5 0.0 copy-done.6
  20.5 1.0 %shard_map.96 = bf16[4,128,256]{2,1,0:T(8,128)(2,1)S(1)} custom-call(s32[1]{0:T(128)} %bitcast.me_ref.me_row_ref, s32[8]{0:T(128)S(1)} %copy-done.5, s32[8]{0:T(128)S(1)} %bitcast.19, bf16[8,128,1024]{2,1,0:T(8,128)(2,1)S(1)} %copy-done.3, bf16[256,1024]{1,0:T(8,128)(2,1)S(1)} %shard_map.94.dens_ref), custom_call_target="tpu_custom_call" | custom-call | flops 268435456 | bytes 1048576 | tf_op jit(solution)/shard_map/pallas_call | solution.py:20
  21.5 0.5 %collective-permute-start.3 = (bf16[4,128,256]{2,1,0:T(8,128)(2,1)S(1)}, bf16[4,128,256]{2,1,0:T(8,128)(2,1)S(1)}, u32[]{:S(2)}, u32[]{:S(2)}) collective-permute-start(bf16[4,128,256]{2,1,0:T(8,128)(2,1)S(1)} %shard_map.96), channel_id=1, source_target_pairs={{0,4},{4,0},{8,12},{12,8},{16,20},{20,16},{24,28},{28,24},{1,5},{5... | collective-permute-start | bytes 786440 | tf_op jit(solution)/shard_map/ppermute | solution.py:32
  22.1 0.0 copy-start.2
  22.1 0.0 copy-start.4
  22.1 1.0 %shard_map.95 = bf16[4,128,256]{2,1,0:T(8,128)(2,1)S(1)} custom-call(s32[1]{0:T(128)} %bitcast.me_ref.me_row_ref, s32[8]{0:T(128)S(1)} %copy-done.5, s32[8]{0:T(128)S(1)} %bitcast.20, bf16[8,128,1024]{2,1,0:T(8,128)(2,1)S(1)} %copy-done.3, bf16[256,1024]{1,0:T(8,128)(2,1)S(1)} %shard_map.94.dens_ref), custom_call_target="tpu_custom_call" | custom-call | flops 268435456 | bytes 1048576 | tf_op jit(solution)/shard_map/pallas_call | solution.py:20
  23.1 0.1 collective-permute-done.3
  23.2 2.0 %collective-permute-start.7 = (bf16[256,256]{1,0:T(8,128)(2,1)S(1)}, bf16[256,256]{1,0:T(8,128)(2,1)S(1)}, u32[]{:S(2)}, u32[]{:S(2)}) collective-permute-start(bf16[256,256]{1,0:T(8,128)(2,1)S(1)} %get-tuple-element.16), channel_id=1, source_target_pairs={{0,8},{4,12},{8,0},{12,4},{16,24},{20,28},{24,16},{28,20},{1,9},{5... | collective-permute-start | bytes 393224 | tf_op jit(solution)/shard_map/ppermute | solution.py:32
  25.2 2.8 %collective-permute-start.8 = (bf16[256,256]{1,0:T(8,128)(2,1)S(1)}, bf16[256,256]{1,0:T(8,128)(2,1)S(1)}, u32[]{:S(2)}, u32[]{:S(2)}) collective-permute-start(bf16[256,256]{1,0:T(8,128)(2,1)S(1)} %get-tuple-element.17), channel_id=1, source_target_pairs={{0,16},{4,20},{8,24},{12,28},{16,0},{20,4},{24,8},{28,12},{1,17},{... | collective-permute-start | bytes 393224 | tf_op jit(solution)/shard_map/ppermute | solution.py:32
  28.0 0.0 collective-permute-done.4
  28.0 0.0 collective-permute-start.9
  28.0 0.0 collective-permute-done.5
  28.0 0.0 collective-permute-done.6
  28.1 0.8 %pad_maximum_fusion.1.bands_ref = bf16[4,32,512]{2,1,0:T(8,128)(2,1)S(1)} fusion(bf16[1,32,512]{2,1,0:T(8,128)(2,1)} %collective-permute-done.6, bf16[1,32,512]{2,1,0:T(8,128)(2,1)} %collective-permute-done.5, bf16[1,32,512]{2,1,0:T(8,128)(2,1)S(1)} %collective-permute-done.4, bf16[1,32,512]{2,1,0:T(8,128)(2,1)S(1)} %constant_dynamic-slice_fusion.bands_ref), kind=kLoop, calls=%fused_computation.17 | loop fusion | flops 196608 | bytes 262144 | tf_op jit(solution)/shard_map/concatenate | solution.py:210
  28.9 0.0 copy-done.2
  28.9 1.8 %shard_map.98.dens_ref = bf16[256,1024]{1,0:T(8,128)(2,1)S(1)} custom-call(s32[4]{0:T(128)S(1)} %iota_xor_fusion.place_ref, bf16[4,32,512]{2,1,0:T(8,128)(2,1)S(1)} %pad_maximum_fusion.1.bands_ref, bf16[2048,1024]{1,0:T(8,128)(2,1)S(1)} %copy-done.2, bf16[256,512]{1,0:T(8,128)(2,1)S(1)} %shard_map.97.refs_0_), custom_call_target="tpu_custom_call" | custom-call | flops 1073741824 | bytes 4194304 | tf_op jit(solution)/shard_map/pallas_call | solution.py:20
  30.7 0.7 %collective-permute-done.7.refs_1_ = bf16[256,256]{1,0:T(8,128)(2,1)S(1)} collective-permute-done((bf16[256,256]{1,0:T(8,128)(2,1)S(1)}, bf16[256,256]{1,0:T(8,128)(2,1)S(1)}, u32[]{:S(2)}, u32[]{:S(2)}) %collective-permute-start.7) | collective-permute-done | bytes 131104 | tf_op jit(solution)/shard_map/ppermute | solution.py:32
  31.4 6.8 %collective-permute-done.8.refs_2_ = bf16[256,256]{1,0:T(8,128)(2,1)S(1)} collective-permute-done((bf16[256,256]{1,0:T(8,128)(2,1)S(1)}, bf16[256,256]{1,0:T(8,128)(2,1)S(1)}, u32[]{:S(2)}, u32[]{:S(2)}) %collective-permute-start.8) | collective-permute-done | bytes 131104 | tf_op jit(solution)/shard_map/ppermute | solution.py:32
  38.2 0.0 collective-permute-done.9.refs_3_
  38.2 0.0 copy-done.4
  38.2 0.6 %shard_map.99 = (f32[64,512]{1,0:T(8,128)S(1)}, bf16[64,512]{1,0:T(8,128)(2,1)S(1)}, bf16[64,512]{1,0:T(8,128)(2,1)S(1)}, bf16[64,512]{1,0:T(8,128)(2,1)S(1)}) custom-call(s32[1]{0:T(128)} %bitcast.me_ref.me_row_ref, s32[1]{0:T(128)} %bitcast.1.me_col_ref, bf16[256,1024]{1,0:T(8,128)(2,1)S(1)} %shard_map.98.dens_ref, bf16[256,512]{1,0:T(8,128)(2,1)S(1)} %copy-done.4, ...), custom_call_target="tpu_custom_call" | custom-call | flops 201326592 | bytes 524288 | tf_op jit(solution)/shard_map/pallas_call | solution.py:20
  38.8 1.6 %collective-permute-start.10 = (bf16[64,512]{1,0:T(8,128)(2,1)S(1)}, bf16[64,512]{1,0:T(8,128)(2,1)S(1)}, u32[]{:S(2)}, u32[]{:S(2)}) collective-permute-start(bf16[64,512]{1,0:T(8,128)(2,1)S(1)} %get-tuple-element.12), channel_id=1, source_target_pairs={{0,1},{1,0},{2,3},{3,2},{4,5},{5,4},{6,7},{7,6},{8,9},{9,8},{10,11... | collective-permute-start | bytes 196616 | tf_op jit(solution)/shard_map/ppermute | solution.py:32
  40.3 1.5 %collective-permute-start.11 = (bf16[64,512]{1,0:T(8,128)(2,1)S(1)}, bf16[64,512]{1,0:T(8,128)(2,1)S(1)}, u32[]{:S(2)}, u32[]{:S(2)}) collective-permute-start(bf16[64,512]{1,0:T(8,128)(2,1)S(1)} %get-tuple-element.13), channel_id=1, source_target_pairs={{0,2},{1,3},{2,0},{3,1},{4,6},{5,7},{6,4},{7,5},{8,10},{9,11},{10,... | collective-permute-start | bytes 196616 | tf_op jit(solution)/shard_map/ppermute | solution.py:32
  41.9 0.5 %collective-permute-start.12 = (bf16[64,512]{1,0:T(8,128)(2,1)S(1)}, bf16[64,512]{1,0:T(8,128)(2,1)S(1)}, u32[]{:S(2)}, u32[]{:S(2)}) collective-permute-start(bf16[64,512]{1,0:T(8,128)(2,1)S(1)} %get-tuple-element.14), channel_id=1, source_target_pairs={{0,3},{1,2},{2,1},{3,0},{4,7},{5,6},{6,5},{7,4},{8,11},{9,10},{10,... | collective-permute-start | bytes 196616 | tf_op jit(solution)/shard_map/ppermute | solution.py:32
  42.3 1.4 %collective-permute-done.10 = bf16[64,512]{1,0:T(8,128)(2,1)S(1)} collective-permute-done((bf16[64,512]{1,0:T(8,128)(2,1)S(1)}, bf16[64,512]{1,0:T(8,128)(2,1)S(1)}, u32[]{:S(2)}, u32[]{:S(2)}) %collective-permute-start.10) | collective-permute-done | bytes 65568 | tf_op jit(solution)/shard_map/ppermute | solution.py:32
  43.8 1.3 %collective-permute-done.11 = bf16[64,512]{1,0:T(8,128)(2,1)S(1)} collective-permute-done((bf16[64,512]{1,0:T(8,128)(2,1)S(1)}, bf16[64,512]{1,0:T(8,128)(2,1)S(1)}, u32[]{:S(2)}, u32[]{:S(2)}) %collective-permute-start.11) | collective-permute-done | bytes 65568 | tf_op jit(solution)/shard_map/ppermute | solution.py:32
  45.0 2.0 %collective-permute-done.12 = bf16[64,512]{1,0:T(8,128)(2,1)S(1)} collective-permute-done((bf16[64,512]{1,0:T(8,128)(2,1)S(1)}, bf16[64,512]{1,0:T(8,128)(2,1)S(1)}, u32[]{:S(2)}, u32[]{:S(2)}) %collective-permute-start.12) | collective-permute-done | bytes 65568 | tf_op jit(solution)/shard_map/ppermute | solution.py:32
  47.0 0.7 %convert_add_fusion = f32[64,512]{1,0:T(8,128)} fusion(bf16[64,512]{1,0:T(8,128)(2,1)S(1)} %collective-permute-done.12, bf16[64,512]{1,0:T(8,128)(2,1)S(1)} %collective-permute-done.11, f32[64,512]{1,0:T(8,128)S(1)} %get-tuple-element.11, bf16[64,512]{1,0:T(8,128)(2,1)S(1)} %collective-permute-done.10), kind=kLoop, calls=%fused_computation.18 | loop fusion | flops 196608 | bytes 458752 | tf_op jit(solution)/shard_map/add | solution.py:231
  (10 shorter events, 0.2 us)
Async XLA Ops:
  0.0 0.8 %copy-start = (bf16[1,64,512]{2,1,0:T(8,128)(2,1)S(1)}, bf16[1,64,512]{2,1,0:T(8,128)(2,1)}, u32[]{:S(2)}) copy-start(bf16[1,64,512]{2,1,0:T(8,128)(2,1)} %param.9) | copy-start | bytes 196612
  0.9 27.2 %collective-permute-start.4 = (bf16[1,32,512]{2,1,0:T(8,128)(2,1)S(1)}, bf16[1,32,512]{2,1,0:T(8,128)(2,1)S(1)}, u32[]{:S(2)}, u32[]{:S(2)}) collective-permute-start(bf16[1,32,512]{2,1,0:T(8,128)(2,1)S(1)} %constant_dynamic-slice_fusion.bands_ref), channel_id=1, source_target_pairs={{0,1},{1,0},{2,3},{3,2},{4,5},{5,4},{6,7},{7,6},{8,9},{9,8},{10,11... | collective-permute-start | bytes 98312 | tf_op jit(solution)/shard_map/ppermute | solution.py:32
  3.9 24.2 %collective-permute-start.5 = (bf16[1,32,512]{2,1,0:T(8,128)(2,1)S(1)}, bf16[1,32,512]{2,1,0:T(8,128)(2,1)}, u32[]{:S(2)}, u32[]{:S(2)}) collective-permute-start(bf16[1,32,512]{2,1,0:T(8,128)(2,1)S(1)} %constant_dynamic-slice_fusion.bands_ref), channel_id=1, source_target_pairs={{0,2},{1,3},{2,0},{3,1},{4,6},{5,7},{6,4},{7,5},{8,10},{9,11},{10,... | collective-permute-start | bytes 98312 | tf_op jit(solution)/shard_map/ppermute | solution.py:32
  5.4 22.6 %collective-permute-start.6 = (bf16[1,32,512]{2,1,0:T(8,128)(2,1)S(1)}, bf16[1,32,512]{2,1,0:T(8,128)(2,1)}, u32[]{:S(2)}, u32[]{:S(2)}) collective-permute-start(bf16[1,32,512]{2,1,0:T(8,128)(2,1)S(1)} %constant_dynamic-slice_fusion.bands_ref), channel_id=1, source_target_pairs={{0,3},{1,2},{2,1},{3,0},{4,7},{5,6},{6,5},{7,4},{8,11},{9,10},{10,... | collective-permute-start | bytes 98312 | tf_op jit(solution)/shard_map/ppermute | solution.py:32
  5.4 4.1 %collective-permute-start = (bf16[1,64,256]{2,1,0:T(8,128)(2,1)}, bf16[1,64,256]{2,1,0:T(8,128)(2,1)S(1)}, u32[]{:S(2)}, u32[]{:S(2)}) collective-permute-start(bf16[1,64,256]{2,1,0:T(8,128)(2,1)} %param.10), channel_id=1, source_target_pairs={{0,8},{4,12},{8,0},{12,4},{16,24},{20,28},{24,16},{28,20},{1,9},{5... | collective-permute-start | bytes 98312 | tf_op jit(solution)/shard_map/ppermute | solution.py:32
  9.6 5.0 %collective-permute-start.1 = (bf16[2,32,256]{2,1,0:T(8,128)(2,1)S(1)}, bf16[2,32,256]{2,1,0:T(8,128)(2,1)S(1)}, u32[]{:S(2)}, u32[]{:S(2)}) collective-permute-start(bf16[2,32,256]{2,1,0:T(8,128)(2,1)S(1)} %pad_maximum_fusion.3.bands_ref), channel_id=1, source_target_pairs={{0,16},{4,20},{8,24},{12,28},{16,0},{20,4},{24,8},{28,12},{1,17},{... | collective-permute-start | bytes 98312 | tf_op jit(solution)/shard_map/ppermute | solution.py:32
  14.6 4.3 %collective-permute-start.2 = (bf16[4,32,256]{2,1,0:T(8,128)(2,1)S(1)}, bf16[4,32,256]{2,1,0:T(8,128)(2,1)S(1)}, u32[]{:S(2)}, u32[]{:S(2)}) collective-permute-start(bf16[4,32,256]{2,1,0:T(8,128)(2,1)S(1)} %pad_maximum_fusion.2.bands_ref), channel_id=1, source_target_pairs={{0,4},{4,0},{8,12},{12,8},{16,20},{20,16},{24,28},{28,24},{1,5},{5... | collective-permute-start | bytes 196616 | tf_op jit(solution)/shard_map/ppermute | solution.py:32
  14.7 2.2 %copy-start.1 = (bf16[2048,1024]{1,0:T(8,128)(2,1)S(1)}, bf16[2048,1024]{1,0:T(8,128)(2,1)}, u32[]{:S(2)}) copy-start(bf16[2048,1024]{1,0:T(8,128)(2,1)} %table_ref.7) | copy-start | bytes 12582916
  18.9 1.6 %copy-start.3 = (bf16[8,128,1024]{2,1,0:T(8,128)(2,1)S(1)}, bf16[8,128,1024]{2,1,0:T(8,128)(2,1)}, u32[]{:S(2)}) copy-start(bf16[8,128,1024]{2,1,0:T(8,128)(2,1)} %screened_ref.3) | copy-start | bytes 6291460
  18.9 1.6 %copy-start.5 = (s32[8]{0:T(128)S(1)}, s32[8]{0:T(128)}, u32[]{:S(2)}) copy-start(s32[8]{0:T(128)} %owner_ref.3) | copy-start | bytes 100
  18.9 1.6 %copy-start.6 = (s32[8,1]{0,1:T(1,128)S(1)}, s32[8,1]{0,1:T(1,128)}, u32[]{:S(2)}) copy-start(s32[8,1]{0,1:T(1,128)} %param.16) | copy-start | bytes 100
  21.5 1.7 %collective-permute-start.3 = (bf16[4,128,256]{2,1,0:T(8,128)(2,1)S(1)}, bf16[4,128,256]{2,1,0:T(8,128)(2,1)S(1)}, u32[]{:S(2)}, u32[]{:S(2)}) collective-permute-start(bf16[4,128,256]{2,1,0:T(8,128)(2,1)S(1)} %shard_map.96), channel_id=1, source_target_pairs={{0,4},{4,0},{8,12},{12,8},{16,20},{20,16},{24,28},{28,24},{1,5},{5... | collective-permute-start | bytes 786440 | tf_op jit(solution)/shard_map/ppermute | solution.py:32
  22.1 6.8 %copy-start.2 = (bf16[2048,1024]{1,0:T(8,128)(2,1)S(1)}, bf16[2048,1024]{1,0:T(8,128)(2,1)}, u32[]{:S(2)}) copy-start(bf16[2048,1024]{1,0:T(8,128)(2,1)} %table_ref.7) | copy-start | bytes 12582916
  22.1 16.1 %copy-start.4 = (bf16[256,512]{1,0:T(8,128)(2,1)S(1)}, bf16[256,512]{1,0:T(8,128)(2,1)}, u32[]{:S(2)}) copy-start(bf16[256,512]{1,0:T(8,128)(2,1)} %trial_ref.1) | copy-start | bytes 786436
  23.2 8.1 %collective-permute-start.7 = (bf16[256,256]{1,0:T(8,128)(2,1)S(1)}, bf16[256,256]{1,0:T(8,128)(2,1)S(1)}, u32[]{:S(2)}, u32[]{:S(2)}) collective-permute-start(bf16[256,256]{1,0:T(8,128)(2,1)S(1)} %get-tuple-element.16), channel_id=1, source_target_pairs={{0,8},{4,12},{8,0},{12,4},{16,24},{20,28},{24,16},{28,20},{1,9},{5... | collective-permute-start | bytes 393224 | tf_op jit(solution)/shard_map/ppermute | solution.py:32
  25.2 12.9 %collective-permute-start.8 = (bf16[256,256]{1,0:T(8,128)(2,1)S(1)}, bf16[256,256]{1,0:T(8,128)(2,1)S(1)}, u32[]{:S(2)}, u32[]{:S(2)}) collective-permute-start(bf16[256,256]{1,0:T(8,128)(2,1)S(1)} %get-tuple-element.17), channel_id=1, source_target_pairs={{0,16},{4,20},{8,24},{12,28},{16,0},{20,4},{24,8},{28,12},{1,17},{... | collective-permute-start | bytes 393224 | tf_op jit(solution)/shard_map/ppermute | solution.py:32
  28.0 10.1 %collective-permute-start.9 = (bf16[256,256]{1,0:T(8,128)(2,1)S(1)}, bf16[256,256]{1,0:T(8,128)(2,1)S(1)}, u32[]{:S(2)}, u32[]{:S(2)}) collective-permute-start(bf16[256,256]{1,0:T(8,128)(2,1)S(1)} %get-tuple-element.15), channel_id=1, source_target_pairs={{0,24},{4,28},{8,16},{12,20},{16,8},{20,12},{24,0},{28,4},{1,25},{... | collective-permute-start | bytes 393224 | tf_op jit(solution)/shard_map/ppermute | solution.py:32
  38.8 5.0 %collective-permute-start.10 = (bf16[64,512]{1,0:T(8,128)(2,1)S(1)}, bf16[64,512]{1,0:T(8,128)(2,1)S(1)}, u32[]{:S(2)}, u32[]{:S(2)}) collective-permute-start(bf16[64,512]{1,0:T(8,128)(2,1)S(1)} %get-tuple-element.12), channel_id=1, source_target_pairs={{0,1},{1,0},{2,3},{3,2},{4,5},{5,4},{6,7},{7,6},{8,9},{9,8},{10,11... | collective-permute-start | bytes 196616 | tf_op jit(solution)/shard_map/ppermute | solution.py:32
  40.3 4.7 %collective-permute-start.11 = (bf16[64,512]{1,0:T(8,128)(2,1)S(1)}, bf16[64,512]{1,0:T(8,128)(2,1)S(1)}, u32[]{:S(2)}, u32[]{:S(2)}) collective-permute-start(bf16[64,512]{1,0:T(8,128)(2,1)S(1)} %get-tuple-element.13), channel_id=1, source_target_pairs={{0,2},{1,3},{2,0},{3,1},{4,6},{5,7},{6,4},{7,5},{8,10},{9,11},{10,... | collective-permute-start | bytes 196616 | tf_op jit(solution)/shard_map/ppermute | solution.py:32
  41.9 5.2 %collective-permute-start.12 = (bf16[64,512]{1,0:T(8,128)(2,1)S(1)}, bf16[64,512]{1,0:T(8,128)(2,1)S(1)}, u32[]{:S(2)}, u32[]{:S(2)}) collective-permute-start(bf16[64,512]{1,0:T(8,128)(2,1)S(1)} %get-tuple-element.14), channel_id=1, source_target_pairs={{0,3},{1,2},{2,1},{3,0},{4,7},{5,6},{6,5},{7,4},{8,11},{9,10},{10,... | collective-permute-start | bytes 196616 | tf_op jit(solution)/shard_map/ppermute | solution.py:32

commit v4 on v3

--- a/solution.py
+++ b/solution.py
@@ -13,7 +13,7 @@
 NP = NVW * NCW
 GRANT = 16 << 20
 VMEM = pl.BlockSpec(memory_space=pltpu.VMEM)
-SMEM = pl.BlockSpec(memory_space=pltpu.SMEM)
+ANY = pl.BlockSpec(memory_space=pl.ANY)
 
 
 def call(kernel, outs, *args, spaces, scratch=(), flops=0, moved=0):
@@ -38,23 +38,56 @@
     return products.reshape(NP, bands.shape[1]).astype(jnp.bfloat16)
 
 
-def products_kernel(bands_ref, out_ref):
-    out_ref[...] = products_of(bands_ref[0])
-
-
-def products(bands):
+def picked(which, window_ref, waves_ref):
+    bands = waves_ref.shape[1]
+    row = lax.broadcasted_iota(jnp.int32, (NVW + NCW, bands), 0)
+    band = lax.broadcasted_iota(jnp.int32, (NVW + NCW, bands), 1)
+    chooser = jnp.where(band - row == window_ref[:, which : which + 1], 1.0, 0.0).astype(jnp.bfloat16)
+    return jnp.dot(chooser, waves_ref[0], preferred_element_type=jnp.float32).astype(jnp.bfloat16)
+
+
+def window_kernel(which, window_ref, waves_ref, bands_ref, prod_ref):
+    bands = picked(which, window_ref, waves_ref)
+    bands_ref[0] = bands
+    prod_ref[...] = products_of(bands)
+
+
+def windowed(which, starts, array):
+    points = array.shape[2]
     return call(
-        products_kernel,
-        jax.ShapeDtypeStruct((NP, bands.shape[2]), jnp.bfloat16),
-        bands,
-        spaces=[VMEM],
+        functools.partial(window_kernel, which),
+        [
+            jax.ShapeDtypeStruct((1, NVW + NCW, points), jnp.bfloat16),
+            jax.ShapeDtypeStruct((NP, points), jnp.bfloat16),
+        ],
+        starts,
+        array,
+        spaces=[VMEM] * 2,
         flops=1 << 32,
-        moved=NP * bands.shape[2],
-    )
-
-
-def density_kernel(todo, given, place_ref, bands_ref, table_ref, *refs):
-    refs, out_ref, prod_ref = list(refs[:-2]), refs[-2], refs[-1]
+        moved=NP * points,
+    )
+
+
+def pair_kernel(window_ref, waves_ref, mine_ref, out_ref):
+    out_ref[0] = mine_ref[0]
+    out_ref[1] = picked(0, window_ref, waves_ref)
+
+
+def pair(starts, array, mine):
+    return call(
+        pair_kernel,
+        jax.ShapeDtypeStruct((2, *mine.shape[1:]), jnp.bfloat16),
+        starts,
+        array,
+        mine,
+        spaces=[VMEM] * 3,
+        flops=2 * mine.size * array.shape[1],
+        moved=array.size * 2,
+    )
+
+
+def density_kernel(todo, given, place, early, bands_ref, table_ref, *refs):
+    refs, out_ref, prod_ref = list(refs[: len(refs) - 2 - early]), refs[-2], refs[-1]
     ready_ref = refs.pop(0) if given else None
     addend_ref = refs.pop(0) if refs else None
     _, _, points = bands_ref.shape
@@ -63,43 +96,43 @@
             prod_ref[s] = products_of(bands_ref[s])
     waves = table_ref.shape[1]
     tile = min(256, waves)
+    starts = [pl.multiple_of(place(s) * points, points) for s in range(bands_ref.shape[0])]
     for n in range(0, waves, tile):
         total = None if addend_ref is None else addend_ref[:, n : n + tile]
         for s in todo:
-            at = pl.multiple_of(place_ref[s] * points, points)
             term = jnp.dot(
                 prod_ref[s] if s or not given else ready_ref[...],
-                table_ref[pl.ds(at, points), n : n + tile],
+                table_ref[pl.ds(starts[s], points), n : n + tile],
                 preferred_element_type=jnp.float32,
             )
             total = term if total is None else total + term
         out_ref[:, n : n + tile] = total.astype(out_ref.dtype)
 
 
-def density(places, bands, table, ready=None, addend=None, final=True, todo=None):
+def density(place, bands, table, ready=None, addend=None, final=True, todo=None, early=()):
     waves = table.shape[1]
     count, _, points = bands.shape
     todo = range(count) if todo is None else todo
     more = [x for x in (ready, addend) if x is not None]
     return call(
-        functools.partial(density_kernel, todo, ready is not None),
+        functools.partial(density_kernel, todo, ready is not None, place, len(early)),
         jax.ShapeDtypeStruct((NP, waves), jnp.bfloat16 if final else jnp.float32),
-        places,
         bands,
         table,
         *more,
-        spaces=[SMEM, VMEM, VMEM] + [VMEM] * len(more),
+        *early,
+        spaces=[VMEM] * (2 + len(more)) + [ANY] * len(early),
         scratch=[pltpu.VMEM((count, NP, points), jnp.bfloat16)],
         flops=2 * NP * len(todo) * points * waves,
         moved=2 * len(todo) * points * waves,
     )
 
 
-def weighted_kernel(flip, me_ref, owner_ref, transfer_ref, screened_ref, dens_ref, out_ref, rows_ref):
+def weighted_kernel(flip, slots_ref, screened_ref, dens_ref, out_ref, rows_ref):
     chips, share, waves = rows_ref.shape
-    me = me_ref[0] ^ flip
+    slots = slots_ref[...]
     for s in range(chips):
-        rows_ref[s] = screened_ref[owner_ref[transfer_ref[me ^ (2 * s)]]]
+        rows_ref[s] = screened_ref[slots[0, flip * chips + s]]
     out_ref[...] = (
         lax.dot_general(
             rows_ref[...].reshape(chips * share, waves),
@@ -112,10 +145,10 @@
     )
 
 
-def partial_kernel(scale, me_row_ref, me_col_ref, dens_ref, trial_ref, *refs):
+def partial_kernel(scale, dens_ref, trial_ref, *refs):
     count = dens_ref.shape[1] // refs[0].shape[0]
     pieces, outs, (weighted_ref, part_ref) = refs[:count], refs[count:-2], refs[-2:]
-    me = me_row_ref[0]
+    me = lax.axis_index("row")
     for s, piece in enumerate(pieces):
         share = piece.shape[0] // 2
         first = me ^ (2 * s)
@@ -127,7 +160,7 @@
     part_ref[...] = jnp.dot(block, trial_ref[...], preferred_element_type=jnp.float32) * scale
     rows = outs[0].shape[0]
     for s, out in enumerate(outs):
-        at = pl.multiple_of((me_col_ref[0] ^ s) * rows, rows)
+        at = pl.multiple_of((lax.axis_index("col") ^ s) * rows, rows)
         out[...] = part_ref[pl.ds(at, rows), :].astype(out.dtype)
 
 
@@ -144,18 +177,27 @@
 ):
     rows, cols = lax.axis_size("row"), lax.axis_size("col")
     chips = rows // 2
-    me_row, me_col = lax.axis_index("row"), lax.axis_index("col")
     waves, share = plane_wave.shape[1], screened.shape[1]
-    steps = jnp.arange(chips, dtype=jnp.int32)
-
-    def window(array, start):
-        return lax.dynamic_slice_in_dim(array, start[0], NVW + NCW, 1)
-
-    near = me_row ^ (2 * steps)
-    bands = window(waves_col, window_col)
-    own = products(bands)
+
+    def near(s):
+        return lax.axis_index("row") ^ (2 * s)
+
+    def across(s):
+        return near(s) ^ 1
+
+    def column(s):
+        return lax.axis_index("col") ^ s
+
+    starts = jnp.where(jnp.arange(2) == 0, window_col, window_row)[None]
+    bands, own = windowed(0, starts, waves_col)
     if rows > 2:
-        bands = jnp.concatenate([bands, window(swap(waves_col, "row", 2), window_col)])
+        bands = pair(starts, swap(waves_col, "row", 2), bands)
+    every = jnp.arange(rows, dtype=jnp.int32)
+    order = lax.axis_index("row") ^ jnp.concatenate([every[::2], every[1::2]])
+    transfers = jnp.sum(jnp.where(order[:, None] == every, transfer_table[:, 0], 0), axis=1)
+    slots = jnp.sum(jnp.where(transfers[:, None] == every, owner_slot, 0), axis=1)[None]
+    early = (slots,)
+
     half, step = None, 4
     while step < rows:
         done = step // 4 if step > 4 else 0
@@ -180,19 +222,18 @@
         todo=range(chips // 2 if half is not None else 0, chips),
         addend=half,
         ready=own if half is None else None,
-    )
-    dens_col = density(near ^ 1, other, plane_wave, addend=half)
+        early=early,
+    )
+    dens_col = density(across, other, plane_wave, addend=half)
 
     def weighted(flip):
         return call(
             functools.partial(weighted_kernel, flip),
             jax.ShapeDtypeStruct((chips, share, NP), jnp.bfloat16),
-            me_row[None],
-            owner_slot,
-            transfer_table[:, 0],
+            slots,
             screened,
             dens_col,
-            spaces=[SMEM, SMEM, SMEM, VMEM, VMEM],
+            spaces=[VMEM] * 3,
             scratch=[pltpu.VMEM((chips, share, waves), jnp.bfloat16)],
             flops=2 * chips * share * waves * NP,
             moved=2 * chips * share * waves,
@@ -205,23 +246,19 @@
         pieces[s] = swap(both[s], "row", 2 * s)
 
     late_waves, _ = lax.optimization_barrier((waves_row, both))
-    bands_row = window(late_waves, window_row)
-    own_row = products(bands_row)
+    bands_row, own_row = windowed(1, starts, late_waves)
     row_bands = jnp.concatenate([bands_row] + [swap(bands_row, "col", s) for s in range(1, cols)])
-    places = me_col ^ jnp.arange(cols, dtype=jnp.int32)
-    dens_row = density(places, row_bands, plane_wave, own_row)
+    dens_row = density(column, row_bands, plane_wave, own_row)
 
     vectors = trial.shape[1]
     kinds = [jnp.float32] + [jnp.bfloat16] * (cols - 1)
     parts = call(
         functools.partial(partial_kernel, (cols * NP) ** (-0.5)),
         [jax.ShapeDtypeStruct((NP // cols, vectors), kind) for kind in kinds],
-        me_row[None],
-        me_col[None],
         dens_row,
         trial,
         *pieces,
-        spaces=[SMEM, SMEM] + [VMEM] * (2 + chips),
+        spaces=[VMEM] * (2 + chips),
         scratch=[pltpu.VMEM((waves, NP), jnp.bfloat16), pltpu.VMEM((NP, vectors), jnp.float32)],
         flops=2 * NP * NP * (waves + vectors),
         moved=2 * waves * NP,

time: 48.1 us -> 44.9 us (0.933)
  Pallas kernels: 7.77 us -> 5.15 us
  starting transfers between devices: 18.7 us -> 17.8 us
  local copies, waits for them, and re-layouts: 3.4 us -> 3.99 us
    pallas_call x9 -> x10, Pallas kernels: 7.77 us -> 5.15 us  [call(): pl.pallas_call(kernel, out_shape=outs, in_specs=spaces, out_specs=jax.tre...]
    unnamed x14 -> x16, local copies, waits for them, and re-layouts: 2.63 us -> 3.79 us
    ppermute x13, starting transfers between devices: 18.7 us -> 17.8 us  [swap(): lax.ppermute(x, axis, [(i, i ^ step) for i in range(lax.axis_size(axis))])]
    concatenate x1, other arithmetic: 0.79 us -> 0.02 us  [shards(): jnp.concatenate([bands_row] + [swap(bands_row, 'col', s) for s in range(1...]
    dynamic_slice x3 -> x0, local copies, waits for them, and re-layouts: 0.77 us -> none  [window(): return lax.dynamic_slice_in_dim(array, start[0], NVW + NCW, 1)]
  transfers between devices with their start and end apart: 13 -> 13, of which waited for: 8 -> 6; matrix products, arithmetic and copies ran while one was open for 3% -> 2% of each run, Pallas kernels for 15% -> 7%
where the time goes in v4:
time: 44.9 us; the launch traced here: 44.6 us
  starting transfers between devices  17.8 us (40%)
  waiting for transfers between devices  14.9 us (33%)
  Pallas kernels  5.15 us (11%)
  local copies, waits for them, and re-layouts  3.99 us (9%)
  between operations  1.51 us (3%)
  other arithmetic  1.2 us (3%)
    ppermute x13, starting transfers between devices, swap(): lax.ppermute(x, axis, [(i, i ^ step) for i in range(lax.axis_size(axis))])  17.8 us
    ppermute x13, waiting for transfers between devices, swap(): lax.ppermute(x, axis, [(i, i ^ step) for i in range(lax.axis_size(axis))])  14.9 us
    pallas_call x10, Pallas kernels, call(): pl.pallas_call(kernel, out_shape=outs, in_specs=spaces, out_specs=jax.tre...  5.15 us
    unnamed x16, local copies, waits for them, and re-layouts  3.79 us
  transfers between devices with their start and end apart: 13, of which 6 were waited for; matrix products, arithmetic and copies ran while one was open for 2% of the time, Pallas kernels for 7%

profile of v4, /device:TPU:0, one launch (start us, length us, event | category | flops | bytes accessed | tf_op | source)
XLA Modules:
  0.0 44.6 jit_solution(16954761877501882596)
XLA Ops:
  0.0 3.1 %collective-permute-start = (bf16[1,64,256]{2,1,0:T(8,128)(2,1)}, bf16[1,64,256]{2,1,0:T(8,128)(2,1)S(1)}, u32[]{:S(2)}, u32[]{:S(2)}) collective-permute-start(bf16[1,64,256]{2,1,0:T(8,128)(2,1)} %waves_ref.1), channel_id=1, source_target_pairs={{0,8},{4,12},{8,0},{12,4},{16,24},{20,28},{24,16},{28,20},{1,9},{5... | collective-permute-start | bytes 98312 | tf_op jit(solution)/shard_map/ppermute | solution.py:32
  4.4 0.0 copy-start.5
  4.4 0.7 %copy-done.5 = bf16[1,64,256]{2,1,0:T(8,128)(2,1)S(1)} copy-done((bf16[1,64,256]{2,1,0:T(8,128)(2,1)S(1)}, bf16[1,64,256]{2,1,0:T(8,128)(2,1)}, u32[]{:S(2)}) %copy-start.5) | copy-done | bytes 32792
  5.1 0.0 copy-start.6
  5.1 0.0 copy-start.7
  5.1 0.2 shard_map.91
  5.4 0.1 slice.18
  5.5 0.1 slice.19
  5.6 0.1 add_xor_fusion
  5.6 0.0 collective-permute-done.waves_ref
  5.6 0.2 shard_map.92.bands_ref
  5.8 2.6 %collective-permute-start.1 = (bf16[2,32,256]{2,1,0:T(8,128)(2,1)S(1)}, bf16[2,32,256]{2,1,0:T(8,128)(2,1)S(1)}, u32[]{:S(2)}, u32[]{:S(2)}) collective-permute-start(bf16[2,32,256]{2,1,0:T(8,128)(2,1)S(1)} %shard_map.92.bands_ref), channel_id=1, source_target_pairs={{0,16},{4,20},{8,24},{12,28},{16,0},{20,4},{24,8},{28,12},{1,17},{... | collective-permute-start | bytes 98312 | tf_op jit(solution)/shard_map/ppermute | solution.py:32
  8.4 0.0 copy-done.6
  8.4 0.2 select_reduce_fusion.1
  8.6 2.0 %collective-permute-done.1 = bf16[2,32,256]{2,1,0:T(8,128)(2,1)S(1)} collective-permute-done((bf16[2,32,256]{2,1,0:T(8,128)(2,1)S(1)}, bf16[2,32,256]{2,1,0:T(8,128)(2,1)S(1)}, u32[]{:S(2)}, u32[]{:S(2)}) %collective-permute-start.1) | collective-permute-done | bytes 32800 | tf_op jit(solution)/shard_map/ppermute | solution.py:32
  10.7 0.1 collective-permute-start.2
  10.7 0.0 copy-done.7
  10.7 0.2 select_reduce_fusion
  10.9 0.0 copy-start
  10.9 2.2 %copy-done = bf16[2048,1024]{1,0:T(8,128)(2,1)S(1)} copy-done((bf16[2048,1024]{1,0:T(8,128)(2,1)S(1)}, bf16[2048,1024]{1,0:T(8,128)(2,1)}, u32[]{:S(2)}) %copy-start) | copy-done | bytes 4194328
  13.1 0.4 shard_map.93.refs_0_
  13.6 0.5 %shard_map.94.refs_0_ = f32[256,1024]{1,0:T(8,128)S(1)} custom-call(bf16[4,32,256]{2,1,0:T(8,128)(2,1)S(1)} %pad_maximum_fusion.2.bands_ref, bf16[2048,1024]{1,0:T(8,128)(2,1)S(1)} %copy-done, f32[256,1024]{1,0:T(8,128)S(1)} %shard_map.93.refs_0_, s32[1,8]{1,0:T(1,128)S(1)} %bitcast.14), custom_call_target="tpu_custom_call" | custom-call | flops 268435456 | bytes 1048576 | tf_op jit(solution)/shard_map/pallas_call | solution.py:20
  14.0 0.0 copy-start.2
  14.0 0.0 copy-start.4
  14.1 0.0 collective-permute-done.2.bands_ref
  14.1 0.7 %shard_map.95.dens_ref = bf16[256,1024]{1,0:T(8,128)(2,1)S(1)} custom-call(bf16[4,32,256]{2,1,0:T(8,128)(2,1)S(1)} %collective-permute-done.2.bands_ref, bf16[2048,1024]{1,0:T(8,128)(2,1)S(1)} %copy-done, f32[256,1024]{1,0:T(8,128)S(1)} %shard_map.94.refs_0_), custom_call_target="tpu_custom_call" | custom-call | flops 536870912 | bytes 2097152 | tf_op jit(solution)/shard_map/pallas_call | solution.py:20
  14.8 0.8 %copy-done.2 = bf16[8,128,1024]{2,1,0:T(8,128)(2,1)S(1)} copy-done((bf16[8,128,1024]{2,1,0:T(8,128)(2,1)S(1)}, bf16[8,128,1024]{2,1,0:T(8,128)(2,1)}, u32[]{:S(2)}) %copy-start.2) | copy-done | bytes 2097176
  15.6 0.5 %shard_map.97 = bf16[4,128,256]{2,1,0:T(8,128)(2,1)S(1)} custom-call(s32[1,8]{1,0:T(1,128)S(1)} %bitcast.15, bf16[8,128,1024]{2,1,0:T(8,128)(2,1)S(1)} %copy-done.2, bf16[256,1024]{1,0:T(8,128)(2,1)S(1)} %shard_map.95.dens_ref), custom_call_target="tpu_custom_call" | custom-call | flops 268435456 | bytes 1048576 | tf_op jit(solution)/shard_map/pallas_call | solution.py:20
  16.1 0.5 %collective-permute-start.3 = (bf16[4,128,256]{2,1,0:T(8,128)(2,1)S(1)}, bf16[4,128,256]{2,1,0:T(8,128)(2,1)S(1)}, u32[]{:S(2)}, u32[]{:S(2)}) collective-permute-start(bf16[4,128,256]{2,1,0:T(8,128)(2,1)S(1)} %shard_map.97), channel_id=1, source_target_pairs={{0,4},{4,0},{8,12},{12,8},{16,20},{20,16},{24,28},{28,24},{1,5},{5... | collective-permute-start | bytes 786440 | tf_op jit(solution)/shard_map/ppermute | solution.py:32
  16.7 0.0 copy-done.4
  16.7 0.2 shard_map.98
  16.9 0.0 copy-start.1
  16.9 0.0 copy-start.3
  17.0 1.6 %collective-permute-start.4 = (bf16[1,32,512]{2,1,0:T(8,128)(2,1)S(1)}, bf16[1,32,512]{2,1,0:T(8,128)(2,1)S(1)}, u32[]{:S(2)}, u32[]{:S(2)}) collective-permute-start(bf16[1,32,512]{2,1,0:T(8,128)(2,1)S(1)} %get-tuple-element.17), channel_id=1, source_target_pairs={{0,1},{1,0},{2,3},{3,2},{4,5},{5,4},{6,7},{7,6},{8,9},{9,8},{10,11... | collective-permute-start | bytes 98312 | tf_op jit(solution)/shard_map/ppermute | solution.py:32
  18.5 1.5 %collective-permute-start.5 = (bf16[1,32,512]{2,1,0:T(8,128)(2,1)S(1)}, bf16[1,32,512]{2,1,0:T(8,128)(2,1)S(1)}, u32[]{:S(2)}, u32[]{:S(2)}) collective-permute-start(bf16[1,32,512]{2,1,0:T(8,128)(2,1)S(1)} %get-tuple-element.17), channel_id=1, source_target_pairs={{0,2},{1,3},{2,0},{3,1},{4,6},{5,7},{6,4},{7,5},{8,10},{9,11},{10,... | collective-permute-start | bytes 98312 | tf_op jit(solution)/shard_map/ppermute | solution.py:32
  20.0 0.5 %collective-permute-start.6 = (bf16[1,32,512]{2,1,0:T(8,128)(2,1)S(1)}, bf16[1,32,512]{2,1,0:T(8,128)(2,1)S(1)}, u32[]{:S(2)}, u32[]{:S(2)}) collective-permute-start(bf16[1,32,512]{2,1,0:T(8,128)(2,1)S(1)} %get-tuple-element.17), channel_id=1, source_target_pairs={{0,3},{1,2},{2,1},{3,0},{4,7},{5,6},{6,5},{7,4},{8,11},{9,10},{10,... | collective-permute-start | bytes 98312 | tf_op jit(solution)/shard_map/ppermute | solution.py:32
  20.5 0.5 %shard_map.96 = bf16[4,128,256]{2,1,0:T(8,128)(2,1)S(1)} custom-call(s32[1,8]{1,0:T(1,128)S(1)} %bitcast.16, bf16[8,128,1024]{2,1,0:T(8,128)(2,1)S(1)} %copy-done.2, bf16[256,1024]{1,0:T(8,128)(2,1)S(1)} %shard_map.95.dens_ref), custom_call_target="tpu_custom_call" | custom-call | flops 268435456 | bytes 1048576 | tf_op jit(solution)/shard_map/pallas_call | solution.py:20
  21.0 0.0 collective-permute-done.3
  21.1 1.6 %collective-permute-start.7 = (bf16[256,256]{1,0:T(8,128)(2,1)S(1)}, bf16[256,256]{1,0:T(8,128)(2,1)S(1)}, u32[]{:S(2)}, u32[]{:S(2)}) collective-permute-start(bf16[256,256]{1,0:T(8,128)(2,1)S(1)} %get-tuple-element.24), channel_id=1, source_target_pairs={{0,8},{4,12},{8,0},{12,4},{16,24},{20,28},{24,16},{28,20},{1,9},{5... | collective-permute-start | bytes 393224 | tf_op jit(solution)/shard_map/ppermute | solution.py:32
  22.7 2.9 %collective-permute-start.8 = (bf16[256,256]{1,0:T(8,128)(2,1)S(1)}, bf16[256,256]{1,0:T(8,128)(2,1)S(1)}, u32[]{:S(2)}, u32[]{:S(2)}) collective-permute-start(bf16[256,256]{1,0:T(8,128)(2,1)S(1)} %get-tuple-element.25), channel_id=1, source_target_pairs={{0,16},{4,20},{8,24},{12,28},{16,0},{20,4},{24,8},{28,12},{1,17},{... | collective-permute-start | bytes 393224 | tf_op jit(solution)/shard_map/ppermute | solution.py:32
  25.5 0.0 collective-permute-done.4
  25.5 0.0 collective-permute-start.9
  25.5 0.0 collective-permute-done.5
  25.5 0.0 collective-permute-done.6
  25.6 0.0 copy-done.1
  25.6 1.3 %shard_map.99.dens_ref = bf16[256,1024]{1,0:T(8,128)(2,1)S(1)} custom-call(bf16[4,32,512]{2,1,0:T(8,128)(2,1)S(1)} %pad_maximum_fusion.1.bands_ref, bf16[2048,1024]{1,0:T(8,128)(2,1)S(1)} %copy-done.1, bf16[256,512]{1,0:T(8,128)(2,1)S(1)} %get-tuple-element.18.refs_0_), custom_call_target="tpu_custom_call" | custom-call | flops 1073741824 | bytes 4194304 | tf_op jit(solution)/shard_map/pallas_call | solution.py:20
  26.9 0.7 %collective-permute-done.7.refs_1_ = bf16[256,256]{1,0:T(8,128)(2,1)S(1)} collective-permute-done((bf16[256,256]{1,0:T(8,128)(2,1)S(1)}, bf16[256,256]{1,0:T(8,128)(2,1)S(1)}, u32[]{:S(2)}, u32[]{:S(2)}) %collective-permute-start.7) | collective-permute-done | bytes 131104 | tf_op jit(solution)/shard_map/ppermute | solution.py:32
  27.6 7.4 %collective-permute-done.8.refs_2_ = bf16[256,256]{1,0:T(8,128)(2,1)S(1)} collective-permute-done((bf16[256,256]{1,0:T(8,128)(2,1)S(1)}, bf16[256,256]{1,0:T(8,128)(2,1)S(1)}, u32[]{:S(2)}, u32[]{:S(2)}) %collective-permute-start.8) | collective-permute-done | bytes 131104 | tf_op jit(solution)/shard_map/ppermute | solution.py:32
  35.0 0.0 collective-permute-done.9.refs_3_
  35.0 0.0 copy-done.3
  35.0 0.6 %shard_map.100 = (f32[64,512]{1,0:T(8,128)S(1)}, bf16[64,512]{1,0:T(8,128)(2,1)S(1)}, bf16[64,512]{1,0:T(8,128)(2,1)S(1)}, bf16[64,512]{1,0:T(8,128)(2,1)S(1)}) custom-call(bf16[256,1024]{1,0:T(8,128)(2,1)S(1)} %shard_map.99.dens_ref, bf16[256,512]{1,0:T(8,128)(2,1)S(1)} %copy-done.3, bf16[256,256]{1,0:T(8,128)(2,1)S(1)} %get-tuple-element.26.refs_0_, ...), custom_call_target="tpu_custom_call" | custom-call | flops 201326592 | bytes 524288 | tf_op jit(solution)/shard_map/pallas_call | solution.py:20
  35.7 1.6 %collective-permute-start.10 = (bf16[64,512]{1,0:T(8,128)(2,1)S(1)}, bf16[64,512]{1,0:T(8,128)(2,1)S(1)}, u32[]{:S(2)}, u32[]{:S(2)}) collective-permute-start(bf16[64,512]{1,0:T(8,128)(2,1)S(1)} %get-tuple-element.20), channel_id=1, source_target_pairs={{0,1},{1,0},{2,3},{3,2},{4,5},{5,4},{6,7},{7,6},{8,9},{9,8},{10,11... | collective-permute-start | bytes 196616 | tf_op jit(solution)/shard_map/ppermute | solution.py:32
  37.2 1.5 %collective-permute-start.11 = (bf16[64,512]{1,0:T(8,128)(2,1)S(1)}, bf16[64,512]{1,0:T(8,128)(2,1)S(1)}, u32[]{:S(2)}, u32[]{:S(2)}) collective-permute-start(bf16[64,512]{1,0:T(8,128)(2,1)S(1)} %get-tuple-element.21), channel_id=1, source_target_pairs={{0,2},{1,3},{2,0},{3,1},{4,6},{5,7},{6,4},{7,5},{8,10},{9,11},{10,... | collective-permute-start | bytes 196616 | tf_op jit(solution)/shard_map/ppermute | solution.py:32
  38.7 0.5 %collective-permute-start.12 = (bf16[64,512]{1,0:T(8,128)(2,1)S(1)}, bf16[64,512]{1,0:T(8,128)(2,1)S(1)}, u32[]{:S(2)}, u32[]{:S(2)}) collective-permute-start(bf16[64,512]{1,0:T(8,128)(2,1)S(1)} %get-tuple-element.22), channel_id=1, source_target_pairs={{0,3},{1,2},{2,1},{3,0},{4,7},{5,6},{6,5},{7,4},{8,11},{9,10},{10,... | collective-permute-start | bytes 196616 | tf_op jit(solution)/shard_map/ppermute | solution.py:32
  39.2 0.8 %collective-permute-done.10 = bf16[64,512]{1,0:T(8,128)(2,1)S(1)} collective-permute-done((bf16[64,512]{1,0:T(8,128)(2,1)S(1)}, bf16[64,512]{1,0:T(8,128)(2,1)S(1)}, u32[]{:S(2)}, u32[]{:S(2)}) %collective-permute-start.10) | collective-permute-done | bytes 65568 | tf_op jit(solution)/shard_map/ppermute | solution.py:32
  40.0 1.5 %collective-permute-done.11 = bf16[64,512]{1,0:T(8,128)(2,1)S(1)} collective-permute-done((bf16[64,512]{1,0:T(8,128)(2,1)S(1)}, bf16[64,512]{1,0:T(8,128)(2,1)S(1)}, u32[]{:S(2)}, u32[]{:S(2)}) %collective-permute-start.11) | collective-permute-done | bytes 65568 | tf_op jit(solution)/shard_map/ppermute | solution.py:32
  41.5 2.4 %collective-permute-done.12 = bf16[64,512]{1,0:T(8,128)(2,1)S(1)} collective-permute-done((bf16[64,512]{1,0:T(8,128)(2,1)S(1)}, bf16[64,512]{1,0:T(8,128)(2,1)S(1)}, u32[]{:S(2)}, u32[]{:S(2)}) %collective-permute-start.12) | collective-permute-done | bytes 65568 | tf_op jit(solution)/shard_map/ppermute | solution.py:32
  43.9 0.7 %convert_add_fusion = f32[64,512]{1,0:T(8,128)} fusion(bf16[64,512]{1,0:T(8,128)(2,1)S(1)} %collective-permute-done.12, bf16[64,512]{1,0:T(8,128)(2,1)S(1)} %collective-permute-done.11, f32[64,512]{1,0:T(8,128)S(1)} %get-tuple-element.19, bf16[64,512]{1,0:T(8,128)(2,1)S(1)} %collective-permute-done.10), kind=kLoop, calls=%fused_computation.18 | loop fusion | flops 196608 | bytes 458752 | tf_op jit(solution)/shard_map/add | solution.py:268
  (6 shorter events, 0.1 us)
Async XLA Ops:
  0.0 5.6 %collective-permute-start = (bf16[1,64,256]{2,1,0:T(8,128)(2,1)}, bf16[1,64,256]{2,1,0:T(8,128)(2,1)S(1)}, u32[]{:S(2)}, u32[]{:S(2)}) collective-permute-start(bf16[1,64,256]{2,1,0:T(8,128)(2,1)} %waves_ref.1), channel_id=1, source_target_pairs={{0,8},{4,12},{8,0},{12,4},{16,24},{20,28},{24,16},{28,20},{1,9},{5... | collective-permute-start | bytes 98312 | tf_op jit(solution)/shard_map/ppermute | solution.py:32
  4.4 0.8 %copy-start.5 = (bf16[1,64,256]{2,1,0:T(8,128)(2,1)S(1)}, bf16[1,64,256]{2,1,0:T(8,128)(2,1)}, u32[]{:S(2)}) copy-start(bf16[1,64,256]{2,1,0:T(8,128)(2,1)} %waves_ref.1) | copy-start | bytes 98308
  5.1 3.3 %copy-start.6 = (s32[8,1]{0,1:T(1,128)S(1)}, s32[8,1]{0,1:T(1,128)}, u32[]{:S(2)}) copy-start(s32[8,1]{0,1:T(1,128)} %param.16) | copy-start | bytes 100
  5.1 5.6 %copy-start.7 = (s32[8]{0:T(128)S(1)}, s32[8]{0:T(128)}, u32[]{:S(2)}) copy-start(s32[8]{0:T(128)} %param.15) | copy-start | bytes 100
  5.8 4.8 %collective-permute-start.1 = (bf16[2,32,256]{2,1,0:T(8,128)(2,1)S(1)}, bf16[2,32,256]{2,1,0:T(8,128)(2,1)S(1)}, u32[]{:S(2)}, u32[]{:S(2)}) collective-permute-start(bf16[2,32,256]{2,1,0:T(8,128)(2,1)S(1)} %shard_map.92.bands_ref), channel_id=1, source_target_pairs={{0,16},{4,20},{8,24},{12,28},{16,0},{20,4},{24,8},{28,12},{1,17},{... | collective-permute-start | bytes 98312 | tf_op jit(solution)/shard_map/ppermute | solution.py:32
  10.7 3.4 %collective-permute-start.2 = (bf16[4,32,256]{2,1,0:T(8,128)(2,1)S(1)}, bf16[4,32,256]{2,1,0:T(8,128)(2,1)S(1)}, u32[]{:S(2)}, u32[]{:S(2)}) collective-permute-start(bf16[4,32,256]{2,1,0:T(8,128)(2,1)S(1)} %pad_maximum_fusion.2.bands_ref), channel_id=1, source_target_pairs={{0,4},{4,0},{8,12},{12,8},{16,20},{20,16},{24,28},{28,24},{1,5},{5... | collective-permute-start | bytes 196616 | tf_op jit(solution)/shard_map/ppermute | solution.py:32
  10.9 2.2 %copy-start = (bf16[2048,1024]{1,0:T(8,128)(2,1)S(1)}, bf16[2048,1024]{1,0:T(8,128)(2,1)}, u32[]{:S(2)}) copy-start(bf16[2048,1024]{1,0:T(8,128)(2,1)} %table_ref.7) | copy-start | bytes 12582916
  14.0 1.6 %copy-start.2 = (bf16[8,128,1024]{2,1,0:T(8,128)(2,1)S(1)}, bf16[8,128,1024]{2,1,0:T(8,128)(2,1)}, u32[]{:S(2)}) copy-start(bf16[8,128,1024]{2,1,0:T(8,128)(2,1)} %screened_ref.3) | copy-start | bytes 6291460
  14.0 2.6 %copy-start.4 = (bf16[1,64,512]{2,1,0:T(8,128)(2,1)S(1)}, bf16[1,64,512]{2,1,0:T(8,128)(2,1)}, u32[]{:S(2)}) copy-start(bf16[1,64,512]{2,1,0:T(8,128)(2,1)} %waves_ref.2) | copy-start | bytes 196612
  16.1 4.9 %collective-permute-start.3 = (bf16[4,128,256]{2,1,0:T(8,128)(2,1)S(1)}, bf16[4,128,256]{2,1,0:T(8,128)(2,1)S(1)}, u32[]{:S(2)}, u32[]{:S(2)}) collective-permute-start(bf16[4,128,256]{2,1,0:T(8,128)(2,1)S(1)} %shard_map.97), channel_id=1, source_target_pairs={{0,4},{4,0},{8,12},{12,8},{16,20},{20,16},{24,28},{28,24},{1,5},{5... | collective-permute-start | bytes 786440 | tf_op jit(solution)/shard_map/ppermute | solution.py:32
  16.9 8.6 %copy-start.1 = (bf16[2048,1024]{1,0:T(8,128)(2,1)S(1)}, bf16[2048,1024]{1,0:T(8,128)(2,1)}, u32[]{:S(2)}) copy-start(bf16[2048,1024]{1,0:T(8,128)(2,1)} %table_ref.7) | copy-start | bytes 12582916
  16.9 18.1 %copy-start.3 = (bf16[256,512]{1,0:T(8,128)(2,1)S(1)}, bf16[256,512]{1,0:T(8,128)(2,1)}, u32[]{:S(2)}) copy-start(bf16[256,512]{1,0:T(8,128)(2,1)} %trial_ref.1) | copy-start | bytes 786436
  17.0 8.6 %collective-permute-start.4 = (bf16[1,32,512]{2,1,0:T(8,128)(2,1)S(1)}, bf16[1,32,512]{2,1,0:T(8,128)(2,1)S(1)}, u32[]{:S(2)}, u32[]{:S(2)}) collective-permute-start(bf16[1,32,512]{2,1,0:T(8,128)(2,1)S(1)} %get-tuple-element.17), channel_id=1, source_target_pairs={{0,1},{1,0},{2,3},{3,2},{4,5},{5,4},{6,7},{7,6},{8,9},{9,8},{10,11... | collective-permute-start | bytes 98312 | tf_op jit(solution)/shard_map/ppermute | solution.py:32
  18.5 7.0 %collective-permute-start.5 = (bf16[1,32,512]{2,1,0:T(8,128)(2,1)S(1)}, bf16[1,32,512]{2,1,0:T(8,128)(2,1)S(1)}, u32[]{:S(2)}, u32[]{:S(2)}) collective-permute-start(bf16[1,32,512]{2,1,0:T(8,128)(2,1)S(1)} %get-tuple-element.17), channel_id=1, source_target_pairs={{0,2},{1,3},{2,0},{3,1},{4,6},{5,7},{6,4},{7,5},{8,10},{9,11},{10,... | collective-permute-start | bytes 98312 | tf_op jit(solution)/shard_map/ppermute | solution.py:32
  20.0 5.5 %collective-permute-start.6 = (bf16[1,32,512]{2,1,0:T(8,128)(2,1)S(1)}, bf16[1,32,512]{2,1,0:T(8,128)(2,1)S(1)}, u32[]{:S(2)}, u32[]{:S(2)}) collective-permute-start(bf16[1,32,512]{2,1,0:T(8,128)(2,1)S(1)} %get-tuple-element.17), channel_id=1, source_target_pairs={{0,3},{1,2},{2,1},{3,0},{4,7},{5,6},{6,5},{7,4},{8,11},{9,10},{10,... | collective-permute-start | bytes 98312 | tf_op jit(solution)/shard_map/ppermute | solution.py:32
  21.1 6.5 %collective-permute-start.7 = (bf16[256,256]{1,0:T(8,128)(2,1)S(1)}, bf16[256,256]{1,0:T(8,128)(2,1)S(1)}, u32[]{:S(2)}, u32[]{:S(2)}) collective-permute-start(bf16[256,256]{1,0:T(8,128)(2,1)S(1)} %get-tuple-element.24), channel_id=1, source_target_pairs={{0,8},{4,12},{8,0},{12,4},{16,24},{20,28},{24,16},{28,20},{1,9},{5... | collective-permute-start | bytes 393224 | tf_op jit(solution)/shard_map/ppermute | solution.py:32
  22.7 12.4 %collective-permute-start.8 = (bf16[256,256]{1,0:T(8,128)(2,1)S(1)}, bf16[256,256]{1,0:T(8,128)(2,1)S(1)}, u32[]{:S(2)}, u32[]{:S(2)}) collective-permute-start(bf16[256,256]{1,0:T(8,128)(2,1)S(1)} %get-tuple-element.25), channel_id=1, source_target_pairs={{0,16},{4,20},{8,24},{12,28},{16,0},{20,4},{24,8},{28,12},{1,17},{... | collective-permute-start | bytes 393224 | tf_op jit(solution)/shard_map/ppermute | solution.py:32
  25.5 9.5 %collective-permute-start.9 = (bf16[256,256]{1,0:T(8,128)(2,1)S(1)}, bf16[256,256]{1,0:T(8,128)(2,1)S(1)}, u32[]{:S(2)}, u32[]{:S(2)}) collective-permute-start(bf16[256,256]{1,0:T(8,128)(2,1)S(1)} %get-tuple-element.23), channel_id=1, source_target_pairs={{0,24},{4,28},{8,16},{12,20},{16,8},{20,12},{24,0},{28,4},{1,25},{... | collective-permute-start | bytes 393224 | tf_op jit(solution)/shard_map/ppermute | solution.py:32
  35.7 4.3 %collective-permute-start.10 = (bf16[64,512]{1,0:T(8,128)(2,1)S(1)}, bf16[64,512]{1,0:T(8,128)(2,1)S(1)}, u32[]{:S(2)}, u32[]{:S(2)}) collective-permute-start(bf16[64,512]{1,0:T(8,128)(2,1)S(1)} %get-tuple-element.20), channel_id=1, source_target_pairs={{0,1},{1,0},{2,3},{3,2},{4,5},{5,4},{6,7},{7,6},{8,9},{9,8},{10,11... | collective-permute-start | bytes 196616 | tf_op jit(solution)/shard_map/ppermute | solution.py:32
  37.2 4.3 %collective-permute-start.11 = (bf16[64,512]{1,0:T(8,128)(2,1)S(1)}, bf16[64,512]{1,0:T(8,128)(2,1)S(1)}, u32[]{:S(2)}, u32[]{:S(2)}) collective-permute-start(bf16[64,512]{1,0:T(8,128)(2,1)S(1)} %get-tuple-element.21), channel_id=1, source_target_pairs={{0,2},{1,3},{2,0},{3,1},{4,6},{5,7},{6,4},{7,5},{8,10},{9,11},{10,... | collective-permute-start | bytes 196616 | tf_op jit(solution)/shard_map/ppermute | solution.py:32
  38.7 5.2 %collective-permute-start.12 = (bf16[64,512]{1,0:T(8,128)(2,1)S(1)}, bf16[64,512]{1,0:T(8,128)(2,1)S(1)}, u32[]{:S(2)}, u32[]{:S(2)}) collective-permute-start(bf16[64,512]{1,0:T(8,128)(2,1)S(1)} %get-tuple-element.22), channel_id=1, source_target_pairs={{0,3},{1,2},{2,1},{3,0},{4,7},{5,6},{6,5},{7,4},{8,11},{9,10},{10,... | collective-permute-start | bytes 196616 | tf_op jit(solution)/shard_map/ppermute | solution.py:32

commit v5 on v4

--- a/solution.py
+++ b/solution.py
@@ -128,20 +128,20 @@
     )
 
 
-def weighted_kernel(flip, slots_ref, screened_ref, dens_ref, out_ref, rows_ref):
-    chips, share, waves = rows_ref.shape
+def weighted_kernel(picks, slots_ref, screened_ref, dens_ref, out_ref, rows_ref):
+    count, share, waves = rows_ref.shape
     slots = slots_ref[...]
-    for s in range(chips):
-        rows_ref[s] = screened_ref[slots[0, flip * chips + s]]
+    for s, pick in enumerate(picks):
+        rows_ref[s] = screened_ref[slots[0, pick]]
     out_ref[...] = (
         lax.dot_general(
-            rows_ref[...].reshape(chips * share, waves),
+            rows_ref[...].reshape(count * share, waves),
             dens_ref[...],
             (((1,), (1,)), ((), ())),
             preferred_element_type=jnp.float32,
         )
         .astype(jnp.bfloat16)
-        .reshape(chips, share, NP)
+        .reshape(count, share, NP)
     )
 
 
@@ -196,7 +196,7 @@
     order = lax.axis_index("row") ^ jnp.concatenate([every[::2], every[1::2]])
     transfers = jnp.sum(jnp.where(order[:, None] == every, transfer_table[:, 0], 0), axis=1)
     slots = jnp.sum(jnp.where(transfers[:, None] == every, owner_slot, 0), axis=1)[None]
-    early = (slots,)
+    early = (slots, screened)
 
     half, step = None, 4
     while step < rows:
@@ -226,26 +226,33 @@
     )
     dens_col = density(across, other, plane_wave, addend=half)
 
-    def weighted(flip):
+    def weighted(picks):
+        count = len(picks)
         return call(
-            functools.partial(weighted_kernel, flip),
-            jax.ShapeDtypeStruct((chips, share, NP), jnp.bfloat16),
+            functools.partial(weighted_kernel, picks),
+            jax.ShapeDtypeStruct((count, share, NP), jnp.bfloat16),
             slots,
             screened,
             dens_col,
             spaces=[VMEM] * 3,
-            scratch=[pltpu.VMEM((chips, share, waves), jnp.bfloat16)],
-            flops=2 * chips * share * waves * NP,
-            moved=2 * chips * share * waves,
+            scratch=[pltpu.VMEM((count, share, waves), jnp.bfloat16)],
+            flops=2 * count * share * waves * NP,
+            moved=2 * count * share * waves,
         )
 
-    give, keep = weighted(1), weighted(0)
+    far = chips // 2
+    rest = [s for s in range(chips) if s != far]
+    first = weighted((far, chips + far)).reshape(2 * share, NP)
+    first = swap(first, "row", 2 * far)
+    give = weighted([chips + s for s in rest])
+    keep = weighted(rest)
     both = jnp.concatenate([keep, swap(give, "row", 1)], axis=1)
-    pieces = [both[0]] + [None] * (chips - 1)
-    for s in [*range(2, chips), 1]:
-        pieces[s] = swap(both[s], "row", 2 * s)
-
-    late_waves, _ = lax.optimization_barrier((waves_row, both))
+    pieces = [None] * chips
+    for index, s in enumerate(rest):
+        pieces[s] = swap(both[index], "row", 2 * s) if s else both[index]
+    pieces[far] = jnp.concatenate([first[:share], swap(first[share:], "row", 1)])
+
+    late_waves, _ = lax.optimization_barrier((waves_row, give))
     bands_row, own_row = windowed(1, starts, late_waves)
     row_bands = jnp.concatenate([bands_row] + [swap(bands_row, "col", s) for s in range(1, cols)])
     dens_row = density(column, row_bands, plane_wave, own_row)

time: 44.9 us -> 49.7 us (1.11)
  waiting for transfers between devices: 14.9 us -> 19 us
  starting transfers between devices: 17.8 us -> 19.2 us
  local copies, waits for them, and re-layouts: 3.99 us -> 3.18 us
    ppermute x13 -> x14, waiting for transfers between devices: 14.9 us -> 19 us  [swap(): lax.ppermute(x, axis, [(i, i ^ step) for i in range(lax.axis_size(axis))])]
    ppermute x13 -> x14, starting transfers between devices: 17.8 us -> 19.2 us  [swap(): lax.ppermute(x, axis, [(i, i ^ step) for i in range(lax.axis_size(axis))])]
    unnamed x16, local copies, waits for them, and re-layouts: 3.79 us -> 2.97 us
    pallas_call x10 -> x11, Pallas kernels: 5.15 us -> 5.36 us  [call(): pl.pallas_call(kernel, out_shape=outs, in_specs=spaces, out_specs=jax.tre...]
  transfers between devices with their start and end apart: 13 -> 14, of which waited for: 6 -> 8; matrix products, arithmetic and copies ran while one was open for 2% -> 1% of each run, Pallas kernels for 7% -> 6%
where the time goes in v5:
time: 49.7 us; the launch traced here: 49.5 us
  starting transfers between devices  19.2 us (39%)
  waiting for transfers between devices  19 us (38%)
  Pallas kernels  5.36 us (11%)
  local copies, waits for them, and re-layouts  3.18 us (6%)
  between operations  1.55 us (3%)
  other arithmetic  1.2 us (2%)
    ppermute x14, starting transfers between devices, swap(): lax.ppermute(x, axis, [(i, i ^ step) for i in range(lax.axis_size(axis))])  19.2 us
    ppermute x14, waiting for transfers between devices, swap(): lax.ppermute(x, axis, [(i, i ^ step) for i in range(lax.axis_size(axis))])  19 us
    pallas_call x11, Pallas kernels, call(): pl.pallas_call(kernel, out_shape=outs, in_specs=spaces, out_specs=jax.tre...  5.36 us
    unnamed x16, local copies, waits for them, and re-layouts  2.97 us
  transfers between devices with their start and end apart: 14, of which 8 were waited for; matrix products, arithmetic and copies ran while one was open for 1% of the time, Pallas kernels for 6%

profile of v5, /device:TPU:0, one launch (start us, length us, event | category | flops | bytes accessed | tf_op | source)
XLA Modules:
  0.0 49.5 jit_solution(6238921883602924956)
XLA Ops:
  0.0 3.1 %collective-permute-start = (bf16[1,64,256]{2,1,0:T(8,128)(2,1)}, bf16[1,64,256]{2,1,0:T(8,128)(2,1)S(1)}, u32[]{:S(2)}, u32[]{:S(2)}) collective-permute-start(bf16[1,64,256]{2,1,0:T(8,128)(2,1)} %waves_ref.1), channel_id=1, source_target_pairs={{0,8},{4,12},{8,0},{12,4},{16,24},{20,28},{24,16},{28,20},{1,9},{5... | collective-permute-start | bytes 98312 | tf_op jit(solution)/shard_map/ppermute | solution.py:32
  4.4 0.0 copy-start.5
  4.4 0.7 %copy-done.5 = bf16[1,64,256]{2,1,0:T(8,128)(2,1)S(1)} copy-done((bf16[1,64,256]{2,1,0:T(8,128)(2,1)S(1)}, bf16[1,64,256]{2,1,0:T(8,128)(2,1)}, u32[]{:S(2)}) %copy-start.5) | copy-done | bytes 32792
  5.1 0.0 copy-start.6
  5.1 0.0 copy-start.7
  5.1 0.0 copy-start.2
  5.1 0.2 shard_map.91
  5.4 0.1 slice.21
  5.5 0.1 slice.22
  5.6 0.1 add_xor_fusion
  5.6 0.0 collective-permute-done.waves_ref
  5.6 0.2 shard_map.92.bands_ref
  5.8 2.6 %collective-permute-start.1 = (bf16[2,32,256]{2,1,0:T(8,128)(2,1)S(1)}, bf16[2,32,256]{2,1,0:T(8,128)(2,1)S(1)}, u32[]{:S(2)}, u32[]{:S(2)}) collective-permute-start(bf16[2,32,256]{2,1,0:T(8,128)(2,1)S(1)} %shard_map.92.bands_ref), channel_id=1, source_target_pairs={{0,16},{4,20},{8,24},{12,28},{16,0},{20,4},{24,8},{28,12},{1,17},{... | collective-permute-start | bytes 98312 | tf_op jit(solution)/shard_map/ppermute | solution.py:32
  8.4 0.0 copy-done.6
  8.4 0.2 select_reduce_fusion.1
  8.6 2.0 %collective-permute-done.1 = bf16[2,32,256]{2,1,0:T(8,128)(2,1)S(1)} collective-permute-done((bf16[2,32,256]{2,1,0:T(8,128)(2,1)S(1)}, bf16[2,32,256]{2,1,0:T(8,128)(2,1)S(1)}, u32[]{:S(2)}, u32[]{:S(2)}) %collective-permute-start.1) | collective-permute-done | bytes 32800 | tf_op jit(solution)/shard_map/ppermute | solution.py:32
  10.7 0.1 collective-permute-start.2
  10.7 0.0 copy-done.7
  10.7 0.2 select_reduce_fusion
  10.9 0.0 copy-start
  10.9 2.2 %copy-done = bf16[2048,1024]{1,0:T(8,128)(2,1)S(1)} copy-done((bf16[2048,1024]{1,0:T(8,128)(2,1)S(1)}, bf16[2048,1024]{1,0:T(8,128)(2,1)}, u32[]{:S(2)}) %copy-start) | copy-done | bytes 4194328
  13.1 0.4 shard_map.93.refs_0_
  13.6 0.0 copy-done.2
  13.6 0.5 shard_map.94.refs_0_
  14.0 0.0 copy-start.4
  14.0 0.0 collective-permute-done.2.bands_ref
  14.1 0.7 %shard_map.95.dens_ref = bf16[256,1024]{1,0:T(8,128)(2,1)S(1)} custom-call(bf16[4,32,256]{2,1,0:T(8,128)(2,1)S(1)} %collective-permute-done.2.bands_ref, bf16[2048,1024]{1,0:T(8,128)(2,1)S(1)} %copy-done, f32[256,1024]{1,0:T(8,128)S(1)} %shard_map.94.refs_0_), custom_call_target="tpu_custom_call" | custom-call | flops 536870912 | bytes 2097152 | tf_op jit(solution)/shard_map/pallas_call | solution.py:20
  14.8 0.4 shard_map.96
  15.3 0.0 copy-done.4
  15.3 0.2 shard_map.97
  15.5 0.0 copy-start.1
  15.5 1.5 %collective-permute-start.3 = (bf16[1,32,512]{2,1,0:T(8,128)(2,1)S(1)}, bf16[1,32,512]{2,1,0:T(8,128)(2,1)S(1)}, u32[]{:S(2)}, u32[]{:S(2)}) collective-permute-start(bf16[1,32,512]{2,1,0:T(8,128)(2,1)S(1)} %get-tuple-element.17), channel_id=1, source_target_pairs={{0,1},{1,0},{2,3},{3,2},{4,5},{5,4},{6,7},{7,6},{8,9},{9,8},{10,11... | collective-permute-start | bytes 98312 | tf_op jit(solution)/shard_map/ppermute | solution.py:32
  17.1 1.5 %collective-permute-start.4 = (bf16[1,32,512]{2,1,0:T(8,128)(2,1)S(1)}, bf16[1,32,512]{2,1,0:T(8,128)(2,1)S(1)}, u32[]{:S(2)}, u32[]{:S(2)}) collective-permute-start(bf16[1,32,512]{2,1,0:T(8,128)(2,1)S(1)} %get-tuple-element.17), channel_id=1, source_target_pairs={{0,2},{1,3},{2,0},{3,1},{4,6},{5,7},{6,4},{7,5},{8,10},{9,11},{10,... | collective-permute-start | bytes 98312 | tf_op jit(solution)/shard_map/ppermute | solution.py:32
  18.6 0.5 collective-permute-start.5
  19.1 0.0 collective-permute-start.6
  19.1 0.4 shard_map.100
  19.5 0.0 copy-start.3
  19.5 2.7 %collective-permute-start.8 = (bf16[256,256]{1,0:T(8,128)(2,1)S(1)}, bf16[256,256]{1,0:T(8,128)(2,1)S(1)}, u32[]{:S(2)}, u32[]{:S(2)}) collective-permute-start(bf16[256,256]{1,0:T(8,128)(2,1)S(1)} %bitcast.13), channel_id=1, source_target_pairs={{0,16},{4,20},{8,24},{12,28},{16,0},{20,4},{24,8},{28,12},{1,17},{... | collective-permute-start | bytes 393224 | tf_op jit(solution)/shard_map/ppermute | solution.py:32
  22.1 0.4 shard_map.99
  22.6 0.0 collective-permute-done.3
  22.6 0.0 collective-permute-done.4
  22.6 0.8 %collective-permute-done.5 = bf16[1,32,512]{2,1,0:T(8,128)(2,1)S(1)} collective-permute-done((bf16[1,32,512]{2,1,0:T(8,128)(2,1)S(1)}, bf16[1,32,512]{2,1,0:T(8,128)(2,1)S(1)}, u32[]{:S(2)}, u32[]{:S(2)}) %collective-permute-start.5) | collective-permute-done | bytes 32800 | tf_op jit(solution)/shard_map/ppermute | solution.py:32
  23.4 5.7 %collective-permute-done.8 = bf16[256,256]{1,0:T(8,128)(2,1)S(1)} collective-permute-done((bf16[256,256]{1,0:T(8,128)(2,1)S(1)}, bf16[256,256]{1,0:T(8,128)(2,1)S(1)}, u32[]{:S(2)}, u32[]{:S(2)}) %collective-permute-start.8) | collective-permute-done | bytes 131104 | tf_op jit(solution)/shard_map/ppermute | solution.py:32
  29.2 0.1 collective-permute-start.9
  29.2 0.0 collective-permute-done.6
  29.3 3.6 %collective-permute-start.10 = (bf16[256,256]{1,0:T(8,128)(2,1)S(1)}, bf16[256,256]{1,0:T(8,128)(2,1)S(1)}, u32[]{:S(2)}, u32[]{:S(2)}) collective-permute-start(bf16[256,256]{1,0:T(8,128)(2,1)S(1)} %get-tuple-element.23), channel_id=1, source_target_pairs={{0,24},{4,28},{8,16},{12,20},{16,8},{20,12},{24,0},{28,4},{1,25},{... | collective-permute-start | bytes 393224 | tf_op jit(solution)/shard_map/ppermute | solution.py:32
  32.9 0.0 collective-permute-start.7
  32.9 0.0 copy-done.1
  32.9 1.3 %shard_map.98.dens_ref = bf16[256,1024]{1,0:T(8,128)(2,1)S(1)} custom-call(bf16[4,32,512]{2,1,0:T(8,128)(2,1)S(1)} %pad_maximum_fusion.1.bands_ref, bf16[2048,1024]{1,0:T(8,128)(2,1)S(1)} %copy-done.1, bf16[256,512]{1,0:T(8,128)(2,1)S(1)} %get-tuple-element.18.refs_0_), custom_call_target="tpu_custom_call" | custom-call | flops 1073741824 | bytes 4194304 | tf_op jit(solution)/shard_map/pallas_call | solution.py:20
  34.2 0.0 collective-permute-done.9
  34.2 3.3 %collective-permute-done.10.refs_3_ = bf16[256,256]{1,0:T(8,128)(2,1)S(1)} collective-permute-done((bf16[256,256]{1,0:T(8,128)(2,1)S(1)}, bf16[256,256]{1,0:T(8,128)(2,1)S(1)}, u32[]{:S(2)}, u32[]{:S(2)}) %collective-permute-start.10) | collective-permute-done | bytes 131104 | tf_op jit(solution)/shard_map/ppermute | solution.py:32
  37.6 2.4 %collective-permute-done.7.refs_1_ = bf16[256,256]{1,0:T(8,128)(2,1)S(1)} collective-permute-done((bf16[256,256]{1,0:T(8,128)(2,1)S(1)}, bf16[256,256]{1,0:T(8,128)(2,1)S(1)}, u32[]{:S(2)}, u32[]{:S(2)}) %collective-permute-start.7) | collective-permute-done | bytes 131104 | tf_op jit(solution)/shard_map/ppermute | solution.py:32
  40.0 0.0 copy-done.3
  40.0 0.6 %shard_map.101 = (f32[64,512]{1,0:T(8,128)S(1)}, bf16[64,512]{1,0:T(8,128)(2,1)S(1)}, bf16[64,512]{1,0:T(8,128)(2,1)S(1)}, bf16[64,512]{1,0:T(8,128)(2,1)S(1)}) custom-call(bf16[256,1024]{1,0:T(8,128)(2,1)S(1)} %shard_map.98.dens_ref, bf16[256,512]{1,0:T(8,128)(2,1)S(1)} %copy-done.3, bf16[256,256]{1,0:T(8,128)(2,1)S(1)} %get-tuple-element.24.refs_0_, ...), custom_call_target="tpu_custom_call" | custom-call | flops 201326592 | bytes 524288 | tf_op jit(solution)/shard_map/pallas_call | solution.py:20
  40.6 1.5 %collective-permute-start.11 = (bf16[64,512]{1,0:T(8,128)(2,1)S(1)}, bf16[64,512]{1,0:T(8,128)(2,1)S(1)}, u32[]{:S(2)}, u32[]{:S(2)}) collective-permute-start(bf16[64,512]{1,0:T(8,128)(2,1)S(1)} %get-tuple-element.20), channel_id=1, source_target_pairs={{0,1},{1,0},{2,3},{3,2},{4,5},{5,4},{6,7},{7,6},{8,9},{9,8},{10,11... | collective-permute-start | bytes 196616 | tf_op jit(solution)/shard_map/ppermute | solution.py:32
  42.1 1.5 %collective-permute-start.12 = (bf16[64,512]{1,0:T(8,128)(2,1)S(1)}, bf16[64,512]{1,0:T(8,128)(2,1)S(1)}, u32[]{:S(2)}, u32[]{:S(2)}) collective-permute-start(bf16[64,512]{1,0:T(8,128)(2,1)S(1)} %get-tuple-element.21), channel_id=1, source_target_pairs={{0,2},{1,3},{2,0},{3,1},{4,6},{5,7},{6,4},{7,5},{8,10},{9,11},{10,... | collective-permute-start | bytes 196616 | tf_op jit(solution)/shard_map/ppermute | solution.py:32
  43.7 0.5 collective-permute-start.13
  44.1 0.8 %collective-permute-done.11 = bf16[64,512]{1,0:T(8,128)(2,1)S(1)} collective-permute-done((bf16[64,512]{1,0:T(8,128)(2,1)S(1)}, bf16[64,512]{1,0:T(8,128)(2,1)S(1)}, u32[]{:S(2)}, u32[]{:S(2)}) %collective-permute-start.11) | collective-permute-done | bytes 65568 | tf_op jit(solution)/shard_map/ppermute | solution.py:32
  44.9 1.5 %collective-permute-done.12 = bf16[64,512]{1,0:T(8,128)(2,1)S(1)} collective-permute-done((bf16[64,512]{1,0:T(8,128)(2,1)S(1)}, bf16[64,512]{1,0:T(8,128)(2,1)S(1)}, u32[]{:S(2)}, u32[]{:S(2)}) %collective-permute-start.12) | collective-permute-done | bytes 65568 | tf_op jit(solution)/shard_map/ppermute | solution.py:32
  46.4 2.4 %collective-permute-done.13 = bf16[64,512]{1,0:T(8,128)(2,1)S(1)} collective-permute-done((bf16[64,512]{1,0:T(8,128)(2,1)S(1)}, bf16[64,512]{1,0:T(8,128)(2,1)S(1)}, u32[]{:S(2)}, u32[]{:S(2)}) %collective-permute-start.13) | collective-permute-done | bytes 65568 | tf_op jit(solution)/shard_map/ppermute | solution.py:32
  48.8 0.7 %convert_add_fusion = f32[64,512]{1,0:T(8,128)} fusion(bf16[64,512]{1,0:T(8,128)(2,1)S(1)} %collective-permute-done.13, bf16[64,512]{1,0:T(8,128)(2,1)S(1)} %collective-permute-done.12, f32[64,512]{1,0:T(8,128)S(1)} %get-tuple-element.19, bf16[64,512]{1,0:T(8,128)(2,1)S(1)} %collective-permute-done.11), kind=kLoop, calls=%fused_computation.12 | loop fusion | flops 196608 | bytes 458752 | tf_op jit(solution)/shard_map/add | solution.py:275
  (8 shorter events, 0.1 us)
Async XLA Ops:
  0.0 5.6 %collective-permute-start = (bf16[1,64,256]{2,1,0:T(8,128)(2,1)}, bf16[1,64,256]{2,1,0:T(8,128)(2,1)S(1)}, u32[]{:S(2)}, u32[]{:S(2)}) collective-permute-start(bf16[1,64,256]{2,1,0:T(8,128)(2,1)} %waves_ref.1), channel_id=1, source_target_pairs={{0,8},{4,12},{8,0},{12,4},{16,24},{20,28},{24,16},{28,20},{1,9},{5... | collective-permute-start | bytes 98312 | tf_op jit(solution)/shard_map/ppermute | solution.py:32
  4.4 0.8 %copy-start.5 = (bf16[1,64,256]{2,1,0:T(8,128)(2,1)S(1)}, bf16[1,64,256]{2,1,0:T(8,128)(2,1)}, u32[]{:S(2)}) copy-start(bf16[1,64,256]{2,1,0:T(8,128)(2,1)} %waves_ref.1) | copy-start | bytes 98308
  5.1 3.3 %copy-start.6 = (s32[8,1]{0,1:T(1,128)S(1)}, s32[8,1]{0,1:T(1,128)}, u32[]{:S(2)}) copy-start(s32[8,1]{0,1:T(1,128)} %param.16) | copy-start | bytes 100
  5.1 5.6 %copy-start.7 = (s32[8]{0:T(128)S(1)}, s32[8]{0:T(128)}, u32[]{:S(2)}) copy-start(s32[8]{0:T(128)} %param.15) | copy-start | bytes 100
  5.1 8.4 %copy-start.2 = (bf16[8,128,1024]{2,1,0:T(8,128)(2,1)S(1)}, bf16[8,128,1024]{2,1,0:T(8,128)(2,1)}, u32[]{:S(2)}) copy-start(bf16[8,128,1024]{2,1,0:T(8,128)(2,1)} %screened_ref.5) | copy-start | bytes 6291460
  5.8 4.8 %collective-permute-start.1 = (bf16[2,32,256]{2,1,0:T(8,128)(2,1)S(1)}, bf16[2,32,256]{2,1,0:T(8,128)(2,1)S(1)}, u32[]{:S(2)}, u32[]{:S(2)}) collective-permute-start(bf16[2,32,256]{2,1,0:T(8,128)(2,1)S(1)} %shard_map.92.bands_ref), channel_id=1, source_target_pairs={{0,16},{4,20},{8,24},{12,28},{16,0},{20,4},{24,8},{28,12},{1,17},{... | collective-permute-start | bytes 98312 | tf_op jit(solution)/shard_map/ppermute | solution.py:32
  10.7 3.4 %collective-permute-start.2 = (bf16[4,32,256]{2,1,0:T(8,128)(2,1)S(1)}, bf16[4,32,256]{2,1,0:T(8,128)(2,1)S(1)}, u32[]{:S(2)}, u32[]{:S(2)}) collective-permute-start(bf16[4,32,256]{2,1,0:T(8,128)(2,1)S(1)} %pad_maximum_fusion.3.bands_ref), channel_id=1, source_target_pairs={{0,4},{4,0},{8,12},{12,8},{16,20},{20,16},{24,28},{28,24},{1,5},{5... | collective-permute-start | bytes 196616 | tf_op jit(solution)/shard_map/ppermute | solution.py:32
  10.9 2.2 %copy-start = (bf16[2048,1024]{1,0:T(8,128)(2,1)S(1)}, bf16[2048,1024]{1,0:T(8,128)(2,1)}, u32[]{:S(2)}) copy-start(bf16[2048,1024]{1,0:T(8,128)(2,1)} %table_ref.7) | copy-start | bytes 12582916
  14.0 1.2 %copy-start.4 = (bf16[1,64,512]{2,1,0:T(8,128)(2,1)S(1)}, bf16[1,64,512]{2,1,0:T(8,128)(2,1)}, u32[]{:S(2)}) copy-start(bf16[1,64,512]{2,1,0:T(8,128)(2,1)} %waves_ref.2) | copy-start | bytes 196612
  15.5 17.4 %copy-start.1 = (bf16[2048,1024]{1,0:T(8,128)(2,1)S(1)}, bf16[2048,1024]{1,0:T(8,128)(2,1)}, u32[]{:S(2)}) copy-start(bf16[2048,1024]{1,0:T(8,128)(2,1)} %table_ref.7) | copy-start | bytes 12582916
  15.5 7.0 %collective-permute-start.3 = (bf16[1,32,512]{2,1,0:T(8,128)(2,1)S(1)}, bf16[1,32,512]{2,1,0:T(8,128)(2,1)S(1)}, u32[]{:S(2)}, u32[]{:S(2)}) collective-permute-start(bf16[1,32,512]{2,1,0:T(8,128)(2,1)S(1)} %get-tuple-element.17), channel_id=1, source_target_pairs={{0,1},{1,0},{2,3},{3,2},{4,5},{5,4},{6,7},{7,6},{8,9},{9,8},{10,11... | collective-permute-start | bytes 98312 | tf_op jit(solution)/shard_map/ppermute | solution.py:32
  17.1 5.5 %collective-permute-start.4 = (bf16[1,32,512]{2,1,0:T(8,128)(2,1)S(1)}, bf16[1,32,512]{2,1,0:T(8,128)(2,1)S(1)}, u32[]{:S(2)}, u32[]{:S(2)}) collective-permute-start(bf16[1,32,512]{2,1,0:T(8,128)(2,1)S(1)} %get-tuple-element.17), channel_id=1, source_target_pairs={{0,2},{1,3},{2,0},{3,1},{4,6},{5,7},{6,4},{7,5},{8,10},{9,11},{10,... | collective-permute-start | bytes 98312 | tf_op jit(solution)/shard_map/ppermute | solution.py:32
  18.6 4.8 %collective-permute-start.5 = (bf16[1,32,512]{2,1,0:T(8,128)(2,1)S(1)}, bf16[1,32,512]{2,1,0:T(8,128)(2,1)S(1)}, u32[]{:S(2)}, u32[]{:S(2)}) collective-permute-start(bf16[1,32,512]{2,1,0:T(8,128)(2,1)S(1)} %get-tuple-element.17), channel_id=1, source_target_pairs={{0,3},{1,2},{2,1},{3,0},{4,7},{5,6},{6,5},{7,4},{8,11},{9,10},{10,... | collective-permute-start | bytes 98312 | tf_op jit(solution)/shard_map/ppermute | solution.py:32
  19.1 10.2 %collective-permute-start.6 = (bf16[3,128,256]{2,1,0:T(8,128)(2,1)S(1)}, bf16[3,128,256]{2,1,0:T(8,128)(2,1)S(1)}, u32[]{:S(2)}, u32[]{:S(2)}) collective-permute-start(bf16[3,128,256]{2,1,0:T(8,128)(2,1)S(1)} %shard_map.96), channel_id=1, source_target_pairs={{0,4},{4,0},{8,12},{12,8},{16,20},{20,16},{24,28},{28,24},{1,5},{5... | collective-permute-start | bytes 589832 | tf_op jit(solution)/shard_map/ppermute | solution.py:32
  19.5 20.5 %copy-start.3 = (bf16[256,512]{1,0:T(8,128)(2,1)S(1)}, bf16[256,512]{1,0:T(8,128)(2,1)}, u32[]{:S(2)}) copy-start(bf16[256,512]{1,0:T(8,128)(2,1)} %trial_ref.1) | copy-start | bytes 786436
  19.5 9.7 %collective-permute-start.8 = (bf16[256,256]{1,0:T(8,128)(2,1)S(1)}, bf16[256,256]{1,0:T(8,128)(2,1)S(1)}, u32[]{:S(2)}, u32[]{:S(2)}) collective-permute-start(bf16[256,256]{1,0:T(8,128)(2,1)S(1)} %bitcast.13), channel_id=1, source_target_pairs={{0,16},{4,20},{8,24},{12,28},{16,0},{20,4},{24,8},{28,12},{1,17},{... | collective-permute-start | bytes 393224 | tf_op jit(solution)/shard_map/ppermute | solution.py:32
  29.2 5.0 %collective-permute-start.9 = (bf16[128,256]{1,0:T(8,128)(2,1)S(1)}, bf16[128,256]{1,0:T(8,128)(2,1)S(1)}, u32[]{:S(2)}, u32[]{:S(2)}) collective-permute-start(bf16[128,256]{1,0:T(8,128)(2,1)S(1)} %get-tuple-element.27), channel_id=1, source_target_pairs={{0,4},{4,0},{8,12},{12,8},{16,20},{20,16},{24,28},{28,24},{1,5},{5... | collective-permute-start | bytes 196616 | tf_op jit(solution)/shard_map/ppermute | solution.py:32
  29.3 8.3 %collective-permute-start.10 = (bf16[256,256]{1,0:T(8,128)(2,1)S(1)}, bf16[256,256]{1,0:T(8,128)(2,1)S(1)}, u32[]{:S(2)}, u32[]{:S(2)}) collective-permute-start(bf16[256,256]{1,0:T(8,128)(2,1)S(1)} %get-tuple-element.23), channel_id=1, source_target_pairs={{0,24},{4,28},{8,16},{12,20},{16,8},{20,12},{24,0},{28,4},{1,25},{... | collective-permute-start | bytes 393224 | tf_op jit(solution)/shard_map/ppermute | solution.py:32
  32.9 7.0 %collective-permute-start.7 = (bf16[256,256]{1,0:T(8,128)(2,1)S(1)}, bf16[256,256]{1,0:T(8,128)(2,1)S(1)}, u32[]{:S(2)}, u32[]{:S(2)}) collective-permute-start(bf16[256,256]{1,0:T(8,128)(2,1)S(1)} %get-tuple-element.25), channel_id=1, source_target_pairs={{0,8},{4,12},{8,0},{12,4},{16,24},{20,28},{24,16},{28,20},{1,9},{5... | collective-permute-start | bytes 393224 | tf_op jit(solution)/shard_map/ppermute | solution.py:32
  40.6 4.3 %collective-permute-start.11 = (bf16[64,512]{1,0:T(8,128)(2,1)S(1)}, bf16[64,512]{1,0:T(8,128)(2,1)S(1)}, u32[]{:S(2)}, u32[]{:S(2)}) collective-permute-start(bf16[64,512]{1,0:T(8,128)(2,1)S(1)} %get-tuple-element.20), channel_id=1, source_target_pairs={{0,1},{1,0},{2,3},{3,2},{4,5},{5,4},{6,7},{7,6},{8,9},{9,8},{10,11... | collective-permute-start | bytes 196616 | tf_op jit(solution)/shard_map/ppermute | solution.py:32
  42.1 4.3 %collective-permute-start.12 = (bf16[64,512]{1,0:T(8,128)(2,1)S(1)}, bf16[64,512]{1,0:T(8,128)(2,1)S(1)}, u32[]{:S(2)}, u32[]{:S(2)}) collective-permute-start(bf16[64,512]{1,0:T(8,128)(2,1)S(1)} %get-tuple-element.21), channel_id=1, source_target_pairs={{0,2},{1,3},{2,0},{3,1},{4,6},{5,7},{6,4},{7,5},{8,10},{9,11},{10,... | collective-permute-start | bytes 196616 | tf_op jit(solution)/shard_map/ppermute | solution.py:32
  43.7 5.2 %collective-permute-start.13 = (bf16[64,512]{1,0:T(8,128)(2,1)S(1)}, bf16[64,512]{1,0:T(8,128)(2,1)S(1)}, u32[]{:S(2)}, u32[]{:S(2)}) collective-permute-start(bf16[64,512]{1,0:T(8,128)(2,1)S(1)} %get-tuple-element.22), channel_id=1, source_target_pairs={{0,3},{1,2},{2,1},{3,0},{4,7},{5,6},{6,5},{7,4},{8,11},{9,10},{10,... | collective-permute-start | bytes 196616 | tf_op jit(solution)/shard_map/ppermute | solution.py:32

commit v6 on v5

--- a/solution.py
+++ b/solution.py
@@ -198,33 +198,28 @@
     slots = jnp.sum(jnp.where(transfers[:, None] == every, owner_slot, 0), axis=1)[None]
     early = (slots, screened)
 
-    half, step = None, 4
-    while step < rows:
-        done = step // 4 if step > 4 else 0
-        more = {} if half is None else {"addend": half}
-        half = density(
-            near,
-            bands,
-            plane_wave,
-            final=False,
-            todo=range(done, step // 2),
-            ready=own if half is None else None,
-            **more,
-        )
+    half, done, step = None, 0, 4
+    while True:
+        more = {"ready": own} if half is None else {"addend": half}
+        todo = range(done, step // 2)
+        half = density(near, bands, plane_wave, final=False, todo=todo, **more)
+        if 2 * step >= rows:
+            break
         bands = jnp.concatenate([bands, swap(bands, "row", step)])
-        step *= 2
+        done, step = step // 2, 2 * step
     other = swap(bands, "row", 1)
-    half = density(
-        near,
-        bands,
-        plane_wave,
-        final=False,
-        todo=range(chips // 2 if half is not None else 0, chips),
-        addend=half,
-        ready=own if half is None else None,
-        early=early,
-    )
-    dens_col = density(across, other, plane_wave, addend=half)
+    half = density(across, other, plane_wave, addend=half, final=False)
+    last = swap(bands, "row", step)
+    other = swap(last, "row", 1)
+
+    def near_last(s):
+        return near(s + chips // 2)
+
+    def across_last(s):
+        return across(s + chips // 2)
+
+    half = density(near_last, last, plane_wave, addend=half, final=False, early=early)
+    dens_col = density(across_last, other, plane_wave, addend=half)
 
     def weighted(picks):
         count = len(picks)
@@ -240,7 +235,7 @@
             moved=2 * count * share * waves,
         )
 
-    far = chips // 2
+    far = chips - 1
     rest = [s for s in range(chips) if s != far]
     first = weighted((far, chips + far)).reshape(2 * share, NP)
     first = swap(first, "row", 2 * far)
@@ -254,8 +249,13 @@
 
     late_waves, _ = lax.optimization_barrier((waves_row, give))
     bands_row, own_row = windowed(1, starts, late_waves)
-    row_bands = jnp.concatenate([bands_row] + [swap(bands_row, "col", s) for s in range(1, cols)])
-    dens_row = density(column, row_bands, plane_wave, own_row)
+    others = [swap(bands_row, "col", s) for s in range(1, cols)]
+
+    def other_column(s):
+        return column(s + 1)
+
+    half = density(column, bands_row, plane_wave, ready=own_row, final=False)
+    dens_row = density(other_column, jnp.concatenate(others), plane_wave, addend=half)
 
     vectors = trial.shape[1]
     kinds = [jnp.float32] + [jnp.bfloat16] * (cols - 1)

time: 49.7 us -> 45.7 us (0.920)
  waiting for transfers between devices: 19 us -> 15.9 us
  local copies, waits for them, and re-layouts: 3.18 us -> 1.34 us
  starting transfers between devices: 19.2 us -> 19.9 us
    ppermute x14 -> x15, waiting for transfers between devices: 19 us -> 15.9 us  [swap(): lax.ppermute(x, axis, [(i, i ^ step) for i in range(lax.axis_size(axis))])]
    unnamed x16 -> x14, local copies, waits for them, and re-layouts: 2.97 us -> 1.14 us
    ppermute x14 -> x15, starting transfers between devices: 19.2 us -> 19.9 us  [swap(): lax.ppermute(x, axis, [(i, i ^ step) for i in range(lax.axis_size(axis))])]
    pallas_call x11 -> x13, Pallas kernels: 5.36 us -> 5.71 us  [call(): pl.pallas_call(kernel, out_shape=outs, in_specs=spaces, out_specs=jax.tre...]
  transfers between devices with their start and end apart: 14 -> 15, of which waited for: 8 -> 8; matrix products, arithmetic and copies ran while one was open for 1% -> 2% of each run, Pallas kernels for 6% -> 8%
where the time goes in v6:
time: 45.7 us; the launch traced here: 45.5 us
  starting transfers between devices  19.9 us (44%)
  waiting for transfers between devices  15.9 us (35%)
  Pallas kernels  5.71 us (12%)
  between operations  1.52 us (3%)
  local copies, waits for them, and re-layouts  1.34 us (3%)
  other arithmetic  1.19 us (3%)
    ppermute x15, starting transfers between devices, swap(): lax.ppermute(x, axis, [(i, i ^ step) for i in range(lax.axis_size(axis))])  19.9 us
    ppermute x15, waiting for transfers between devices, swap(): lax.ppermute(x, axis, [(i, i ^ step) for i in range(lax.axis_size(axis))])  15.9 us
    pallas_call x13, Pallas kernels, call(): pl.pallas_call(kernel, out_shape=outs, in_specs=spaces, out_specs=jax.tre...  5.71 us
    unnamed x14, local copies, waits for them, and re-layouts  1.14 us
  transfers between devices with their start and end apart: 15, of which 8 were waited for; matrix products, arithmetic and copies ran while one was open for 2% of the time, Pallas kernels for 8%

profile of v6, /device:TPU:0, one launch (start us, length us, event | category | flops | bytes accessed | tf_op | source)
XLA Modules:
  0.0 45.5 jit_solution(3499866343556713346)
XLA Ops:
  0.0 3.1 %collective-permute-start = (bf16[1,64,256]{2,1,0:T(8,128)(2,1)}, bf16[1,64,256]{2,1,0:T(8,128)(2,1)S(1)}, u32[]{:S(2)}, u32[]{:S(2)}) collective-permute-start(bf16[1,64,256]{2,1,0:T(8,128)(2,1)} %waves_ref.1), channel_id=1, source_target_pairs={{0,8},{4,12},{8,0},{12,4},{16,24},{20,28},{24,16},{28,20},{1,9},{5... | collective-permute-start | bytes 98312 | tf_op jit(solution)/shard_map/ppermute | solution.py:32
  4.4 0.1 slice.22
  4.5 0.1 slice.21
  4.6 0.0 copy-start.4
  4.6 0.8 %copy-done.4 = bf16[1,64,256]{2,1,0:T(8,128)(2,1)S(1)} copy-done((bf16[1,64,256]{2,1,0:T(8,128)(2,1)S(1)}, bf16[1,64,256]{2,1,0:T(8,128)(2,1)}, u32[]{:S(2)}) %copy-start.4) | copy-done | bytes 32792
  5.3 0.0 copy-start.5
  5.3 0.0 copy-start.6
  5.3 0.0 copy-start
  5.3 0.2 shard_map.91
  5.5 0.1 add_xor_fusion
  5.6 0.3 copy-done.5
  6.0 0.2 select_reduce_fusion.1
  6.2 0.0 collective-permute-done.waves_ref
  6.2 0.2 shard_map.92.bands_ref
  6.3 0.0 collective-permute-start.3
  6.4 2.6 %collective-permute-start.1 = (bf16[2,32,256]{2,1,0:T(8,128)(2,1)S(1)}, bf16[2,32,256]{2,1,0:T(8,128)(2,1)S(1)}, u32[]{:S(2)}, u32[]{:S(2)}) collective-permute-start(bf16[2,32,256]{2,1,0:T(8,128)(2,1)S(1)} %shard_map.92.bands_ref), channel_id=1, source_target_pairs={{0,16},{4,20},{8,24},{12,28},{16,0},{20,4},{24,8},{28,12},{1,17},{... | collective-permute-start | bytes 98312 | tf_op jit(solution)/shard_map/ppermute | solution.py:32
  8.9 0.0 copy-done.6
  8.9 0.2 select_reduce_fusion
  9.1 0.0 copy-done
  9.1 0.4 shard_map.93.refs_0_
  9.6 0.0 copy-start.1
  9.6 2.3 %collective-permute-done.1.bands_ref = bf16[2,32,256]{2,1,0:T(8,128)(2,1)S(1)} collective-permute-done((bf16[2,32,256]{2,1,0:T(8,128)(2,1)S(1)}, bf16[2,32,256]{2,1,0:T(8,128)(2,1)S(1)}, u32[]{:S(2)}, u32[]{:S(2)}) %collective-permute-start.1) | collective-permute-done | bytes 32800 | tf_op jit(solution)/shard_map/ppermute | solution.py:32
  11.9 0.0 collective-permute-start.2
  11.9 0.0 collective-permute-done.3.bands_ref
  11.9 0.4 shard_map.94.refs_0_
  12.3 0.0 copy-done.1
  12.3 0.5 shard_map.95.refs_0_
  12.8 0.3 collective-permute-done.2.bands_ref
  13.1 0.4 shard_map.96.dens_ref
  13.5 0.0 copy-start.3
  13.5 0.4 shard_map.102
  13.9 0.4 shard_map.97
  14.4 0.3 collective-permute-start.7
  14.7 0.0 copy-done.3
  14.7 0.2 shard_map.98
  14.9 2.5 %collective-permute-start.6 = (bf16[1,32,512]{2,1,0:T(8,128)(2,1)S(1)}, bf16[1,32,512]{2,1,0:T(8,128)(2,1)S(1)}, u32[]{:S(2)}, u32[]{:S(2)}) collective-permute-start(bf16[1,32,512]{2,1,0:T(8,128)(2,1)S(1)} %get-tuple-element.17.bands_ref), channel_id=1, source_target_pairs={{0,3},{1,2},{2,1},{3,0},{4,7},{5,6},{6,5},{7,4},{8,11},{9,10},{10,... | collective-permute-start | bytes 98312 | tf_op jit(solution)/shard_map/ppermute | solution.py:32
  17.4 0.5 %collective-permute-start.5 = (bf16[1,32,512]{2,1,0:T(8,128)(2,1)S(1)}, bf16[1,32,512]{2,1,0:T(8,128)(2,1)S(1)}, u32[]{:S(2)}, u32[]{:S(2)}) collective-permute-start(bf16[1,32,512]{2,1,0:T(8,128)(2,1)S(1)} %get-tuple-element.17.bands_ref), channel_id=1, source_target_pairs={{0,2},{1,3},{2,0},{3,1},{4,6},{5,7},{6,4},{7,5},{8,10},{9,11},{10,... | collective-permute-start | bytes 98312 | tf_op jit(solution)/shard_map/ppermute | solution.py:32
  17.9 0.5 %collective-permute-start.4 = (bf16[1,32,512]{2,1,0:T(8,128)(2,1)S(1)}, bf16[1,32,512]{2,1,0:T(8,128)(2,1)S(1)}, u32[]{:S(2)}, u32[]{:S(2)}) collective-permute-start(bf16[1,32,512]{2,1,0:T(8,128)(2,1)S(1)} %get-tuple-element.17.bands_ref), channel_id=1, source_target_pairs={{0,1},{1,0},{2,3},{3,2},{4,5},{5,4},{6,7},{7,6},{8,9},{9,8},{10,11... | collective-permute-start | bytes 98312 | tf_op jit(solution)/shard_map/ppermute | solution.py:32
  18.5 3.0 %collective-permute-start.10 = (bf16[256,256]{1,0:T(8,128)(2,1)S(1)}, bf16[256,256]{1,0:T(8,128)(2,1)S(1)}, u32[]{:S(2)}, u32[]{:S(2)}) collective-permute-start(bf16[256,256]{1,0:T(8,128)(2,1)S(1)} %bitcast.13), channel_id=1, source_target_pairs={{0,24},{4,28},{8,16},{12,20},{16,8},{20,12},{24,0},{28,4},{1,25},{... | collective-permute-start | bytes 393224 | tf_op jit(solution)/shard_map/ppermute | solution.py:32
  21.5 0.4 shard_map.99.refs_0_
  21.9 0.4 shard_map.101
  22.4 0.0 copy-start.2
  22.4 0.0 collective-permute-done.6
  22.4 0.0 collective-permute-done.5
  22.4 0.0 collective-permute-done.4
  22.4 2.8 %collective-permute-done.10 = bf16[256,256]{1,0:T(8,128)(2,1)S(1)} collective-permute-done((bf16[256,256]{1,0:T(8,128)(2,1)S(1)}, bf16[256,256]{1,0:T(8,128)(2,1)S(1)}, u32[]{:S(2)}, u32[]{:S(2)}) %collective-permute-start.10) | collective-permute-done | bytes 131104 | tf_op jit(solution)/shard_map/ppermute | solution.py:32
  25.2 0.1 collective-permute-start.11
  25.3 0.0 collective-permute-done.7
  25.4 3.0 %collective-permute-start.9 = (bf16[256,256]{1,0:T(8,128)(2,1)S(1)}, bf16[256,256]{1,0:T(8,128)(2,1)S(1)}, u32[]{:S(2)}, u32[]{:S(2)}) collective-permute-start(bf16[256,256]{1,0:T(8,128)(2,1)S(1)} %get-tuple-element.23), channel_id=1, source_target_pairs={{0,16},{4,20},{8,24},{12,28},{16,0},{20,4},{24,8},{28,12},{1,17},{... | collective-permute-start | bytes 393224 | tf_op jit(solution)/shard_map/ppermute | solution.py:32
  28.4 0.7 %collective-permute-start.8 = (bf16[256,256]{1,0:T(8,128)(2,1)S(1)}, bf16[256,256]{1,0:T(8,128)(2,1)S(1)}, u32[]{:S(2)}, u32[]{:S(2)}) collective-permute-start(bf16[256,256]{1,0:T(8,128)(2,1)S(1)} %get-tuple-element.25), channel_id=1, source_target_pairs={{0,8},{4,12},{8,0},{12,4},{16,24},{20,28},{24,16},{28,20},{1,9},{5... | collective-permute-start | bytes 393224 | tf_op jit(solution)/shard_map/ppermute | solution.py:32
  29.0 1.0 %shard_map.100.dens_ref = bf16[256,1024]{1,0:T(8,128)(2,1)S(1)} custom-call(bf16[3,32,512]{2,1,0:T(8,128)(2,1)S(1)} %pad_maximum_fusion.2.bands_ref, bf16[2048,1024]{1,0:T(8,128)(2,1)S(1)} %copy-done, f32[256,1024]{1,0:T(8,128)S(1)} %shard_map.99.refs_0_), custom_call_target="tpu_custom_call" | custom-call | flops 805306368 | bytes 3145728 | tf_op jit(solution)/shard_map/pallas_call | solution.py:20
  30.1 0.0 collective-permute-done.11
  30.1 5.3 %collective-permute-done.9.refs_2_ = bf16[256,256]{1,0:T(8,128)(2,1)S(1)} collective-permute-done((bf16[256,256]{1,0:T(8,128)(2,1)S(1)}, bf16[256,256]{1,0:T(8,128)(2,1)S(1)}, u32[]{:S(2)}, u32[]{:S(2)}) %collective-permute-start.9) | collective-permute-done | bytes 131104 | tf_op jit(solution)/shard_map/ppermute | solution.py:32
  35.4 0.5 %collective-permute-done.8.refs_1_ = bf16[256,256]{1,0:T(8,128)(2,1)S(1)} collective-permute-done((bf16[256,256]{1,0:T(8,128)(2,1)S(1)}, bf16[256,256]{1,0:T(8,128)(2,1)S(1)}, u32[]{:S(2)}, u32[]{:S(2)}) %collective-permute-start.8) | collective-permute-done | bytes 131104 | tf_op jit(solution)/shard_map/ppermute | solution.py:32
  35.9 0.0 copy-done.2
  35.9 0.6 %shard_map.103 = (f32[64,512]{1,0:T(8,128)S(1)}, bf16[64,512]{1,0:T(8,128)(2,1)S(1)}, bf16[64,512]{1,0:T(8,128)(2,1)S(1)}, bf16[64,512]{1,0:T(8,128)(2,1)S(1)}) custom-call(bf16[256,1024]{1,0:T(8,128)(2,1)S(1)} %shard_map.100.dens_ref, bf16[256,512]{1,0:T(8,128)(2,1)S(1)} %copy-done.2, bf16[256,256]{1,0:T(8,128)(2,1)S(1)} %get-tuple-element.24.refs_0_, ...), custom_call_target="tpu_custom_call" | custom-call | flops 201326592 | bytes 524288 | tf_op jit(solution)/shard_map/pallas_call | solution.py:20
  36.5 1.5 %collective-permute-start.12 = (bf16[64,512]{1,0:T(8,128)(2,1)S(1)}, bf16[64,512]{1,0:T(8,128)(2,1)S(1)}, u32[]{:S(2)}, u32[]{:S(2)}) collective-permute-start(bf16[64,512]{1,0:T(8,128)(2,1)S(1)} %get-tuple-element.20), channel_id=1, source_target_pairs={{0,1},{1,0},{2,3},{3,2},{4,5},{5,4},{6,7},{7,6},{8,9},{9,8},{10,11... | collective-permute-start | bytes 196616 | tf_op jit(solution)/shard_map/ppermute | solution.py:32
  38.1 1.6 %collective-permute-start.13 = (bf16[64,512]{1,0:T(8,128)(2,1)S(1)}, bf16[64,512]{1,0:T(8,128)(2,1)S(1)}, u32[]{:S(2)}, u32[]{:S(2)}) collective-permute-start(bf16[64,512]{1,0:T(8,128)(2,1)S(1)} %get-tuple-element.21), channel_id=1, source_target_pairs={{0,2},{1,3},{2,0},{3,1},{4,6},{5,7},{6,4},{7,5},{8,10},{9,11},{10,... | collective-permute-start | bytes 196616 | tf_op jit(solution)/shard_map/ppermute | solution.py:32
  39.6 0.5 %collective-permute-start.14 = (bf16[64,512]{1,0:T(8,128)(2,1)S(1)}, bf16[64,512]{1,0:T(8,128)(2,1)S(1)}, u32[]{:S(2)}, u32[]{:S(2)}) collective-permute-start(bf16[64,512]{1,0:T(8,128)(2,1)S(1)} %get-tuple-element.22), channel_id=1, source_target_pairs={{0,3},{1,2},{2,1},{3,0},{4,7},{5,6},{6,5},{7,4},{8,11},{9,10},{10,... | collective-permute-start | bytes 196616 | tf_op jit(solution)/shard_map/ppermute | solution.py:32
  40.1 0.8 %collective-permute-done.12 = bf16[64,512]{1,0:T(8,128)(2,1)S(1)} collective-permute-done((bf16[64,512]{1,0:T(8,128)(2,1)S(1)}, bf16[64,512]{1,0:T(8,128)(2,1)S(1)}, u32[]{:S(2)}, u32[]{:S(2)}) %collective-permute-start.12) | collective-permute-done | bytes 65568 | tf_op jit(solution)/shard_map/ppermute | solution.py:32
  40.9 2.2 %collective-permute-done.13 = bf16[64,512]{1,0:T(8,128)(2,1)S(1)} collective-permute-done((bf16[64,512]{1,0:T(8,128)(2,1)S(1)}, bf16[64,512]{1,0:T(8,128)(2,1)S(1)}, u32[]{:S(2)}, u32[]{:S(2)}) %collective-permute-start.13) | collective-permute-done | bytes 65568 | tf_op jit(solution)/shard_map/ppermute | solution.py:32
  43.0 1.7 %collective-permute-done.14 = bf16[64,512]{1,0:T(8,128)(2,1)S(1)} collective-permute-done((bf16[64,512]{1,0:T(8,128)(2,1)S(1)}, bf16[64,512]{1,0:T(8,128)(2,1)S(1)}, u32[]{:S(2)}, u32[]{:S(2)}) %collective-permute-start.14) | collective-permute-done | bytes 65568 | tf_op jit(solution)/shard_map/ppermute | solution.py:32
  44.8 0.7 %convert_add_fusion = f32[64,512]{1,0:T(8,128)} fusion(bf16[64,512]{1,0:T(8,128)(2,1)S(1)} %collective-permute-done.14, bf16[64,512]{1,0:T(8,128)(2,1)S(1)} %collective-permute-done.13, f32[64,512]{1,0:T(8,128)S(1)} %get-tuple-element.19, bf16[64,512]{1,0:T(8,128)(2,1)S(1)} %collective-permute-done.12), kind=kLoop, calls=%fused_computation.11 | loop fusion | flops 196608 | bytes 458752 | tf_op jit(solution)/shard_map/add | solution.py:275
  (7 shorter events, 0.1 us)
Async XLA Ops:
  0.0 6.2 %collective-permute-start = (bf16[1,64,256]{2,1,0:T(8,128)(2,1)}, bf16[1,64,256]{2,1,0:T(8,128)(2,1)S(1)}, u32[]{:S(2)}, u32[]{:S(2)}) collective-permute-start(bf16[1,64,256]{2,1,0:T(8,128)(2,1)} %waves_ref.1), channel_id=1, source_target_pairs={{0,8},{4,12},{8,0},{12,4},{16,24},{20,28},{24,16},{28,20},{1,9},{5... | collective-permute-start | bytes 98312 | tf_op jit(solution)/shard_map/ppermute | solution.py:32
  4.6 0.8 %copy-start.4 = (bf16[1,64,256]{2,1,0:T(8,128)(2,1)S(1)}, bf16[1,64,256]{2,1,0:T(8,128)(2,1)}, u32[]{:S(2)}) copy-start(bf16[1,64,256]{2,1,0:T(8,128)(2,1)} %waves_ref.1) | copy-start | bytes 98308
  5.3 0.7 %copy-start.5 = (s32[8,1]{0,1:T(1,128)S(1)}, s32[8,1]{0,1:T(1,128)}, u32[]{:S(2)}) copy-start(s32[8,1]{0,1:T(1,128)} %param.16) | copy-start | bytes 100
  5.3 3.6 %copy-start.6 = (s32[8]{0:T(128)S(1)}, s32[8]{0:T(128)}, u32[]{:S(2)}) copy-start(s32[8]{0:T(128)} %param.15) | copy-start | bytes 100
  5.3 3.8 %copy-start = (bf16[2048,1024]{1,0:T(8,128)(2,1)S(1)}, bf16[2048,1024]{1,0:T(8,128)(2,1)}, u32[]{:S(2)}) copy-start(bf16[2048,1024]{1,0:T(8,128)(2,1)} %table_ref.11) | copy-start | bytes 12582916
  6.3 5.5 %collective-permute-start.3 = (bf16[2,32,256]{2,1,0:T(8,128)(2,1)S(1)}, bf16[2,32,256]{2,1,0:T(8,128)(2,1)S(1)}, u32[]{:S(2)}, u32[]{:S(2)}) collective-permute-start(bf16[2,32,256]{2,1,0:T(8,128)(2,1)S(1)} %shard_map.92.bands_ref), channel_id=1, source_target_pairs={{0,4},{4,0},{8,12},{12,8},{16,20},{20,16},{24,28},{28,24},{1,5},{5... | collective-permute-start | bytes 98312 | tf_op jit(solution)/shard_map/ppermute | solution.py:32
  6.4 5.5 %collective-permute-start.1 = (bf16[2,32,256]{2,1,0:T(8,128)(2,1)S(1)}, bf16[2,32,256]{2,1,0:T(8,128)(2,1)S(1)}, u32[]{:S(2)}, u32[]{:S(2)}) collective-permute-start(bf16[2,32,256]{2,1,0:T(8,128)(2,1)S(1)} %shard_map.92.bands_ref), channel_id=1, source_target_pairs={{0,16},{4,20},{8,24},{12,28},{16,0},{20,4},{24,8},{28,12},{1,17},{... | collective-permute-start | bytes 98312 | tf_op jit(solution)/shard_map/ppermute | solution.py:32
  9.6 2.7 %copy-start.1 = (bf16[8,128,1024]{2,1,0:T(8,128)(2,1)S(1)}, bf16[8,128,1024]{2,1,0:T(8,128)(2,1)}, u32[]{:S(2)}) copy-start(bf16[8,128,1024]{2,1,0:T(8,128)(2,1)} %screened_ref.5) | copy-start | bytes 6291460
  11.9 1.2 %collective-permute-start.2 = (bf16[2,32,256]{2,1,0:T(8,128)(2,1)S(1)}, bf16[2,32,256]{2,1,0:T(8,128)(2,1)S(1)}, u32[]{:S(2)}, u32[]{:S(2)}) collective-permute-start(bf16[2,32,256]{2,1,0:T(8,128)(2,1)S(1)} %collective-permute-done.1.bands_ref), channel_id=1, source_target_pairs={{0,4},{4,0},{8,12},{12,8},{16,20},{20,16},{24,28},{28,24},{1,5},{5... | collective-permute-start | bytes 98312 | tf_op jit(solution)/shard_map/ppermute | solution.py:32
  13.5 1.1 %copy-start.3 = (bf16[1,64,512]{2,1,0:T(8,128)(2,1)S(1)}, bf16[1,64,512]{2,1,0:T(8,128)(2,1)}, u32[]{:S(2)}) copy-start(bf16[1,64,512]{2,1,0:T(8,128)(2,1)} %waves_ref.2) | copy-start | bytes 196612
  14.4 11.0 %collective-permute-start.7 = (bf16[3,128,256]{2,1,0:T(8,128)(2,1)S(1)}, bf16[3,128,256]{2,1,0:T(8,128)(2,1)S(1)}, u32[]{:S(2)}, u32[]{:S(2)}) collective-permute-start(bf16[3,128,256]{2,1,0:T(8,128)(2,1)S(1)} %shard_map.97), channel_id=1, source_target_pairs={{0,4},{4,0},{8,12},{12,8},{16,20},{20,16},{24,28},{28,24},{1,5},{5... | collective-permute-start | bytes 589832 | tf_op jit(solution)/shard_map/ppermute | solution.py:32
  14.9 7.5 %collective-permute-start.6 = (bf16[1,32,512]{2,1,0:T(8,128)(2,1)S(1)}, bf16[1,32,512]{2,1,0:T(8,128)(2,1)S(1)}, u32[]{:S(2)}, u32[]{:S(2)}) collective-permute-start(bf16[1,32,512]{2,1,0:T(8,128)(2,1)S(1)} %get-tuple-element.17.bands_ref), channel_id=1, source_target_pairs={{0,3},{1,2},{2,1},{3,0},{4,7},{5,6},{6,5},{7,4},{8,11},{9,10},{10,... | collective-permute-start | bytes 98312 | tf_op jit(solution)/shard_map/ppermute | solution.py:32
  17.4 5.0 %collective-permute-start.5 = (bf16[1,32,512]{2,1,0:T(8,128)(2,1)S(1)}, bf16[1,32,512]{2,1,0:T(8,128)(2,1)S(1)}, u32[]{:S(2)}, u32[]{:S(2)}) collective-permute-start(bf16[1,32,512]{2,1,0:T(8,128)(2,1)S(1)} %get-tuple-element.17.bands_ref), channel_id=1, source_target_pairs={{0,2},{1,3},{2,0},{3,1},{4,6},{5,7},{6,4},{7,5},{8,10},{9,11},{10,... | collective-permute-start | bytes 98312 | tf_op jit(solution)/shard_map/ppermute | solution.py:32
  17.9 4.5 %collective-permute-start.4 = (bf16[1,32,512]{2,1,0:T(8,128)(2,1)S(1)}, bf16[1,32,512]{2,1,0:T(8,128)(2,1)S(1)}, u32[]{:S(2)}, u32[]{:S(2)}) collective-permute-start(bf16[1,32,512]{2,1,0:T(8,128)(2,1)S(1)} %get-tuple-element.17.bands_ref), channel_id=1, source_target_pairs={{0,1},{1,0},{2,3},{3,2},{4,5},{5,4},{6,7},{7,6},{8,9},{9,8},{10,11... | collective-permute-start | bytes 98312 | tf_op jit(solution)/shard_map/ppermute | solution.py:32
  18.5 6.8 %collective-permute-start.10 = (bf16[256,256]{1,0:T(8,128)(2,1)S(1)}, bf16[256,256]{1,0:T(8,128)(2,1)S(1)}, u32[]{:S(2)}, u32[]{:S(2)}) collective-permute-start(bf16[256,256]{1,0:T(8,128)(2,1)S(1)} %bitcast.13), channel_id=1, source_target_pairs={{0,24},{4,28},{8,16},{12,20},{16,8},{20,12},{24,0},{28,4},{1,25},{... | collective-permute-start | bytes 393224 | tf_op jit(solution)/shard_map/ppermute | solution.py:32
  22.4 13.6 %copy-start.2 = (bf16[256,512]{1,0:T(8,128)(2,1)S(1)}, bf16[256,512]{1,0:T(8,128)(2,1)}, u32[]{:S(2)}) copy-start(bf16[256,512]{1,0:T(8,128)(2,1)} %trial_ref.1) | copy-start | bytes 786436
  25.2 4.8 %collective-permute-start.11 = (bf16[128,256]{1,0:T(8,128)(2,1)S(1)}, bf16[128,256]{1,0:T(8,128)(2,1)S(1)}, u32[]{:S(2)}, u32[]{:S(2)}) collective-permute-start(bf16[128,256]{1,0:T(8,128)(2,1)S(1)} %get-tuple-element.27), channel_id=1, source_target_pairs={{0,4},{4,0},{8,12},{12,8},{16,20},{20,16},{24,28},{28,24},{1,5},{5... | collective-permute-start | bytes 196616 | tf_op jit(solution)/shard_map/ppermute | solution.py:32
  25.4 10.0 %collective-permute-start.9 = (bf16[256,256]{1,0:T(8,128)(2,1)S(1)}, bf16[256,256]{1,0:T(8,128)(2,1)S(1)}, u32[]{:S(2)}, u32[]{:S(2)}) collective-permute-start(bf16[256,256]{1,0:T(8,128)(2,1)S(1)} %get-tuple-element.23), channel_id=1, source_target_pairs={{0,16},{4,20},{8,24},{12,28},{16,0},{20,4},{24,8},{28,12},{1,17},{... | collective-permute-start | bytes 393224 | tf_op jit(solution)/shard_map/ppermute | solution.py:32
  28.4 7.6 %collective-permute-start.8 = (bf16[256,256]{1,0:T(8,128)(2,1)S(1)}, bf16[256,256]{1,0:T(8,128)(2,1)S(1)}, u32[]{:S(2)}, u32[]{:S(2)}) collective-permute-start(bf16[256,256]{1,0:T(8,128)(2,1)S(1)} %get-tuple-element.25), channel_id=1, source_target_pairs={{0,8},{4,12},{8,0},{12,4},{16,24},{20,28},{24,16},{28,20},{1,9},{5... | collective-permute-start | bytes 393224 | tf_op jit(solution)/shard_map/ppermute | solution.py:32
  36.5 4.3 %collective-permute-start.12 = (bf16[64,512]{1,0:T(8,128)(2,1)S(1)}, bf16[64,512]{1,0:T(8,128)(2,1)S(1)}, u32[]{:S(2)}, u32[]{:S(2)}) collective-permute-start(bf16[64,512]{1,0:T(8,128)(2,1)S(1)} %get-tuple-element.20), channel_id=1, source_target_pairs={{0,1},{1,0},{2,3},{3,2},{4,5},{5,4},{6,7},{7,6},{8,9},{9,8},{10,11... | collective-permute-start | bytes 196616 | tf_op jit(solution)/shard_map/ppermute | solution.py:32
  38.1 5.0 %collective-permute-start.13 = (bf16[64,512]{1,0:T(8,128)(2,1)S(1)}, bf16[64,512]{1,0:T(8,128)(2,1)S(1)}, u32[]{:S(2)}, u32[]{:S(2)}) collective-permute-start(bf16[64,512]{1,0:T(8,128)(2,1)S(1)} %get-tuple-element.21), channel_id=1, source_target_pairs={{0,2},{1,3},{2,0},{3,1},{4,6},{5,7},{6,4},{7,5},{8,10},{9,11},{10,... | collective-permute-start | bytes 196616 | tf_op jit(solution)/shard_map/ppermute | solution.py:32
  39.6 5.2 %collective-permute-start.14 = (bf16[64,512]{1,0:T(8,128)(2,1)S(1)}, bf16[64,512]{1,0:T(8,128)(2,1)S(1)}, u32[]{:S(2)}, u32[]{:S(2)}) collective-permute-start(bf16[64,512]{1,0:T(8,128)(2,1)S(1)} %get-tuple-element.22), channel_id=1, source_target_pairs={{0,3},{1,2},{2,1},{3,0},{4,7},{5,6},{6,5},{7,4},{8,11},{9,10},{10,... | collective-permute-start | bytes 196616 | tf_op jit(solution)/shard_map/ppermute | solution.py:32
